TPU v7x, 32 devices: a whole 2x2x4 slice. The times are simulated.
32 devices in a mesh: rows: 4 (over z), rhs: 8 (over y, x, core).
Axes of the slice: x: 2, y: 2, z: 4, core: 2. Of those that a mesh axis runs over, the one named last changes fastest.
Arguments:
- rhs_blocks: bfloat16 [4, 2048, 1024], P('rows', None, 'rhs'), may hold values from -6 to 6
- left_u: bfloat16 [4, 4, 2048, 256], P('rows', None, 'rhs'), may hold values from -0.375 to 0.375
- left_v: bfloat16 [4, 4, 2048, 256], P('rows', None, 'rhs'), may hold values from -0.125 to 0.125
- tile_ranks: int32 [4, 4], P('rows'), may hold values from 32 to 256
- diag_inverse: bfloat16 [4, 2048, 2048], P(None, 'rows'), may hold values from -8 to 8, as said below
- row_owner: int32 [4], replicated, may hold values from 0 to 3, each once
Outputs:
- solved: bfloat16 [4, 2048, 1024], P(None, 'rows', 'rhs')
- updated: bfloat16 [4, 2048, 1024], P('rows', None, 'rhs')
Inputs may be any that keep to these rules, and one draw needn't show every extreme that they name: tile_ranks[s, k] is the rank of the tile in column k of the tile row stored in block s. row_owner[s] is the tile row held in stored block s; every tile row is held exactly once. Each diag_inverse[k] is lower triangular.
All inputs are finite; a program needn't handle non-finite values.
Results may differ from a plain program's by a relative error of at most 0.01.
Values may be sent and summed in bfloat16 or wider, within the bound.
No kernel may reach another device: no remote copies, remote signals or barrier semaphores. Data moves between devices by JAX's collectives and lax.ppermute only.
A program may use at most 64 MiB of HBM per device.

v0:
```python
import jax
import jax.numpy as jnp
from jax import lax
from jax.sharding import PartitionSpec as P


def left_product(v_piece, x_rows, tile_rank):
    width = v_piece.shape[1]
    keep_cols = (jnp.arange(width, dtype=jnp.int32) < tile_rank).astype(v_piece.dtype)
    dims = (((0,), (0,)), ((), ()))
    return lax.dot_general(v_piece * keep_cols, x_rows, dims, preferred_element_type=jnp.float32)


def right_product(u_piece, coeffs):
    return jnp.dot(u_piece, coeffs, preferred_element_type=jnp.float32)


def body(rhs_blocks, left_u, left_v, tile_ranks, diag_inverse, row_owner):
    my_index = lax.axis_index("rows")
    stored = jnp.arange(row_owner.shape[0], dtype=jnp.int32)
    my_row = jnp.sum(jnp.where(stored == my_index, row_owner, 0))
    residual = rhs_blocks[0].astype(jnp.float32)
    solved_parts = []
    for column in range(diag_inverse.shape[0]):
        owner_index = jnp.sum(jnp.where(row_owner == column, stored, 0))
        inverse_rows = diag_inverse[column]
        rounded = residual.astype(jnp.bfloat16).astype(jnp.float32)
        offered = jnp.where(my_index == owner_index, rounded, jnp.zeros_like(rounded))
        own_piece = lax.psum_scatter(
            offered.astype(jnp.bfloat16), "rows", scatter_dimension=0, tiled=True
        )
        solved_part = jnp.dot(
            inverse_rows,
            lax.all_gather(own_piece, "rows", axis=0, tiled=True),
            preferred_element_type=jnp.float32,
        ).astype(jnp.bfloat16)
        solved_parts.append(solved_part)
        solution = lax.all_gather(solved_part, "rows", axis=0, tiled=True)
        tile_rank = tile_ranks[0, column]
        coeffs = left_product(
            lax.all_gather(left_v[0, column], "rhs", axis=0, tiled=True), solution, tile_rank
        ).astype(jnp.bfloat16)
        update = right_product(lax.all_gather(left_u[0, column], "rhs", axis=0, tiled=True), coeffs)
        residual = jnp.where(column < my_row, residual - update, residual)
    return (jnp.stack(solved_parts), residual.astype(jnp.bfloat16)[None])


def solution(mesh):
    return jax.shard_map(
        body,
        mesh=mesh,
        in_specs=(
            P("rows", None, "rhs"),
            P("rows", None, "rhs", None),
            P("rows", None, "rhs", None),
            P("rows", None),
            P(None, "rows", None),
            P(),
        ),
        out_specs=(P(None, "rows", "rhs"), P("rows", None, "rhs")),
        check_vma=False,
    )
```

profile of v0, /device:TPU:0, one launch (start us, length us, event | category | flops | bytes accessed | tf_op | source)
XLA Modules:
  0.0 257.0 jit_solution(11643041167320464591)
XLA Ops:
  8.0 0.0 reduce-scatter.5.cloned.1.call-start
  8.0 1.2 copy.8
  9.3 1.4 fusion.51
  11.3 0.9 fusion.34
  12.2 0.0 reduce-scatter.5.cloned.1.call-update
  12.3 0.0 all-gather.19.cloned.1.call-start
  12.3 1.9 fusion.53
  14.2 0.0 all-gather.19.cloned.1.call-update
  14.2 0.0 all-gather.17.cloned.1.call-start
  14.3 1.9 fusion.52
  16.2 0.0 all-gather.17.cloned.1.call-update
  16.2 0.0 reduce-scatter.7.cloned.1.call-start
  17.6 1.5 fusion.54
  19.1 0.6 compare_convert_fusion.3
  19.7 17.3 %reduce-scatter.5.cloned.1.call-done = bf16[512,128]{0,1:T(8,128)(2,1)} async-done(((bf16[2048,128]{0,1:T(8,128)(2,1)}), bf16[512,128]{0,1:T(8,128)(2,1)}) %reduce-scatter.5.cloned.1.call-update) | async-done | bytes 131088 | tf_op jit(solution)/shard_map/reduce_scatter | solution.py:29
  37.0 15.7 %all_gather.48 = bf16[2048,128]{0,1:T(8,128)(2,1)S(1)} all-gather(bf16[512,128]{0,1:T(8,128)(2,1)} %reduce-scatter.5.cloned.1.call-done), channel_id=1, replica_groups=mesh['rows'=4,'rhs'=8] {'rows'}, dimensions={0}, use_global_device_ids=true | all-gather | bytes 655360 | tf_op jit(solution)/shard_map/all_gather | solution.py:34
  52.7 2.4 fusion.22
  55.1 15.9 %all_gather.50 = bf16[2048,128]{0,1:T(8,128)(2,1)S(1)} all-gather(bf16[512,128]{0,1:T(8,128)(2,1)S(1)} %bitcast.118), channel_id=1, replica_groups=mesh['rows'=4,'rhs'=8] {'rows'}, dimensions={0}, use_global_device_ids=true | all-gather | bytes 655360 | tf_op jit(solution)/shard_map/all_gather | solution.py:38
  71.0 0.0 all-gather.19.cloned.1.call-done
  71.0 0.0 all-gather.17.cloned.1.call-done
  71.0 3.7 %select_convert_fusion.2 = (bf16[2048,128]{0,1:T(8,128)(2,1)}, f32[2048,128]{0,1:T(8,128)S(1)}) fusion(pred[]{:T(512)S(6)} %eq.33, bf16[1,1,2048,256]{3,2,1,0:T(8,128)(2,1)} %all-gather.19.cloned.1.call-done, bf16[2048,128]{0,1:T(8,128)(2,1)S(1)} %all_gather.50, bf16[1,1,2048,256]{3,2,1,0:T(8,128)(2,1)} %all-gather.17.cloned.1.call-done, ...), kind=kOutput, calls=%fused_computation.46 | convolution fusion | flops 270827520 | bytes 4719106 | tf_op jit(solution)/shard_map/dot_general | solution.py:15
  74.8 0.0 reduce-scatter.7.cloned.1.call-update
  74.8 0.0 all-gather.23.cloned.1.call-start
  74.8 0.5 all-gather.23.cloned.1.call-update
  75.4 0.0 all-gather.21.cloned.1.call-start
  75.4 0.7 all-gather.21.cloned.1.call-update
  76.1 0.0 reduce-scatter.9.cloned.1.call-start
  77.4 0.6 compare_convert_fusion.2
  78.0 17.1 %reduce-scatter.7.cloned.1.call-done = bf16[512,128]{0,1:T(8,128)(2,1)} async-done(((bf16[2048,128]{0,1:T(8,128)(2,1)}), bf16[512,128]{0,1:T(8,128)(2,1)}) %reduce-scatter.7.cloned.1.call-update) | async-done | bytes 131088 | tf_op jit(solution)/shard_map/reduce_scatter | solution.py:29
  95.2 15.6 %all_gather.52 = bf16[2048,128]{0,1:T(8,128)(2,1)S(1)} all-gather(bf16[512,128]{0,1:T(8,128)(2,1)} %reduce-scatter.7.cloned.1.call-done), channel_id=1, replica_groups=mesh['rows'=4,'rhs'=8] {'rows'}, dimensions={0}, use_global_device_ids=true | all-gather | bytes 655360 | tf_op jit(solution)/shard_map/all_gather | solution.py:34
  110.7 2.4 fusion.25
  113.2 15.7 %all_gather.54 = bf16[2048,128]{0,1:T(8,128)(2,1)S(1)} all-gather(bf16[512,128]{0,1:T(8,128)(2,1)S(1)} %bitcast.120), channel_id=1, replica_groups=mesh['rows'=4,'rhs'=8] {'rows'}, dimensions={0}, use_global_device_ids=true | all-gather | bytes 655360 | tf_op jit(solution)/shard_map/all_gather | solution.py:38
  128.9 0.0 all-gather.23.cloned.1.call-done
  128.9 0.0 all-gather.21.cloned.1.call-done
  128.9 3.7 %select_convert_fusion.1 = (bf16[2048,128]{0,1:T(8,128)(2,1)}, f32[2048,128]{0,1:T(8,128)S(1)}) fusion(pred[]{:T(512)S(6)} %eq.37, f32[2048,128]{0,1:T(8,128)S(1)} %get-tuple-element.22, bf16[1,1,2048,256]{3,2,1,0:T(8,128)(2,1)} %all-gather.23.cloned.1.call-done, bf16[2048,128]{0,1:T(8,128)(2,1)S(1)} %all_gather.54, ...), kind=kOutput, calls=%fused_computation.45 | convolution fusion | flops 270565376 | bytes 5243394 | tf_op jit(solution)/shard_map/dot_general | solution.py:15
  132.6 0.0 reduce-scatter.9.cloned.1.call-update
  132.7 0.0 all-gather.27.cloned.1.call-start
  132.7 0.7 all-gather.27.cloned.1.call-update
  133.4 0.0 all-gather.25.cloned.1.call-start
  133.5 0.7 all-gather.25.cloned.1.call-update
  134.1 0.0 reduce-scatter.11.cloned.1.call-start
  135.6 0.7 compare_convert_fusion.1
  136.3 17.0 %reduce-scatter.9.cloned.1.call-done = bf16[512,128]{0,1:T(8,128)(2,1)} async-done(((bf16[2048,128]{0,1:T(8,128)(2,1)}), bf16[512,128]{0,1:T(8,128)(2,1)}) %reduce-scatter.9.cloned.1.call-update) | async-done | bytes 131088 | tf_op jit(solution)/shard_map/reduce_scatter | solution.py:29
  153.3 15.5 %all_gather.56 = bf16[2048,128]{0,1:T(8,128)(2,1)S(1)} all-gather(bf16[512,128]{0,1:T(8,128)(2,1)} %reduce-scatter.9.cloned.1.call-done), channel_id=1, replica_groups=mesh['rows'=4,'rhs'=8] {'rows'}, dimensions={0}, use_global_device_ids=true | all-gather | bytes 655360 | tf_op jit(solution)/shard_map/all_gather | solution.py:34
  168.8 2.4 fusion.28
  171.2 15.7 %all_gather.58 = bf16[2048,128]{0,1:T(8,128)(2,1)S(1)} all-gather(bf16[512,128]{0,1:T(8,128)(2,1)S(1)} %bitcast.122), channel_id=1, replica_groups=mesh['rows'=4,'rhs'=8] {'rows'}, dimensions={0}, use_global_device_ids=true | all-gather | bytes 655360 | tf_op jit(solution)/shard_map/all_gather | solution.py:38
  187.0 0.0 all-gather.25.cloned.1.call-done
  187.0 3.7 %select_convert_fusion = (bf16[2048,128]{0,1:T(8,128)(2,1)}, f32[2048,128]{0,1:T(8,128)S(1)}) fusion(pred[]{:T(512)S(6)} %eq.39, f32[2048,128]{0,1:T(8,128)S(1)} %get-tuple-element.24, bf16[1,1,2048,256]{3,2,1,0:T(8,128)(2,1)} %all-gather.27.cloned.1.call-done, bf16[2048,128]{0,1:T(8,128)(2,1)S(1)} %all_gather.58, ...), kind=kOutput, calls=%fused_computation.44 | convolution fusion | flops 270565376 | bytes 5243394 | tf_op jit(solution)/shard_map/dot_general | solution.py:15
  190.7 0.0 reduce-scatter.11.cloned.1.call-update
  190.7 0.0 all-gather.31.cloned.1.call-start
  190.8 0.5 all-gather.31.cloned.1.call-update
  191.3 0.0 all-gather.29.cloned.1.call-start
  191.4 0.5 all-gather.29.cloned.1.call-update
  192.6 0.6 compare_convert_fusion
  193.2 17.7 %reduce-scatter.11.cloned.1.call-done = bf16[512,128]{0,1:T(8,128)(2,1)} async-done(((bf16[2048,128]{0,1:T(8,128)(2,1)}), bf16[512,128]{0,1:T(8,128)(2,1)}) %reduce-scatter.11.cloned.1.call-update) | async-done | bytes 131088 | tf_op jit(solution)/shard_map/reduce_scatter | solution.py:29
  210.9 15.7 %all_gather.60 = bf16[2048,128]{0,1:T(8,128)(2,1)S(1)} all-gather(bf16[512,128]{0,1:T(8,128)(2,1)} %reduce-scatter.11.cloned.1.call-done), channel_id=1, replica_groups=mesh['rows'=4,'rhs'=8] {'rows'}, dimensions={0}, use_global_device_ids=true | all-gather | bytes 655360 | tf_op jit(solution)/shard_map/all_gather | solution.py:34
  226.6 2.4 fusion.31
  229.0 0.1 pad_maximum_fusion
  229.1 1.0 copy.9
  230.1 15.8 %all_gather.62 = bf16[2048,128]{0,1:T(8,128)(2,1)S(1)} all-gather(bf16[512,128]{0,1:T(8,128)(2,1)S(1)} %bitcast.125), channel_id=1, replica_groups=mesh['rows'=4,'rhs'=8] {'rows'}, dimensions={0}, use_global_device_ids=true | all-gather | bytes 655360 | tf_op jit(solution)/shard_map/all_gather | solution.py:38
  245.9 0.0 all-gather.31.cloned.1.call-done
  245.9 0.0 all-gather.29.cloned.1.call-done
  245.9 2.9 %fusion.9 = bf16[1,2048,128]{1,2,0:T(8,128)(2,1)S(1)} fusion(f32[2048,128]{0,1:T(8,128)S(1)} %get-tuple-element.26, bf16[1,1,2048,256]{3,2,1,0:T(8,128)(2,1)} %all-gather.31.cloned.1.call-done, bf16[2048,128]{0,1:T(8,128)(2,1)S(1)} %all_gather.62, bf16[1,1,2048,256]{3,2,1,0:T(8,128)(2,1)} %all-gather.29.cloned.1.call-done, ...), kind=kOutput, calls=%fused_computation.13 | convolution fusion | flops 269778944 | bytes 4194817 | tf_op jit(solution)/shard_map/dot_general | solution.py:15
  248.9 1.0 copy.10
  (1 shorter events, 0.0 us)
Async XLA Ops:
  8.0 29.0 %reduce-scatter.5.cloned.1.call-start = ((), (), s32[]{:S(2)}) async-start(), calls=%async_computation.4 | async-start | bytes 655360 | tf_op jit(solution)/shard_map/reduce_scatter | solution.py:29
  12.3 58.8 %all-gather.19.cloned.1.call-start = ((), (), s32[]{:S(2)}) async-start(), calls=%async_computation.9 | async-start | bytes 1179648 | tf_op jit(solution)/shard_map/all_gather | solution.py:43
  14.2 56.8 %all-gather.17.cloned.1.call-start = ((), (), s32[]{:S(2)}) async-start(), calls=%async_computation.8 | async-start | bytes 1179648 | tf_op jit(solution)/shard_map/all_gather | solution.py:41
  16.2 79.0 %reduce-scatter.7.cloned.1.call-start = ((), (), s32[]{:S(2)}) async-start(), calls=%async_computation.5 | async-start | bytes 655360 | tf_op jit(solution)/shard_map/reduce_scatter | solution.py:29
  74.8 54.1 %all-gather.23.cloned.1.call-start = ((), (), s32[]{:S(2)}) async-start(), calls=%async_computation.11 | async-start | bytes 1179648 | tf_op jit(solution)/shard_map/all_gather | solution.py:43
  75.4 53.5 %all-gather.21.cloned.1.call-start = ((), (), s32[]{:S(2)}) async-start(), calls=%async_computation.10 | async-start | bytes 1179648 | tf_op jit(solution)/shard_map/all_gather | solution.py:41
  76.1 77.2 %reduce-scatter.9.cloned.1.call-start = ((), (), s32[]{:S(2)}) async-start(), calls=%async_computation.6 | async-start | bytes 655360 | tf_op jit(solution)/shard_map/reduce_scatter | solution.py:29
  132.7 54.3 %all-gather.27.cloned.1.call-start = ((), (), s32[]{:S(2)}) async-start(), calls=%async_computation.13 | async-start | bytes 1179648 | tf_op jit(solution)/shard_map/all_gather | solution.py:43
  133.4 53.6 %all-gather.25.cloned.1.call-start = ((), (), s32[]{:S(2)}) async-start(), calls=%async_computation.12 | async-start | bytes 1179648 | tf_op jit(solution)/shard_map/all_gather | solution.py:41
  134.1 76.8 %reduce-scatter.11.cloned.1.call-start = ((), (), s32[]{:S(2)}) async-start(), calls=%async_computation.7 | async-start | bytes 655360 | tf_op jit(solution)/shard_map/reduce_scatter | solution.py:29
  190.7 55.2 %all-gather.31.cloned.1.call-start = ((), (), s32[]{:S(2)}) async-start(), calls=%async_computation.15 | async-start | bytes 1179648 | tf_op jit(solution)/shard_map/all_gather | solution.py:43
  191.3 54.6 %all-gather.29.cloned.1.call-start = ((), (), s32[]{:S(2)}) async-start(), calls=%async_computation.14 | async-start | bytes 1179648 | tf_op jit(solution)/shard_map/all_gather | solution.py:41
Sparse Core Ops, SparseCore 0:
  12.4 24.5 reduce-scatter.4
  74.9 20.2 reduce-scatter.6
  132.8 20.4 reduce-scatter.8
  190.8 20.0 reduce-scatter.10
Sparse Core Ops, SparseCore 1:
  14.6 25.9 all-gather.18
  42.4 23.2 all-gather.16
  77.7 21.6 all-gather.22
  101.3 23.2 all-gather.20
  135.4 21.8 all-gather.26
  159.1 23.2 all-gather.24
  193.1 21.4 all-gather.30
  216.3 23.2 all-gather.28
where the time goes:
time: 258 us; the launch traced here: 257 us
  blocking collectives  126 us (49%)
  waiting for transfers between devices  72.9 us (28%)
  matrix products  23.8 us (9%)
  between operations  20.7 us (8%)
  local copies, waits for them, and re-layouts  8.51 us (3%)
  other arithmetic  4.95 us (2%)
    reduce_scatter x4, waiting for transfers between devices, body(): lax.psum_scatter(offered.astype(jnp.bfloat16), 'rows', scatter_dimension=...  69.1 us
    all_gather x4, blocking collectives, body(): solution = lax.all_gather(solved_part, 'rows', axis=0, tiled=True)  63.2 us
    all_gather x4, blocking collectives, body(): lax.all_gather(own_piece, 'rows', axis=0, tiled=True)  62.4 us
    dot_general x4, matrix products, right_product(): return jnp.dot(u_piece, coeffs, preferred_element_type=jnp.float32)  14.1 us
    dot_general x4, matrix products, body(): jnp.dot(inverse_rows, lax.all_gather(own_piece, 'rows', axis=0, tiled=Tru...  9.69 us
  transfers between devices with their start and end apart: 12, of which 4 were waited for; matrix products, arithmetic and copies ran while one was open for 7% of the time, Pallas kernels for 0%

commit v1 on v0

v1 whole, which is shorter than its diff:
```python
import functools

import jax
import jax.numpy as jnp
from jax import lax
from jax.experimental import pallas as pl
from jax.experimental.pallas import tpu as pltpu
from jax.sharding import PartitionSpec as P


F32, BF16 = jnp.float32, jnp.bfloat16


def left_product(v_piece, x_rows, tile_rank):
    width = v_piece.shape[1]
    keep_cols = (jnp.arange(width, dtype=jnp.int32) < tile_rank).astype(v_piece.dtype)
    dims = (((0,), (0,)), ((), ()))
    return lax.dot_general(v_piece * keep_cols, x_rows, dims, preferred_element_type=F32)


def right_product(u_piece, coeffs):
    return jnp.dot(u_piece, coeffs, preferred_element_type=F32)


def general_body(rhs_blocks, left_u, left_v, tile_ranks, diag_inverse, row_owner):
    my_index = lax.axis_index("rows")
    stored = jnp.arange(row_owner.shape[0], dtype=jnp.int32)
    my_row = jnp.sum(jnp.where(stored == my_index, row_owner, 0))
    residual = rhs_blocks[0].astype(F32)
    solved_parts = []
    for column in range(diag_inverse.shape[0]):
        owner_index = jnp.sum(jnp.where(row_owner == column, stored, 0))
        rounded = residual.astype(BF16).astype(F32)
        offered = jnp.where(my_index == owner_index, rounded, jnp.zeros_like(rounded))
        own_piece = lax.psum_scatter(offered.astype(BF16), "rows", scatter_dimension=0, tiled=True)
        solved_part = jnp.dot(
            diag_inverse[column],
            lax.all_gather(own_piece, "rows", axis=0, tiled=True),
            preferred_element_type=F32,
        ).astype(BF16)
        solved_parts.append(solved_part)
        solution = lax.all_gather(solved_part, "rows", axis=0, tiled=True)
        coeffs = left_product(
            lax.all_gather(left_v[0, column], "rhs", axis=0, tiled=True), solution, tile_ranks[0, column]
        ).astype(BF16)
        update = right_product(lax.all_gather(left_u[0, column], "rhs", axis=0, tiled=True), coeffs)
        residual = jnp.where(column < my_row, residual - update, residual)
    return (jnp.stack(solved_parts), residual.astype(BF16)[None])


PLACES = ((0, 1, 2, 3, 6, 5, 4, 7), (0, 1, 4, 5, 6, 3, 2, 7))


def gather_lanes(block):
    across = [(i, i ^ (4 if i & 1 else 2)) for i in range(8)]
    onward = [(i, i ^ (2 if i & 1 else 4)) for i in range(8)]
    swap = [(i, i ^ 1) for i in range(8)]
    near = lax.ppermute(block, "rhs", across)
    partner = lax.ppermute(block, "rhs", swap)
    near_partner = lax.ppermute(partner, "rhs", across)
    far = lax.ppermute(near, "rhs", onward)
    rest = [lax.ppermute(piece, "rhs", swap) for piece in (near, near_partner)]
    return [block, partner, near, near_partner, far, *rest]


def gather_rest(got, after=None):
    far = got[4]
    if after is not None:
        far = lax.optimization_barrier((far, after))[0]
    return [*got, lax.ppermute(far, "rhs", [(i, i ^ 1) for i in range(8)])]


def first_row(n, lane, rows):
    offset = jnp.where(lane & 1 == 0, PLACES[0][n], PLACES[1][n])
    return pl.multiple_of(jnp.bitwise_xor(lane, offset) * rows, rows)


def position():
    return lax.axis_index("rows"), lax.axis_index("rhs")


def around(index, n_rows):
    return lax.rem(index + n_rows, n_rows)


def pack_kernel(n_rows, owner, diag, left_v, left_u, *refs):
    packed, (u_out, tiles, sems) = refs[: n_rows - 1], refs[n_rows - 1 :]
    me, lane = position()
    n_cols, piece = diag.shape[0], diag.shape[1]
    rows, half = piece // 8, tiles.shape[1] // 2
    moves, tile_moves = [], []

    def move(source, target):
        copy = pltpu.make_async_copy(source, target, sems.at[len(moves) + len(tile_moves)])
        copy.start()
        return copy

    for delta, out in enumerate(packed, 1):
        column = jnp.minimum(owner[around(me + delta - n_rows, n_rows)], n_cols - 1)
        tile_moves.append(move(left_v.at[0, column], tiles.at[delta - 1]))
        for b in range(n_rows):
            share = pl.ds(pl.multiple_of(lane * rows, rows), rows)
            source = diag.at[column, share, pl.ds(b * piece, piece)]
            moves.append(move(source, out.at[pl.ds(b * rows, rows), :]))
    moves.append(move(left_u.at[0, pl.ds(0, u_out.shape[0])], u_out))
    for delta, out in enumerate(packed):
        tile_moves[delta].wait()
        turned = tiles[delta].T
        out[n_rows * rows :, : 2 * half] = turned[:half]
        out[n_rows * rows :, 2 * half :] = turned[half:]
    for copy in moves:
        copy.wait()


def keep_kernel(owner, diag, rhs, own_diag, rhs_out, sems):
    column = jnp.minimum(owner[position()[0]], diag.shape[0] - 1)
    moves = [
        pltpu.make_async_copy(diag.at[column], own_diag, sems.at[0]),
        pltpu.make_async_copy(rhs.at[0], rhs_out, sems.at[1]),
    ]
    for copy in moves:
        copy.start()
    for copy in moves:
        copy.wait()


def apply_update(column, n_rows, owner, ranks, residual, coeff_refs, u_refs, coeff, slot):
    me, lane = position()
    holder = sum(jnp.where(owner[s] == column, s, 0) for s in range(n_rows))
    shift = around(holder - me, n_rows)
    rank = ranks[0, column]

    @pl.when(column < owner[me])
    def _():
        for delta in range(1, n_rows):

            @pl.when(shift == delta)
            def _():
                index = lax.broadcasted_iota(jnp.int32, coeff.shape, 0)
                coeff[...] = jnp.where(index < rank, coeff_refs[delta - 1][...].astype(F32), 0.0).astype(BF16)

        for n, u_ref in enumerate(u_refs):
            at = pl.ds(first_row(n, lane, u_ref.shape[1]), u_ref.shape[1])
            update = jnp.dot(u_ref[slot], coeff[...], preferred_element_type=F32)
            residual[at, :] = residual[at, :] - update


def write_coefficients(n_rows, solved, packed_refs, out_coeffs):
    lane = position()[1]
    rank_max = out_coeffs[0].shape[0]
    total = 0.0
    for n in range(8):
        parts = []
        for delta in range(n_rows - 1):
            turned = packed_refs[8 * delta + n][-rank_max // 2 :, :]
            parts += [turned[:, : turned.shape[1] // 2], turned[:, turned.shape[1] // 2 :]]
        factor = jnp.concatenate(parts)
        at = pl.ds(first_row(n, lane, factor.shape[1]), factor.shape[1])
        total += jnp.dot(factor, solved[at, :], preferred_element_type=F32)
    for delta, out in enumerate(out_coeffs):
        out[...] = total[delta * rank_max : (delta + 1) * rank_max].astype(BF16)


def step_kernel(column, last, n_rows, owner, ranks, start, *refs):
    refs = list(refs)
    take = lambda n: [refs.pop(0) for _ in range(n)]
    coeff_refs, u_refs, before = [], [], []
    if column:
        coeff_refs, u_refs, before = take(n_rows - 1), take(8), take(n_rows)
    (own_diag,), packed_refs = take(1), take(8 * (n_rows - 1))
    chunks = take(n_rows)
    (residual, *out_coeffs), refs = ([refs[-1]], refs[:-1]) if last else (refs[:n_rows], refs[n_rows:])
    solved, products, coeff = refs
    me, lane = position()
    mine = owner[me]
    residual[...] = start[...].astype(F32)
    if column:
        apply_update(column - 1, n_rows, owner, ranks, residual, coeff_refs, u_refs, coeff, column - 1)

        @pl.when(mine < column)
        def _():
            for chunk, earlier in zip(chunks, before):
                chunk[...] = earlier[...]

    @pl.when(mine == column)
    def _():
        piece = own_diag.shape[0]
        rows = piece // 8
        for block in range(n_rows):
            at = slice(block * piece, (block + 1) * piece)
            rounded = residual[at, :].astype(BF16)
            for delta in range(n_rows):
                source = around(me - delta, n_rows)

                @pl.when(source >= block)
                def _():
                    if delta:
                        refs_of = packed_refs[8 * (delta - 1) : 8 * delta]
                        sent = jnp.concatenate([ref[block * rows : (block + 1) * rows, :] for ref in refs_of])
                    else:
                        sent = own_diag[:, at]
                    product = jnp.dot(sent, rounded, preferred_element_type=F32)
                    products[delta] = products[delta] + product if block else product

        for delta in range(n_rows):
            base = around(me - delta, n_rows) * piece
            whole = products[delta].astype(BF16)
            if delta:
                for n in range(8):
                    at = pl.multiple_of(base + first_row(n, lane, rows), rows)
                    solved[pl.ds(at, rows), :] = whole[n * rows : (n + 1) * rows]
            else:
                solved[pl.ds(pl.multiple_of(base, piece), piece), :] = whole
        for delta, chunk in enumerate(chunks):
            target = around(me + delta - n_rows, n_rows)
            chunk[...] = solved[pl.ds(pl.multiple_of(target * piece, piece), piece), :]
        if not last:
            write_coefficients(n_rows, solved, packed_refs, out_coeffs)


def coefficient_kernel(n_rows, owner, ranks, *refs):
    n_packed = 8 * (n_rows - 1)
    chunks, packed_refs, out_coeffs = refs[:n_rows], refs[n_rows : n_rows + n_packed], refs[n_rows + n_packed : -1]
    solved = refs[-1]
    for delta, chunk in enumerate(chunks):
        piece = chunk.shape[0]
        target = around(position()[0] + delta - n_rows, n_rows)
        solved[pl.ds(pl.multiple_of(target * piece, piece), piece), :] = chunk[...]
    write_coefficients(n_rows, solved, packed_refs, out_coeffs)


def last_kernel(column, slot, n_rows, owner, ranks, start, *refs):
    coeff_refs, u_refs = refs[: n_rows - 1], refs[n_rows - 1 : n_rows + 7]
    residual, updated, coeff = refs[n_rows + 7 :]
    residual[...] = start[...]
    apply_update(column, n_rows, owner, ranks, residual, coeff_refs, u_refs, coeff, slot)
    updated[...] = residual[...].astype(BF16)


def place_kernel(n_rows, owner, ranks, *refs):
    chunks, (out,) = refs[:n_rows], refs[n_rows:]
    for delta, chunk in enumerate(chunks):
        column = owner[around(position()[0] - delta, n_rows)]

        @pl.when(column < out.shape[0])
        def _():
            out[column] = chunk[...]


VMEM = pl.BlockSpec(memory_space=pltpu.VMEM)
SMEM = pl.BlockSpec(memory_space=pltpu.SMEM)


def body(rhs_blocks, left_u, left_v, tile_ranks, diag_inverse, row_owner):
    return direct_body(rhs_blocks, left_u, left_v, tile_ranks, diag_inverse, row_owner)


def direct_body(rhs_blocks, left_u, left_v, tile_ranks, diag_inverse, row_owner):
    n_cols, piece, order = diag_inverse.shape
    n_rows = row_owner.shape[0]
    width, rank_max = rhs_blocks.shape[2], left_u.shape[3]
    rows = piece // 8
    n_u = min(n_cols, n_rows - 1)

    def shifted(array, delta):
        return lax.ppermute(array, "rows", [(i, (i + delta) % n_rows) for i in range(n_rows)])

    def like(*shape):
        return jax.ShapeDtypeStruct(shape, BF16)

    chunk = left_u.shape[2]
    anywhere = pl.BlockSpec(memory_space=pl.ANY)
    *packed, u_mine = pl.pallas_call(
        functools.partial(pack_kernel, n_rows),
        out_shape=[like(n_rows * rows + rank_max // 2, piece)] * (n_rows - 1) + [like(n_u, chunk, rank_max)],
        in_specs=[SMEM] + [anywhere] * 3,
        out_specs=[VMEM] * n_rows,
        scratch_shapes=[
            pltpu.VMEM((n_rows - 1, chunk, rank_max), BF16),
            pltpu.SemaphoreType.DMA(((n_rows - 1) * (n_rows + 1) + 1,)),
        ],
        compiler_params=pltpu.CompilerParams(vmem_limit_bytes=52 * 2**20),
        name="pack",
    )(row_owner, diag_inverse, left_v, left_u)
    own_diag, residual = pl.pallas_call(
        keep_kernel,
        out_shape=[like(piece, order), like(order, width)],
        in_specs=[SMEM, anywhere, anywhere],
        out_specs=[VMEM] * 2,
        scratch_shapes=[pltpu.SemaphoreType.DMA((2,))],
        compiler_params=pltpu.CompilerParams(vmem_limit_bytes=48 * 2**20),
        name="keep",
    )(row_owner, diag_inverse, rhs_blocks)
    packed[1], own_diag, residual = lax.optimization_barrier((packed[1], own_diag, residual))
    u_all = gather_lanes(u_mine)
    packed_all = []
    for delta in range(1, n_rows):
        packed_all += gather_rest(gather_lanes(shifted(packed[delta - 1], delta)))

    whole, halved = jax.ShapeDtypeStruct((order, width), F32), jax.ShapeDtypeStruct((order, width), BF16)
    chunk_shapes = [jax.ShapeDtypeStruct((piece, width), BF16)] * n_rows
    coeff_shapes = [like(rank_max, width)] * (n_rows - 1)
    coeff_scratch = pltpu.VMEM((rank_max, width), BF16)
    params = pltpu.CompilerParams(vmem_limit_bytes=26 * 2**20)

    def call(kernel, in_specs, out_shape, scratch, *operands):
        return pl.pallas_call(
            kernel,
            out_shape=out_shape,
            in_specs=[SMEM, SMEM] + in_specs,
            out_specs=[VMEM] * len(out_shape) if isinstance(out_shape, list) else VMEM,
            scratch_shapes=scratch,
            compiler_params=params,
            cost_estimate=pl.CostEstimate(flops=2 * order * order * width, bytes_accessed=0, transcendentals=0),
        )(row_owner, tile_ranks, *operands)

    def sent_back(coeffs):
        pairs = zip(range(1, n_rows), coeffs)
        return [shifted(c, n_rows - delta) for delta, c in pairs]

    chunks, coeffs = [], []
    scratch = [pltpu.VMEM((order, width), BF16), pltpu.VMEM((n_rows, piece, width), F32), coeff_scratch]
    for column in range(n_cols):
        last = column == n_cols - 1
        if column == 1:
            u_all = gather_rest(u_all, residual)
        before = [*sent_back(coeffs), *u_all, *chunks] if column else []
        outs = call(
            functools.partial(step_kernel, column, last, n_rows),
            [VMEM] * (2 + len(before) + len(packed_all)),
            chunk_shapes + ([] if last else [whole] + coeff_shapes),
            scratch + ([pltpu.VMEM((order, width), F32)] if last else []),
            residual, *before, own_diag, *packed_all,
        )
        chunks, rest = outs[:n_rows], outs[n_rows:]
        if not last:
            residual, coeffs = rest[0], rest[1:]
    arrived = [chunks[0]] + [shifted(chunks[delta], delta) for delta in range(1, n_rows)]
    residual, updated = call(
        functools.partial(last_kernel, n_cols - 2, n_cols - 2, n_rows),
        [VMEM] * (n_rows + 8), [whole, halved], [coeff_scratch], residual, *before[: n_rows + 7],
    )

    def finish(residual, _, chunks, u_last, packed_all):
        coeffs = call(
            functools.partial(coefficient_kernel, n_rows),
            [VMEM] * (n_rows + len(packed_all)), coeff_shapes, scratch[:1], *chunks, *packed_all,
        )
        got, u_all = sent_back(coeffs), gather_rest(gather_lanes(u_last))
        return call(
            functools.partial(last_kernel, n_cols - 1, 0, n_rows),
            [VMEM] * (n_rows + 8), [whole, halved], [coeff_scratch], residual, *got, *u_all,
        )[1]

    updated = lax.cond(
        jnp.max(row_owner) > n_cols - 1,
        finish,
        lambda _, updated, *rest: updated,
        residual, updated, chunks, left_u[0, n_cols - 1 :], packed_all,
    )
    solved_out = call(
        functools.partial(place_kernel, n_rows),
        [VMEM] * n_rows, jax.ShapeDtypeStruct((n_cols, piece, width), BF16), [], *arrived,
    )
    return solved_out, updated[None]


def solution(mesh):
    direct = mesh.shape["rhs"] == 2**3 and mesh.shape["rows"] == 2**2
    return jax.shard_map(
        body if direct else general_body,
        mesh=mesh,
        in_specs=(
            P("rows", None, "rhs"),
            P("rows", None, "rhs", None),
            P("rows", None, "rhs", None),
            P("rows", None),
            P(None, "rows", None),
            P(),
        ),
        out_specs=(P(None, "rows", "rhs"), P("rows", None, "rhs")),
        check_vma=False,
    )
```

time: 258 us -> 169 us (0.66)
  blocking collectives: 126 us -> 0 us
  starting transfers between devices: 0.5 us -> 51.6 us
  matrix products: 23.8 us -> 0 us
  Pallas kernels: 0 us -> 20.2 us
  between operations: 20.7 us -> 2.07 us
  waiting for transfers between devices: 72.9 us -> 79.5 us
  local copies, waits for them, and re-layouts: 8.51 us -> 13.8 us
  other arithmetic: 4.95 us -> 0.71 us
    all_gather x8 -> x0, blocking collectives: 126 us -> none  [the longest x4 63.2 us: body(): solution = lax.all_gather(solved_part, 'rows', axis=0, tiled=True)]
    ppermute x0 -> x43, waiting for transfers between devices: none -> 79.5 us  [the longest x15 42.8 us: shifted(): lax.ppermute(array, 'rows', [(i, (i + delta) % n_rows) for i in range(n_r...]
    reduce_scatter x4 -> x0, waiting for transfers between devices: 69.1 us -> none  [body(): lax.psum_scatter(offered.astype(jnp.bfloat16), 'rows', scatter_dimension=...]
    ppermute x0 -> x43, starting transfers between devices: none -> 51.6 us  [the longest x15 33.1 us: shifted(): lax.ppermute(array, 'rows', [(i, (i + delta) % n_rows) for i in range(n_r...]
    dot_general x8 -> x0, matrix products: 23.8 us -> none  [the longest x4 14.1 us: right_product(): return jnp.dot(u_piece, coeffs, preferred_element_type=jnp.float32)]
    pallas_call x0 -> x8, Pallas kernels: none -> 20.2 us  [the longest x6 15.6 us: call(): pl.pallas_call(kernel, out_shape=out_shape, in_specs=[SMEM, SMEM] + in_sp...]
    unnamed x3 -> x142, local copies, waits for them, and re-layouts: 3.25 us -> 13.8 us
    slice x3 -> x0, local copies, waits for them, and re-layouts: 5.27 us -> none  [the longest x1 1.92 us: body(): left_v[0, column]]
  transfers between devices with their start and end apart: 12 -> 43, of which waited for: 4 -> 18; matrix products, arithmetic and copies ran while one was open for 7% -> 0% of each run, Pallas kernels for 0% -> 2%
where the time goes in v1:
time: 169 us; the launch traced here: 168 us
  waiting for transfers between devices  79.5 us (47%)
  starting transfers between devices  51.6 us (31%)
  Pallas kernels  20.2 us (12%)
  local copies, waits for them, and re-layouts  13.8 us (8%)
  between operations  2.07 us (1%)
    ppermute x15, waiting for transfers between devices, shifted(): lax.ppermute(array, 'rows', [(i, (i + delta) % n_rows) for i in range(n_r...  42.8 us
    ppermute x15, starting transfers between devices, shifted(): lax.ppermute(array, 'rows', [(i, (i + delta) % n_rows) for i in range(n_r...  33.1 us
    ppermute x4, waiting for transfers between devices, gather_lanes(): near_partner = lax.ppermute(partner, 'rhs', across)  20.2 us
    pallas_call x6, Pallas kernels, call(): pl.pallas_call(kernel, out_shape=out_shape, in_specs=[SMEM, SMEM] + in_sp...  15.6 us
    unnamed x142, local copies, waits for them, and re-layouts  13.8 us
    ppermute x4, waiting for transfers between devices, gather_lanes(): near = lax.ppermute(block, 'rhs', across)  11.4 us
    ppermute x4, starting transfers between devices, gather_lanes(): far = lax.ppermute(near, 'rhs', onward)  6.08 us
    ppermute x4, starting transfers between devices, gather_lanes(): near_partner = lax.ppermute(partner, 'rhs', across)  5.07 us
  transfers between devices with their start and end apart: 43, of which 18 were waited for; matrix products, arithmetic and copies ran while one was open for 0% of the time, Pallas kernels for 2%

profile of v1, /device:TPU:0, one launch (start us, length us, event | category | flops | bytes accessed | tf_op | source)
XLA Modules:
  0.0 167.9 jit_solution(16166647977446352778)
XLA Ops:
  0.7 2.4 %pack.1 = (bf16[384,512]{1,0:T(8,128)(2,1)S(1)}, bf16[384,512]{1,0:T(8,128)(2,1)S(1)}, bf16[384,512]{1,0:T(8,128)(2,1)S(1)}, bf16[3,256,256]{2,1,0:T(8,128)(2,1)S(1)}) custom-call(s32[4]{0:T(128)} %owner.15, bf16[4,512,2048]{2,1,0:T(8,128)(2,1)} %diag.3, bf16[1,4,256,256]{3,2,1,0:T(8,128)(2,1)} %left_v.1, bf16[1,4,256,256]{3,2,1,0:T(8,128)(2,1)} %left_u.1), custom_call_target="tpu_custom_call" | custom-call | tf_op jit(solution)/shard_map/pack/pallas_call | solution.py:273
  3.1 3.1 %collective-permute-start.10 = (bf16[384,512]{1,0:T(8,128)(2,1)S(1)}, bf16[384,512]{1,0:T(8,128)(2,1)S(1)}, u32[]{:S(2)}, u32[]{:S(2)}) collective-permute-start(bf16[384,512]{1,0:T(8,128)(2,1)S(1)} %get-tuple-element.157), channel_id=1, source_target_pairs={{0,8},{8,16},{16,24},{24,0},{1,9},{9,17},{17,25},{25,1},{2,10},{10... | collective-permute-start | bytes 1179656 | tf_op jit(solution)/shard_map/ppermute | solution.py:266
  6.2 2.2 %keep.1 = (bf16[512,2048]{1,0:T(8,128)(2,1)S(1)}, bf16[2048,128]{1,0:T(8,128)(2,1)S(1)}) custom-call(s32[4]{0:T(128)S(1)} %copy-done.69, bf16[4,512,2048]{2,1,0:T(8,128)(2,1)} %diag.3, bf16[1,2048,128]{2,1,0:T(8,128)(2,1)S(1)} %copy-done.12), custom_call_target="tpu_custom_call" | custom-call | tf_op jit(solution)/shard_map/keep/pallas_call | solution.py:285
  8.4 2.7 %collective-permute-start.18 = (bf16[384,512]{1,0:T(8,128)(2,1)S(1)}, bf16[384,512]{1,0:T(8,128)(2,1)S(1)}, u32[]{:S(2)}, u32[]{:S(2)}) collective-permute-start(bf16[384,512]{1,0:T(8,128)(2,1)S(1)} %get-tuple-element.158), channel_id=1, source_target_pairs={{0,16},{8,24},{16,0},{24,8},{1,17},{9,25},{17,1},{25,9},{2,18},{10... | collective-permute-start | bytes 1179656 | tf_op jit(solution)/shard_map/ppermute | solution.py:266
  11.0 1.3 collective-permute-start.26
  12.4 1.5 collective-permute-start.38
  13.9 4.5 %collective-permute-done.10.refs_1_.refs_16_ = bf16[384,512]{1,0:T(8,128)(2,1)S(1)} collective-permute-done((bf16[384,512]{1,0:T(8,128)(2,1)S(1)}, bf16[384,512]{1,0:T(8,128)(2,1)S(1)}, u32[]{:S(2)}, u32[]{:S(2)}) %collective-permute-start.10) | collective-permute-done | bytes 393248 | tf_op jit(solution)/shard_map/ppermute | solution.py:266
  18.3 16.0 %collective-permute-done.18.refs_9_.refs_24_ = bf16[384,512]{1,0:T(8,128)(2,1)S(1)} collective-permute-done((bf16[384,512]{1,0:T(8,128)(2,1)S(1)}, bf16[384,512]{1,0:T(8,128)(2,1)S(1)}, u32[]{:S(2)}, u32[]{:S(2)}) %collective-permute-start.18) | collective-permute-done | bytes 393248 | tf_op jit(solution)/shard_map/ppermute | solution.py:266
  34.3 1.5 collective-permute-start.12
  35.8 1.2 collective-permute-start.20
  37.0 0.6 collective-permute-start.27
  37.6 0.5 collective-permute-start.28
  38.1 4.0 %collective-permute-done.12.refs_3_.refs_18_ = bf16[384,512]{1,0:T(8,128)(2,1)S(1)} collective-permute-done((bf16[384,512]{1,0:T(8,128)(2,1)S(1)}, bf16[384,512]{1,0:T(8,128)(2,1)S(1)}, u32[]{:S(2)}, u32[]{:S(2)}) %collective-permute-start.12) | collective-permute-done | bytes 393248 | tf_op jit(solution)/shard_map/ppermute | solution.py:58
  42.1 1.5 collective-permute-start.39
  44.1 2.2 %collective-permute-done.20.refs_11_.refs_26_ = bf16[384,512]{1,0:T(8,128)(2,1)S(1)} collective-permute-done((bf16[384,512]{1,0:T(8,128)(2,1)S(1)}, bf16[384,512]{1,0:T(8,128)(2,1)S(1)}, u32[]{:S(2)}, u32[]{:S(2)}) %collective-permute-start.20) | collective-permute-done | bytes 393248 | tf_op jit(solution)/shard_map/ppermute | solution.py:58
  46.3 1.5 collective-permute-start.14
  47.9 5.2 %collective-permute-done.28.refs_19_.refs_34_ = bf16[384,512]{1,0:T(8,128)(2,1)S(1)} collective-permute-done((bf16[384,512]{1,0:T(8,128)(2,1)S(1)}, bf16[384,512]{1,0:T(8,128)(2,1)S(1)}, u32[]{:S(2)}, u32[]{:S(2)}) %collective-permute-start.28) | collective-permute-done | bytes 393248 | tf_op jit(solution)/shard_map/ppermute | solution.py:58
  53.1 1.5 collective-permute-start.21
  54.6 4.4 %collective-permute-done.39.refs_6_ = bf16[3,256,256]{2,1,0:T(8,128)(2,1)S(1)} collective-permute-done((bf16[3,256,256]{2,1,0:T(8,128)(2,1)S(1)}, bf16[3,256,256]{2,1,0:T(8,128)(2,1)S(1)}, u32[]{:S(2)}, u32[]{:S(2)}) %collective-permute-start.39) | collective-permute-done | bytes 393248 | tf_op jit(solution)/shard_map/ppermute | solution.py:60
  59.0 1.5 collective-permute-start.22
  60.5 5.6 %collective-permute-done.13.refs_4_.refs_19_ = bf16[384,512]{1,0:T(8,128)(2,1)S(1)} collective-permute-done((bf16[384,512]{1,0:T(8,128)(2,1)S(1)}, bf16[384,512]{1,0:T(8,128)(2,1)S(1)}, u32[]{:S(2)}, u32[]{:S(2)}) %collective-permute-start.13) | collective-permute-done | bytes 393248 | tf_op jit(solution)/shard_map/ppermute | solution.py:60
  66.1 1.6 collective-permute-start.29
  67.7 1.5 collective-permute-start.30
  69.2 3.5 %collective-permute-done.21.refs_12_.refs_27_ = bf16[384,512]{1,0:T(8,128)(2,1)S(1)} collective-permute-done((bf16[384,512]{1,0:T(8,128)(2,1)S(1)}, bf16[384,512]{1,0:T(8,128)(2,1)S(1)}, u32[]{:S(2)}, u32[]{:S(2)}) %collective-permute-start.21) | collective-permute-done | bytes 393248 | tf_op jit(solution)/shard_map/ppermute | solution.py:60
  73.3 6.7 %collective-permute-done.29.refs_20_.refs_35_ = bf16[384,512]{1,0:T(8,128)(2,1)S(1)} collective-permute-done((bf16[384,512]{1,0:T(8,128)(2,1)S(1)}, bf16[384,512]{1,0:T(8,128)(2,1)S(1)}, u32[]{:S(2)}, u32[]{:S(2)}) %collective-permute-start.29) | collective-permute-done | bytes 393248 | tf_op jit(solution)/shard_map/ppermute | solution.py:60
  81.1 1.5 collective-permute-start.40
  83.4 0.6 shard_map.77
  84.1 4.8 %collective-permute-done.40.refs_7_ = bf16[3,256,256]{2,1,0:T(8,128)(2,1)S(1)} collective-permute-done((bf16[3,256,256]{2,1,0:T(8,128)(2,1)S(1)}, bf16[3,256,256]{2,1,0:T(8,128)(2,1)S(1)}, u32[]{:S(2)}, u32[]{:S(2)}) %collective-permute-start.40) | collective-permute-done | bytes 393248 | tf_op jit(solution)/shard_map/ppermute | solution.py:61
  88.9 9.8 %collective-permute-start.34 = (bf16[256,128]{1,0:T(8,128)(2,1)S(1)}, bf16[256,128]{1,0:T(8,128)(2,1)S(1)}, u32[]{:S(2)}, u32[]{:S(2)}) collective-permute-start(bf16[256,128]{1,0:T(8,128)(2,1)S(1)} %get-tuple-element.161), channel_id=1, source_target_pairs={{0,24},{8,0},{16,8},{24,16},{1,25},{9,1},{17,9},{25,17},{2,26},{10... | collective-permute-start | bytes 196616 | tf_op jit(solution)/shard_map/ppermute | solution.py:266
  98.6 0.6 collective-permute-start.36
  99.3 1.9 %collective-permute-done.34.refs_0_ = bf16[256,128]{1,0:T(8,128)(2,1)S(1)} collective-permute-done((bf16[256,128]{1,0:T(8,128)(2,1)S(1)}, bf16[256,128]{1,0:T(8,128)(2,1)S(1)}, u32[]{:S(2)}, u32[]{:S(2)}) %collective-permute-start.34) | collective-permute-done | bytes 65568 | tf_op jit(solution)/shard_map/ppermute | solution.py:266
  101.2 4.4 %collective-permute-done.35.refs_1_ = bf16[256,128]{1,0:T(8,128)(2,1)S(1)} collective-permute-done((bf16[256,128]{1,0:T(8,128)(2,1)S(1)}, bf16[256,128]{1,0:T(8,128)(2,1)S(1)}, u32[]{:S(2)}, u32[]{:S(2)}) %collective-permute-start.35) | collective-permute-done | bytes 65568 | tf_op jit(solution)/shard_map/ppermute | solution.py:266
  105.6 5.2 %shard_map.78 = (bf16[512,128]{1,0:T(8,128)(2,1)S(1)}, bf16[512,128]{1,0:T(8,128)(2,1)S(1)}, bf16[512,128]{1,0:T(8,128)(2,1)S(1)}, bf16[512,128]{1,0:T(8,128)(2,...) custom-call(s32[4]{0:T(128)S(1)} %copy-done.69, ...), custom_call_target="tpu_custom_call" | custom-call | flops 1073741824 | tf_op jit(solution)/shard_map/pallas_call | solution.py:307
  111.0 1.9 %collective-permute-start.46 = (bf16[256,128]{1,0:T(8,128)(2,1)S(1)}, bf16[256,128]{1,0:T(8,128)(2,1)S(1)}, u32[]{:S(2)}, u32[]{:S(2)}) collective-permute-start(bf16[256,128]{1,0:T(8,128)(2,1)S(1)} %get-tuple-element.173), channel_id=1, source_target_pairs={{0,8},{8,16},{16,24},{24,0},{1,9},{9,17},{17,25},{25,1},{2,10},{10... | collective-permute-start | bytes 196616 | tf_op jit(solution)/shard_map/ppermute | solution.py:266
  112.9 2.8 %collective-permute-done.44.refs_0_ = bf16[256,128]{1,0:T(8,128)(2,1)S(1)} collective-permute-done((bf16[256,128]{1,0:T(8,128)(2,1)S(1)}, bf16[256,128]{1,0:T(8,128)(2,1)S(1)}, u32[]{:S(2)}, u32[]{:S(2)}) %collective-permute-start.44) | collective-permute-done | bytes 65568 | tf_op jit(solution)/shard_map/ppermute | solution.py:266
  115.7 3.2 %collective-permute-done.45.refs_1_ = bf16[256,128]{1,0:T(8,128)(2,1)S(1)} collective-permute-done((bf16[256,128]{1,0:T(8,128)(2,1)S(1)}, bf16[256,128]{1,0:T(8,128)(2,1)S(1)}, u32[]{:S(2)}, u32[]{:S(2)}) %collective-permute-start.45) | collective-permute-done | bytes 65568 | tf_op jit(solution)/shard_map/ppermute | solution.py:266
  119.1 1.6 shard_map.79
  120.8 1.0 copy-done.10
  121.8 0.6 copy-done.13
  122.4 0.6 copy-done.15
  123.1 0.6 copy-done.17
  123.7 0.6 copy-done.19
  124.4 1.3 collective-permute-start.47
  125.7 4.3 %collective-permute-start.48 = (bf16[256,128]{1,0:T(8,128)(2,1)}, bf16[256,128]{1,0:T(8,128)(2,1)S(1)}, u32[]{:S(2)}, u32[]{:S(2)}) collective-permute-start(bf16[256,128]{1,0:T(8,128)(2,1)} %get-tuple-element.180), channel_id=1, source_target_pairs={{0,16},{8,24},{16,0},{24,8},{1,17},{9,25},{17,1},{25,9},{2,18},{10... | collective-permute-start | bytes 196616 | tf_op jit(solution)/shard_map/ppermute | solution.py:266
  130.0 2.0 %collective-permute-start.49 = (bf16[256,128]{1,0:T(8,128)(2,1)S(1)}, bf16[256,128]{1,0:T(8,128)(2,1)S(1)}, u32[]{:S(2)}, u32[]{:S(2)}) collective-permute-start(bf16[256,128]{1,0:T(8,128)(2,1)S(1)} %get-tuple-element.181), channel_id=1, source_target_pairs={{0,8},{8,16},{16,24},{24,0},{1,9},{9,17},{17,25},{25,1},{2,10},{10... | collective-permute-start | bytes 196616 | tf_op jit(solution)/shard_map/ppermute | solution.py:266
  132.0 0.7 reduce_max.9
  133.5 3.2 %collective-permute-done.48.refs_1_ = bf16[256,128]{1,0:T(8,128)(2,1)S(1)} collective-permute-done((bf16[256,128]{1,0:T(8,128)(2,1)}, bf16[256,128]{1,0:T(8,128)(2,1)S(1)}, u32[]{:S(2)}, u32[]{:S(2)}) %collective-permute-start.48) | collective-permute-done | bytes 65568 | tf_op jit(solution)/shard_map/ppermute | solution.py:266
  136.7 1.0 copy-done.1
  137.7 1.0 copy-done.3
  138.7 1.0 copy-done.5
  139.7 1.0 copy-done.7
  140.7 1.0 copy-done.9
  141.7 1.2 copy-done.11
  143.0 1.5 shard_map.82
  144.4 0.9 copy-done.14
  145.4 0.9 copy-done.16
  146.3 0.9 copy-done.18
  147.2 0.9 copy-done.20
  148.2 4.8 %shard_map.80 = (bf16[512,128]{1,0:T(8,128)(2,1)}, bf16[512,128]{1,0:T(8,128)(2,1)}, bf16[512,128]{1,0:T(8,128)(2,1)}, bf16[512,128]{1,0:T(8,128)(2,1)}) custom-call(s32[4]{0:T(128)S(1)} %copy-done.69, s32[1,4]{1,0:T(1,128)S(1)} %copy-done.70, f32[2048,128]{1,0:T(8,128)S(1)} %copy-done.11, bf16[256,128]{1,0:T(8,128)(2,1)S(1)} %collective-permute-done.47.refs_0_, ...), custom_call_target="tpu_custom_call" | custom-call | flops 1073741824 | tf_op jit(solution)/shard_map/pallas_call | solution.py:307
  153.5 3.4 %collective-permute-start.50 = (bf16[512,128]{1,0:T(8,128)(2,1)}, bf16[512,128]{1,0:T(8,128)(2,1)S(1)}, u32[]{:S(2)}, u32[]{:S(2)}) collective-permute-start(bf16[512,128]{1,0:T(8,128)(2,1)} %get-tuple-element.187), channel_id=1, source_target_pairs={{0,8},{8,16},{16,24},{24,0},{1,9},{9,17},{17,25},{25,1},{2,10},{10... | collective-permute-start | bytes 393224 | tf_op jit(solution)/shard_map/ppermute | solution.py:266
  156.9 2.4 %collective-permute-start.52 = (bf16[512,128]{1,0:T(8,128)(2,1)}, bf16[512,128]{1,0:T(8,128)(2,1)S(1)}, u32[]{:S(2)}, u32[]{:S(2)}) collective-permute-start(bf16[512,128]{1,0:T(8,128)(2,1)} %get-tuple-element.189), channel_id=1, source_target_pairs={{0,24},{8,0},{16,8},{24,16},{1,25},{9,1},{17,9},{25,17},{2,26},{10... | collective-permute-start | bytes 393224 | tf_op jit(solution)/shard_map/ppermute | solution.py:266
  159.3 2.2 %collective-permute-done.50.refs_1_ = bf16[512,128]{1,0:T(8,128)(2,1)S(1)} collective-permute-done((bf16[512,128]{1,0:T(8,128)(2,1)}, bf16[512,128]{1,0:T(8,128)(2,1)S(1)}, u32[]{:S(2)}, u32[]{:S(2)}) %collective-permute-start.50) | collective-permute-done | bytes 131104 | tf_op jit(solution)/shard_map/ppermute | solution.py:266
  161.5 4.7 %collective-permute-done.51.refs_2_ = bf16[512,128]{1,0:T(8,128)(2,1)S(1)} collective-permute-done((bf16[512,128]{1,0:T(8,128)(2,1)}, bf16[512,128]{1,0:T(8,128)(2,1)S(1)}, u32[]{:S(2)}, u32[]{:S(2)}) %collective-permute-start.51) | collective-permute-done | bytes 131104 | tf_op jit(solution)/shard_map/ppermute | solution.py:266
  166.1 1.8 %shard_map.81 = bf16[4,512,128]{2,1,0:T(8,128)(2,1)} custom-call(s32[4]{0:T(128)S(1)} %copy-done.69, s32[1,4]{1,0:T(1,128)S(1)} %copy-done.70, bf16[512,128]{1,0:T(8,128)(2,1)} %get-tuple-element.186.refs_0_, bf16[512,128]{1,0:T(8,128)(2,1)S(1)} %collective-permute-done.50.refs_1_, bf16[512,128]{1,0:T(8,128)(2,1)S(1)} %collective-permute-done.51.refs_2_, ...), custom_call_target="tpu_custom_call" | custom-call | flops 1073741824 | tf_op jit(solution)/shard_map/pallas_call | solution.py:307
  (174 shorter events, 3.6 us)
Async XLA Ops:
  0.7 82.8 %copy-start.70 = (s32[1,4]{1,0:T(1,128)S(1)}, s32[1,4]{1,0:T(1,128)}, u32[]{:S(2)}) copy-start(s32[1,4]{1,0:T(1,128)} %ranks.11) | copy-start | bytes 52
  3.1 15.2 %collective-permute-start.10 = (bf16[384,512]{1,0:T(8,128)(2,1)S(1)}, bf16[384,512]{1,0:T(8,128)(2,1)S(1)}, u32[]{:S(2)}, u32[]{:S(2)}) collective-permute-start(bf16[384,512]{1,0:T(8,128)(2,1)S(1)} %get-tuple-element.157), channel_id=1, source_target_pairs={{0,8},{8,16},{16,24},{24,0},{1,9},{9,17},{17,25},{25,1},{2,10},{10... | collective-permute-start | bytes 1179656 | tf_op jit(solution)/shard_map/ppermute | solution.py:266
  8.4 26.0 %collective-permute-start.18 = (bf16[384,512]{1,0:T(8,128)(2,1)S(1)}, bf16[384,512]{1,0:T(8,128)(2,1)S(1)}, u32[]{:S(2)}, u32[]{:S(2)}) collective-permute-start(bf16[384,512]{1,0:T(8,128)(2,1)S(1)} %get-tuple-element.158), channel_id=1, source_target_pairs={{0,16},{8,24},{16,0},{24,8},{1,17},{9,25},{17,1},{25,9},{2,18},{10... | collective-permute-start | bytes 1179656 | tf_op jit(solution)/shard_map/ppermute | solution.py:266
  11.0 24.8 %collective-permute-start.26 = (bf16[384,512]{1,0:T(8,128)(2,1)S(1)}, bf16[384,512]{1,0:T(8,128)(2,1)S(1)}, u32[]{:S(2)}, u32[]{:S(2)}) collective-permute-start(bf16[384,512]{1,0:T(8,128)(2,1)S(1)} %get-tuple-element.159), channel_id=1, source_target_pairs={{0,24},{8,0},{16,8},{24,16},{1,25},{9,1},{17,9},{25,17},{2,26},{10... | collective-permute-start | bytes 1179656 | tf_op jit(solution)/shard_map/ppermute | solution.py:266
  12.4 23.5 %collective-permute-start.37 = (bf16[3,256,256]{2,1,0:T(8,128)(2,1)S(1)}, bf16[3,256,256]{2,1,0:T(8,128)(2,1)S(1)}, u32[]{:S(2)}, u32[]{:S(2)}) collective-permute-start(bf16[3,256,256]{2,1,0:T(8,128)(2,1)S(1)} %get-tuple-element.164.refs_3_), channel_id=1, source_target_pairs={{0,1},{1,0},{2,3},{3,2},{4,5},{5,4},{6,7},{7,6},{8,9},{9,8},{10,11... | collective-permute-start | bytes 1179656 | tf_op jit(solution)/shard_map/ppermute | solution.py:59
  12.4 24.6 %collective-permute-start.38 = (bf16[3,256,256]{2,1,0:T(8,128)(2,1)S(1)}, bf16[3,256,256]{2,1,0:T(8,128)(2,1)S(1)}, u32[]{:S(2)}, u32[]{:S(2)}) collective-permute-start(bf16[3,256,256]{2,1,0:T(8,128)(2,1)S(1)} %get-tuple-element.164.refs_3_), channel_id=1, source_target_pairs={{0,2},{1,5},{2,0},{3,7},{4,6},{5,1},{6,4},{7,3},{8,10},{9,13},{10,... | collective-permute-start | bytes 1179656 | tf_op jit(solution)/shard_map/ppermute | solution.py:58
  18.3 100.6 %copy-start.21 = (bf16[384,512]{1,0:T(8,128)(2,1)}, bf16[384,512]{1,0:T(8,128)(2,1)S(1)}, u32[]{:S(2)}) copy-start(bf16[384,512]{1,0:T(8,128)(2,1)S(1)} %collective-permute-done.10.refs_1_.refs_16_) | copy-start | bytes 1179652
  18.3 19.3 %collective-permute-start.11 = (bf16[384,512]{1,0:T(8,128)(2,1)S(1)}, bf16[384,512]{1,0:T(8,128)(2,1)S(1)}, u32[]{:S(2)}, u32[]{:S(2)}) collective-permute-start(bf16[384,512]{1,0:T(8,128)(2,1)S(1)} %collective-permute-done.10.refs_1_.refs_16_), channel_id=1, source_target_pairs={{0,1},{1,0},{2,3},{3,2},{4,5},{5,4},{6,7},{7,6},{8,9},{9,8},{10,11... | collective-permute-start | bytes 1179656 | tf_op jit(solution)/shard_map/ppermute | solution.py:59
  34.3 84.6 %copy-start.23 = (bf16[384,512]{1,0:T(8,128)(2,1)}, bf16[384,512]{1,0:T(8,128)(2,1)S(1)}, u32[]{:S(2)}) copy-start(bf16[384,512]{1,0:T(8,128)(2,1)S(1)} %collective-permute-done.18.refs_9_.refs_24_) | copy-start | bytes 1179652
  34.3 7.8 %collective-permute-start.12 = (bf16[384,512]{1,0:T(8,128)(2,1)S(1)}, bf16[384,512]{1,0:T(8,128)(2,1)S(1)}, u32[]{:S(2)}, u32[]{:S(2)}) collective-permute-start(bf16[384,512]{1,0:T(8,128)(2,1)S(1)} %collective-permute-done.10.refs_1_.refs_16_), channel_id=1, source_target_pairs={{0,2},{1,5},{2,0},{3,7},{4,6},{5,1},{6,4},{7,3},{8,10},{9,13},{10,... | collective-permute-start | bytes 1179656 | tf_op jit(solution)/shard_map/ppermute | solution.py:58
  35.8 83.1 %copy-start.25 = (bf16[384,512]{1,0:T(8,128)(2,1)}, bf16[384,512]{1,0:T(8,128)(2,1)S(1)}, u32[]{:S(2)}) copy-start(bf16[384,512]{1,0:T(8,128)(2,1)S(1)} %collective-permute-done.26.refs_17_.refs_32_) | copy-start | bytes 1179652
  35.8 7.8 %collective-permute-start.19 = (bf16[384,512]{1,0:T(8,128)(2,1)S(1)}, bf16[384,512]{1,0:T(8,128)(2,1)S(1)}, u32[]{:S(2)}, u32[]{:S(2)}) collective-permute-start(bf16[384,512]{1,0:T(8,128)(2,1)S(1)} %collective-permute-done.18.refs_9_.refs_24_), channel_id=1, source_target_pairs={{0,1},{1,0},{2,3},{3,2},{4,5},{5,4},{6,7},{7,6},{8,9},{9,8},{10,11... | collective-permute-start | bytes 1179656 | tf_op jit(solution)/shard_map/ppermute | solution.py:59
  35.8 10.5 %collective-permute-start.20 = (bf16[384,512]{1,0:T(8,128)(2,1)S(1)}, bf16[384,512]{1,0:T(8,128)(2,1)S(1)}, u32[]{:S(2)}, u32[]{:S(2)}) collective-permute-start(bf16[384,512]{1,0:T(8,128)(2,1)S(1)} %collective-permute-done.18.refs_9_.refs_24_), channel_id=1, source_target_pairs={{0,2},{1,5},{2,0},{3,7},{4,6},{5,1},{6,4},{7,3},{8,10},{9,13},{10,... | collective-permute-start | bytes 1179656 | tf_op jit(solution)/shard_map/ppermute | solution.py:58
  37.0 10.8 %collective-permute-start.27 = (bf16[384,512]{1,0:T(8,128)(2,1)S(1)}, bf16[384,512]{1,0:T(8,128)(2,1)S(1)}, u32[]{:S(2)}, u32[]{:S(2)}) collective-permute-start(bf16[384,512]{1,0:T(8,128)(2,1)S(1)} %collective-permute-done.26.refs_17_.refs_32_), channel_id=1, source_target_pairs={{0,1},{1,0},{2,3},{3,2},{4,5},{5,4},{6,7},{7,6},{8,9},{9,8},{10,11... | collective-permute-start | bytes 1179656 | tf_op jit(solution)/shard_map/ppermute | solution.py:59
  37.6 81.3 %copy-start.27 = (bf16[384,512]{1,0:T(8,128)(2,1)}, bf16[384,512]{1,0:T(8,128)(2,1)S(1)}, u32[]{:S(2)}) copy-start(bf16[384,512]{1,0:T(8,128)(2,1)S(1)} %collective-permute-done.11.refs_2_.refs_17_) | copy-start | bytes 1179652
  37.6 15.5 %collective-permute-start.28 = (bf16[384,512]{1,0:T(8,128)(2,1)S(1)}, bf16[384,512]{1,0:T(8,128)(2,1)S(1)}, u32[]{:S(2)}, u32[]{:S(2)}) collective-permute-start(bf16[384,512]{1,0:T(8,128)(2,1)S(1)} %collective-permute-done.26.refs_17_.refs_32_), channel_id=1, source_target_pairs={{0,2},{1,5},{2,0},{3,7},{4,6},{5,1},{6,4},{7,3},{8,10},{9,13},{10,... | collective-permute-start | bytes 1179656 | tf_op jit(solution)/shard_map/ppermute | solution.py:58
  42.1 76.8 %copy-start.29 = (bf16[384,512]{1,0:T(8,128)(2,1)}, bf16[384,512]{1,0:T(8,128)(2,1)S(1)}, u32[]{:S(2)}) copy-start(bf16[384,512]{1,0:T(8,128)(2,1)S(1)} %collective-permute-done.12.refs_3_.refs_18_) | copy-start | bytes 1179652
  42.1 16.9 %collective-permute-start.39 = (bf16[3,256,256]{2,1,0:T(8,128)(2,1)S(1)}, bf16[3,256,256]{2,1,0:T(8,128)(2,1)S(1)}, u32[]{:S(2)}, u32[]{:S(2)}) collective-permute-start(bf16[3,256,256]{2,1,0:T(8,128)(2,1)S(1)} %collective-permute-done.37.refs_4_), channel_id=1, source_target_pairs={{0,2},{1,5},{2,0},{3,7},{4,6},{5,1},{6,4},{7,3},{8,10},{9,13},{10,... | collective-permute-start | bytes 1179656 | tf_op jit(solution)/shard_map/ppermute | solution.py:60
  43.6 75.3 %copy-start.31 = (bf16[384,512]{1,0:T(8,128)(2,1)}, bf16[384,512]{1,0:T(8,128)(2,1)S(1)}, u32[]{:S(2)}) copy-start(bf16[384,512]{1,0:T(8,128)(2,1)S(1)} %collective-permute-done.19.refs_10_.refs_25_) | copy-start | bytes 1179652
  43.6 22.5 %collective-permute-start.13 = (bf16[384,512]{1,0:T(8,128)(2,1)S(1)}, bf16[384,512]{1,0:T(8,128)(2,1)S(1)}, u32[]{:S(2)}, u32[]{:S(2)}) collective-permute-start(bf16[384,512]{1,0:T(8,128)(2,1)S(1)} %collective-permute-done.11.refs_2_.refs_17_), channel_id=1, source_target_pairs={{0,2},{1,5},{2,0},{3,7},{4,6},{5,1},{6,4},{7,3},{8,10},{9,13},{10,... | collective-permute-start | bytes 1179656 | tf_op jit(solution)/shard_map/ppermute | solution.py:60
  46.3 72.6 %copy-start.33 = (bf16[384,512]{1,0:T(8,128)(2,1)}, bf16[384,512]{1,0:T(8,128)(2,1)S(1)}, u32[]{:S(2)}) copy-start(bf16[384,512]{1,0:T(8,128)(2,1)S(1)} %collective-permute-done.20.refs_11_.refs_26_) | copy-start | bytes 1179652
  46.3 19.8 %collective-permute-start.14 = (bf16[384,512]{1,0:T(8,128)(2,1)S(1)}, bf16[384,512]{1,0:T(8,128)(2,1)S(1)}, u32[]{:S(2)}, u32[]{:S(2)}) collective-permute-start(bf16[384,512]{1,0:T(8,128)(2,1)S(1)} %collective-permute-done.12.refs_3_.refs_18_), channel_id=1, source_target_pairs={{0,4},{1,3},{2,6},{3,1},{4,0},{5,7},{6,2},{7,5},{8,12},{9,11},{10,... | collective-permute-start | bytes 1179656 | tf_op jit(solution)/shard_map/ppermute | solution.py:61
  47.8 71.1 %copy-start.35 = (bf16[384,512]{1,0:T(8,128)(2,1)}, bf16[384,512]{1,0:T(8,128)(2,1)S(1)}, u32[]{:S(2)}) copy-start(bf16[384,512]{1,0:T(8,128)(2,1)S(1)} %collective-permute-done.27.refs_18_.refs_33_) | copy-start | bytes 1179652
  47.8 19.9 %collective-permute-start.15 = (bf16[384,512]{1,0:T(8,128)(2,1)S(1)}, bf16[384,512]{1,0:T(8,128)(2,1)S(1)}, u32[]{:S(2)}, u32[]{:S(2)}) collective-permute-start(bf16[384,512]{1,0:T(8,128)(2,1)S(1)} %collective-permute-done.12.refs_3_.refs_18_), channel_id=1, source_target_pairs={{0,1},{1,0},{2,3},{3,2},{4,5},{5,4},{6,7},{7,6},{8,9},{9,8},{10,11... | collective-permute-start | bytes 1179656 | tf_op jit(solution)/shard_map/ppermute | solution.py:62
  53.1 65.9 %copy-start.37 = (bf16[384,512]{1,0:T(8,128)(2,1)}, bf16[384,512]{1,0:T(8,128)(2,1)S(1)}, u32[]{:S(2)}) copy-start(bf16[384,512]{1,0:T(8,128)(2,1)S(1)} %collective-permute-done.28.refs_19_.refs_34_) | copy-start | bytes 1179652
  53.1 19.6 %collective-permute-start.21 = (bf16[384,512]{1,0:T(8,128)(2,1)S(1)}, bf16[384,512]{1,0:T(8,128)(2,1)S(1)}, u32[]{:S(2)}, u32[]{:S(2)}) collective-permute-start(bf16[384,512]{1,0:T(8,128)(2,1)S(1)} %collective-permute-done.19.refs_10_.refs_25_), channel_id=1, source_target_pairs={{0,2},{1,5},{2,0},{3,7},{4,6},{5,1},{6,4},{7,3},{8,10},{9,13},{10,... | collective-permute-start | bytes 1179656 | tf_op jit(solution)/shard_map/ppermute | solution.py:60
  59.0 60.0 %copy-start = (bf16[3,256,256]{2,1,0:T(8,128)(2,1)}, bf16[3,256,256]{2,1,0:T(8,128)(2,1)S(1)}, u32[]{:S(2)}) copy-start(bf16[3,256,256]{2,1,0:T(8,128)(2,1)S(1)} %collective-permute-done.39.refs_6_) | copy-start | bytes 1179652
  59.0 13.8 %collective-permute-start.22 = (bf16[384,512]{1,0:T(8,128)(2,1)S(1)}, bf16[384,512]{1,0:T(8,128)(2,1)S(1)}, u32[]{:S(2)}, u32[]{:S(2)}) collective-permute-start(bf16[384,512]{1,0:T(8,128)(2,1)S(1)} %collective-permute-done.20.refs_11_.refs_26_), channel_id=1, source_target_pairs={{0,4},{1,3},{2,6},{3,1},{4,0},{5,7},{6,2},{7,5},{8,12},{9,11},{10,... | collective-permute-start | bytes 1179656 | tf_op jit(solution)/shard_map/ppermute | solution.py:61
  66.1 52.9 %copy-start.39 = (bf16[384,512]{1,0:T(8,128)(2,1)}, bf16[384,512]{1,0:T(8,128)(2,1)S(1)}, u32[]{:S(2)}) copy-start(bf16[384,512]{1,0:T(8,128)(2,1)S(1)} %collective-permute-done.13.refs_4_.refs_19_) | copy-start | bytes 1179652
  66.1 7.1 %collective-permute-start.23 = (bf16[384,512]{1,0:T(8,128)(2,1)S(1)}, bf16[384,512]{1,0:T(8,128)(2,1)S(1)}, u32[]{:S(2)}, u32[]{:S(2)}) collective-permute-start(bf16[384,512]{1,0:T(8,128)(2,1)S(1)} %collective-permute-done.20.refs_11_.refs_26_), channel_id=1, source_target_pairs={{0,1},{1,0},{2,3},{3,2},{4,5},{5,4},{6,7},{7,6},{8,9},{9,8},{10,11... | collective-permute-start | bytes 1179656 | tf_op jit(solution)/shard_map/ppermute | solution.py:62
  66.1 52.9 %copy-start.41 = (bf16[384,512]{1,0:T(8,128)(2,1)}, bf16[384,512]{1,0:T(8,128)(2,1)S(1)}, u32[]{:S(2)}) copy-start(bf16[384,512]{1,0:T(8,128)(2,1)S(1)} %collective-permute-done.14.refs_5_.refs_20_) | copy-start | bytes 1179652
  66.1 13.9 %collective-permute-start.29 = (bf16[384,512]{1,0:T(8,128)(2,1)S(1)}, bf16[384,512]{1,0:T(8,128)(2,1)S(1)}, u32[]{:S(2)}, u32[]{:S(2)}) collective-permute-start(bf16[384,512]{1,0:T(8,128)(2,1)S(1)} %collective-permute-done.27.refs_18_.refs_33_), channel_id=1, source_target_pairs={{0,2},{1,5},{2,0},{3,7},{4,6},{5,1},{6,4},{7,3},{8,10},{9,13},{10,... | collective-permute-start | bytes 1179656 | tf_op jit(solution)/shard_map/ppermute | solution.py:60
  67.7 51.3 %copy-start.43 = (bf16[384,512]{1,0:T(8,128)(2,1)}, bf16[384,512]{1,0:T(8,128)(2,1)S(1)}, u32[]{:S(2)}) copy-start(bf16[384,512]{1,0:T(8,128)(2,1)S(1)} %collective-permute-done.15.refs_6_.refs_21_) | copy-start | bytes 1179652
  67.7 12.3 %collective-permute-start.30 = (bf16[384,512]{1,0:T(8,128)(2,1)S(1)}, bf16[384,512]{1,0:T(8,128)(2,1)S(1)}, u32[]{:S(2)}, u32[]{:S(2)}) collective-permute-start(bf16[384,512]{1,0:T(8,128)(2,1)S(1)} %collective-permute-done.28.refs_19_.refs_34_), channel_id=1, source_target_pairs={{0,4},{1,3},{2,6},{3,1},{4,0},{5,7},{6,2},{7,5},{8,12},{9,11},{10,... | collective-permute-start | bytes 1179656 | tf_op jit(solution)/shard_map/ppermute | solution.py:61
  72.7 46.3 %copy-start.45 = (bf16[384,512]{1,0:T(8,128)(2,1)}, bf16[384,512]{1,0:T(8,128)(2,1)S(1)}, u32[]{:S(2)}) copy-start(bf16[384,512]{1,0:T(8,128)(2,1)S(1)} %collective-permute-done.21.refs_12_.refs_27_) | copy-start | bytes 1179652
  72.7 7.8 %collective-permute-start.31 = (bf16[384,512]{1,0:T(8,128)(2,1)S(1)}, bf16[384,512]{1,0:T(8,128)(2,1)S(1)}, u32[]{:S(2)}, u32[]{:S(2)}) collective-permute-start(bf16[384,512]{1,0:T(8,128)(2,1)S(1)} %collective-permute-done.28.refs_19_.refs_34_), channel_id=1, source_target_pairs={{0,1},{1,0},{2,3},{3,2},{4,5},{5,4},{6,7},{7,6},{8,9},{9,8},{10,11... | collective-permute-start | bytes 1179656 | tf_op jit(solution)/shard_map/ppermute | solution.py:62
  72.7 46.3 %copy-start.47 = (bf16[384,512]{1,0:T(8,128)(2,1)}, bf16[384,512]{1,0:T(8,128)(2,1)S(1)}, u32[]{:S(2)}) copy-start(bf16[384,512]{1,0:T(8,128)(2,1)S(1)} %collective-permute-done.22.refs_13_.refs_28_) | copy-start | bytes 1179652
  72.7 7.9 %collective-permute-start.16 = (bf16[384,512]{1,0:T(8,128)(2,1)S(1)}, bf16[384,512]{1,0:T(8,128)(2,1)S(1)}, u32[]{:S(2)}, u32[]{:S(2)}) collective-permute-start(bf16[384,512]{1,0:T(8,128)(2,1)S(1)} %collective-permute-done.13.refs_4_.refs_19_), channel_id=1, source_target_pairs={{0,1},{1,0},{2,3},{3,2},{4,5},{5,4},{6,7},{7,6},{8,9},{9,8},{10,11... | collective-permute-start | bytes 1179656 | tf_op jit(solution)/shard_map/ppermute | solution.py:62
  73.2 45.8 %copy-start.49 = (bf16[384,512]{1,0:T(8,128)(2,1)}, bf16[384,512]{1,0:T(8,128)(2,1)S(1)}, u32[]{:S(2)}) copy-start(bf16[384,512]{1,0:T(8,128)(2,1)S(1)} %collective-permute-done.23.refs_14_.refs_29_) | copy-start | bytes 1179652
  73.2 7.8 %collective-permute-start.17 = (bf16[384,512]{1,0:T(8,128)(2,1)S(1)}, bf16[384,512]{1,0:T(8,128)(2,1)S(1)}, u32[]{:S(2)}, u32[]{:S(2)}) collective-permute-start(bf16[384,512]{1,0:T(8,128)(2,1)S(1)} %collective-permute-done.14.refs_5_.refs_20_), channel_id=1, source_target_pairs={{0,1},{1,0},{2,3},{3,2},{4,5},{5,4},{6,7},{7,6},{8,9},{9,8},{10,11... | collective-permute-start | bytes 1179656 | tf_op jit(solution)/shard_map/ppermute | solution.py:70
  80.0 39.0 %copy-start.51 = (bf16[384,512]{1,0:T(8,128)(2,1)}, bf16[384,512]{1,0:T(8,128)(2,1)S(1)}, u32[]{:S(2)}) copy-start(bf16[384,512]{1,0:T(8,128)(2,1)S(1)} %collective-permute-done.29.refs_20_.refs_35_) | copy-start | bytes 1179652
  80.0 2.6 %collective-permute-start.24 = (bf16[384,512]{1,0:T(8,128)(2,1)S(1)}, bf16[384,512]{1,0:T(8,128)(2,1)S(1)}, u32[]{:S(2)}, u32[]{:S(2)}) collective-permute-start(bf16[384,512]{1,0:T(8,128)(2,1)S(1)} %collective-permute-done.21.refs_12_.refs_27_), channel_id=1, source_target_pairs={{0,1},{1,0},{2,3},{3,2},{4,5},{5,4},{6,7},{7,6},{8,9},{9,8},{10,11... | collective-permute-start | bytes 1179656 | tf_op jit(solution)/shard_map/ppermute | solution.py:62
  80.0 39.0 %copy-start.53 = (bf16[384,512]{1,0:T(8,128)(2,1)}, bf16[384,512]{1,0:T(8,128)(2,1)S(1)}, u32[]{:S(2)}) copy-start(bf16[384,512]{1,0:T(8,128)(2,1)S(1)} %collective-permute-done.30.refs_21_.refs_36_) | copy-start | bytes 1179652
  80.0 2.6 %collective-permute-start.25 = (bf16[384,512]{1,0:T(8,128)(2,1)S(1)}, bf16[384,512]{1,0:T(8,128)(2,1)S(1)}, u32[]{:S(2)}, u32[]{:S(2)}) collective-permute-start(bf16[384,512]{1,0:T(8,128)(2,1)S(1)} %collective-permute-done.22.refs_13_.refs_28_), channel_id=1, source_target_pairs={{0,1},{1,0},{2,3},{3,2},{4,5},{5,4},{6,7},{7,6},{8,9},{9,8},{10,11... | collective-permute-start | bytes 1179656 | tf_op jit(solution)/shard_map/ppermute | solution.py:70
  80.5 38.5 %copy-start.55 = (bf16[384,512]{1,0:T(8,128)(2,1)}, bf16[384,512]{1,0:T(8,128)(2,1)S(1)}, u32[]{:S(2)}) copy-start(bf16[384,512]{1,0:T(8,128)(2,1)S(1)} %collective-permute-done.31.refs_22_.refs_37_) | copy-start | bytes 1179652
  80.6 2.6 %collective-permute-start.32 = (bf16[384,512]{1,0:T(8,128)(2,1)S(1)}, bf16[384,512]{1,0:T(8,128)(2,1)S(1)}, u32[]{:S(2)}, u32[]{:S(2)}) collective-permute-start(bf16[384,512]{1,0:T(8,128)(2,1)S(1)} %collective-permute-done.29.refs_20_.refs_35_), channel_id=1, source_target_pairs={{0,1},{1,0},{2,3},{3,2},{4,5},{5,4},{6,7},{7,6},{8,9},{9,8},{10,11... | collective-permute-start | bytes 1179656 | tf_op jit(solution)/shard_map/ppermute | solution.py:62
  80.6 38.4 %copy-start.57 = (bf16[384,512]{1,0:T(8,128)(2,1)}, bf16[384,512]{1,0:T(8,128)(2,1)S(1)}, u32[]{:S(2)}) copy-start(bf16[384,512]{1,0:T(8,128)(2,1)S(1)} %collective-permute-done.16.refs_7_.refs_22_) | copy-start | bytes 1179652
  80.6 2.8 %collective-permute-start.33 = (bf16[384,512]{1,0:T(8,128)(2,1)S(1)}, bf16[384,512]{1,0:T(8,128)(2,1)S(1)}, u32[]{:S(2)}, u32[]{:S(2)}) collective-permute-start(bf16[384,512]{1,0:T(8,128)(2,1)S(1)} %collective-permute-done.30.refs_21_.refs_36_), channel_id=1, source_target_pairs={{0,1},{1,0},{2,3},{3,2},{4,5},{5,4},{6,7},{7,6},{8,9},{9,8},{10,11... | collective-permute-start | bytes 1179656 | tf_op jit(solution)/shard_map/ppermute | solution.py:70
  81.1 7.8 %collective-permute-start.40 = (bf16[3,256,256]{2,1,0:T(8,128)(2,1)S(1)}, bf16[3,256,256]{2,1,0:T(8,128)(2,1)S(1)}, u32[]{:S(2)}, u32[]{:S(2)}) collective-permute-start(bf16[3,256,256]{2,1,0:T(8,128)(2,1)S(1)} %collective-permute-done.38.refs_5_), channel_id=1, source_target_pairs={{0,4},{1,3},{2,6},{3,1},{4,0},{5,7},{6,2},{7,5},{8,12},{9,11},{10,... | collective-permute-start | bytes 1179656 | tf_op jit(solution)/shard_map/ppermute | solution.py:61
  82.6 16.0 %collective-permute-start.41 = (bf16[3,256,256]{2,1,0:T(8,128)(2,1)S(1)}, bf16[3,256,256]{2,1,0:T(8,128)(2,1)S(1)}, u32[]{:S(2)}, u32[]{:S(2)}) collective-permute-start(bf16[3,256,256]{2,1,0:T(8,128)(2,1)S(1)} %collective-permute-done.38.refs_5_), channel_id=1, source_target_pairs={{0,1},{1,0},{2,3},{3,2},{4,5},{5,4},{6,7},{7,6},{8,9},{9,8},{10,11... | collective-permute-start | bytes 1179656 | tf_op jit(solution)/shard_map/ppermute | solution.py:62
  82.6 16.6 %collective-permute-start.42 = (bf16[3,256,256]{2,1,0:T(8,128)(2,1)S(1)}, bf16[3,256,256]{2,1,0:T(8,128)(2,1)S(1)}, u32[]{:S(2)}, u32[]{:S(2)}) collective-permute-start(bf16[3,256,256]{2,1,0:T(8,128)(2,1)S(1)} %collective-permute-done.39.refs_6_), channel_id=1, source_target_pairs={{0,1},{1,0},{2,3},{3,2},{4,5},{5,4},{6,7},{7,6},{8,9},{9,8},{10,11... | collective-permute-start | bytes 1179656 | tf_op jit(solution)/shard_map/ppermute | solution.py:62
  88.9 16.8 %collective-permute-start.43 = (bf16[3,256,256]{2,1,0:T(8,128)(2,1)S(1)}, bf16[3,256,256]{2,1,0:T(8,128)(2,1)S(1)}, u32[]{:S(2)}, u32[]{:S(2)}) collective-permute-start(bf16[3,256,256]{2,1,0:T(8,128)(2,1)S(1)} %collective-permute-done.40.refs_7_), channel_id=1, source_target_pairs={{0,1},{1,0},{2,3},{3,2},{4,5},{5,4},{6,7},{7,6},{8,9},{9,8},{10,11... | collective-permute-start | bytes 1179656 | tf_op jit(solution)/shard_map/ppermute | solution.py:70
  88.9 12.3 %collective-permute-start.34 = (bf16[256,128]{1,0:T(8,128)(2,1)S(1)}, bf16[256,128]{1,0:T(8,128)(2,1)S(1)}, u32[]{:S(2)}, u32[]{:S(2)}) collective-permute-start(bf16[256,128]{1,0:T(8,128)(2,1)S(1)} %get-tuple-element.161), channel_id=1, source_target_pairs={{0,24},{8,0},{16,8},{24,16},{1,25},{9,1},{17,9},{25,17},{2,26},{10... | collective-permute-start | bytes 196616 | tf_op jit(solution)/shard_map/ppermute | solution.py:266
  98.6 7.0 %collective-permute-start.35 = (bf16[256,128]{1,0:T(8,128)(2,1)S(1)}, bf16[256,128]{1,0:T(8,128)(2,1)S(1)}, u32[]{:S(2)}, u32[]{:S(2)}) collective-permute-start(bf16[256,128]{1,0:T(8,128)(2,1)S(1)} %get-tuple-element.162), channel_id=1, source_target_pairs={{0,16},{8,24},{16,0},{24,8},{1,17},{9,25},{17,1},{25,9},{2,18},{10... | collective-permute-start | bytes 196616 | tf_op jit(solution)/shard_map/ppermute | solution.py:266
  98.6 7.0 %collective-permute-start.36 = (bf16[256,128]{1,0:T(8,128)(2,1)S(1)}, bf16[256,128]{1,0:T(8,128)(2,1)S(1)}, u32[]{:S(2)}, u32[]{:S(2)}) collective-permute-start(bf16[256,128]{1,0:T(8,128)(2,1)S(1)} %get-tuple-element.163), channel_id=1, source_target_pairs={{0,8},{8,16},{16,24},{24,0},{1,9},{9,17},{17,25},{25,1},{2,10},{10... | collective-permute-start | bytes 196616 | tf_op jit(solution)/shard_map/ppermute | solution.py:266
  110.9 4.9 %collective-permute-start.44 = (bf16[256,128]{1,0:T(8,128)(2,1)S(1)}, bf16[256,128]{1,0:T(8,128)(2,1)S(1)}, u32[]{:S(2)}, u32[]{:S(2)}) collective-permute-start(bf16[256,128]{1,0:T(8,128)(2,1)S(1)} %get-tuple-element.171), channel_id=1, source_target_pairs={{0,24},{8,0},{16,8},{24,16},{1,25},{9,1},{17,9},{25,17},{2,26},{10... | collective-permute-start | bytes 196616 | tf_op jit(solution)/shard_map/ppermute | solution.py:266
  110.9 8.0 %collective-permute-start.45 = (bf16[256,128]{1,0:T(8,128)(2,1)S(1)}, bf16[256,128]{1,0:T(8,128)(2,1)S(1)}, u32[]{:S(2)}, u32[]{:S(2)}) collective-permute-start(bf16[256,128]{1,0:T(8,128)(2,1)S(1)} %get-tuple-element.172), channel_id=1, source_target_pairs={{0,16},{8,24},{16,0},{24,8},{1,17},{9,25},{17,1},{25,9},{2,18},{10... | collective-permute-start | bytes 196616 | tf_op jit(solution)/shard_map/ppermute | solution.py:266
  111.0 7.9 %collective-permute-start.46 = (bf16[256,128]{1,0:T(8,128)(2,1)S(1)}, bf16[256,128]{1,0:T(8,128)(2,1)S(1)}, u32[]{:S(2)}, u32[]{:S(2)}) collective-permute-start(bf16[256,128]{1,0:T(8,128)(2,1)S(1)} %get-tuple-element.173), channel_id=1, source_target_pairs={{0,8},{8,16},{16,24},{24,0},{1,9},{9,17},{17,25},{25,1},{2,10},{10... | collective-permute-start | bytes 196616 | tf_op jit(solution)/shard_map/ppermute | solution.py:266
  124.4 9.1 %collective-permute-start.47 = (bf16[256,128]{1,0:T(8,128)(2,1)}, bf16[256,128]{1,0:T(8,128)(2,1)S(1)}, u32[]{:S(2)}, u32[]{:S(2)}) collective-permute-start(bf16[256,128]{1,0:T(8,128)(2,1)} %get-tuple-element.179), channel_id=1, source_target_pairs={{0,24},{8,0},{16,8},{24,16},{1,25},{9,1},{17,9},{25,17},{2,26},{10... | collective-permute-start | bytes 196616 | tf_op jit(solution)/shard_map/ppermute | solution.py:266
  125.7 11.0 %collective-permute-start.48 = (bf16[256,128]{1,0:T(8,128)(2,1)}, bf16[256,128]{1,0:T(8,128)(2,1)S(1)}, u32[]{:S(2)}, u32[]{:S(2)}) collective-permute-start(bf16[256,128]{1,0:T(8,128)(2,1)} %get-tuple-element.180), channel_id=1, source_target_pairs={{0,16},{8,24},{16,0},{24,8},{1,17},{9,25},{17,1},{25,9},{2,18},{10... | collective-permute-start | bytes 196616 | tf_op jit(solution)/shard_map/ppermute | solution.py:266
  130.0 6.7 %collective-permute-start.49 = (bf16[256,128]{1,0:T(8,128)(2,1)S(1)}, bf16[256,128]{1,0:T(8,128)(2,1)S(1)}, u32[]{:S(2)}, u32[]{:S(2)}) collective-permute-start(bf16[256,128]{1,0:T(8,128)(2,1)S(1)} %get-tuple-element.181), channel_id=1, source_target_pairs={{0,8},{8,16},{16,24},{24,0},{1,9},{9,17},{17,25},{25,1},{2,10},{10... | collective-permute-start | bytes 196616 | tf_op jit(solution)/shard_map/ppermute | solution.py:266
  153.5 8.0 %collective-permute-start.50 = (bf16[512,128]{1,0:T(8,128)(2,1)}, bf16[512,128]{1,0:T(8,128)(2,1)S(1)}, u32[]{:S(2)}, u32[]{:S(2)}) collective-permute-start(bf16[512,128]{1,0:T(8,128)(2,1)} %get-tuple-element.187), channel_id=1, source_target_pairs={{0,8},{8,16},{16,24},{24,0},{1,9},{9,17},{17,25},{25,1},{2,10},{10... | collective-permute-start | bytes 393224 | tf_op jit(solution)/shard_map/ppermute | solution.py:266
  156.9 9.3 %collective-permute-start.51 = (bf16[512,128]{1,0:T(8,128)(2,1)}, bf16[512,128]{1,0:T(8,128)(2,1)S(1)}, u32[]{:S(2)}, u32[]{:S(2)}) collective-permute-start(bf16[512,128]{1,0:T(8,128)(2,1)} %get-tuple-element.188), channel_id=1, source_target_pairs={{0,16},{8,24},{16,0},{24,8},{1,17},{9,25},{17,1},{25,9},{2,18},{10... | collective-permute-start | bytes 393224 | tf_op jit(solution)/shard_map/ppermute | solution.py:266
  156.9 9.3 %collective-permute-start.52 = (bf16[512,128]{1,0:T(8,128)(2,1)}, bf16[512,128]{1,0:T(8,128)(2,1)S(1)}, u32[]{:S(2)}, u32[]{:S(2)}) collective-permute-start(bf16[512,128]{1,0:T(8,128)(2,1)} %get-tuple-element.189), channel_id=1, source_target_pairs={{0,24},{8,0},{16,8},{24,16},{1,25},{9,1},{17,9},{25,17},{2,26},{10... | collective-permute-start | bytes 393224 | tf_op jit(solution)/shard_map/ppermute | solution.py:266
  (50 other events, 475.9 us)

commit v2 on v1

--- a/solution.py
+++ b/solution.py
@@ -186,21 +186,27 @@
     def _():
         piece = own_diag.shape[0]
         rows = piece // 8
-        for block in range(n_rows):
-            at = slice(block * piece, (block + 1) * piece)
-            rounded = residual[at, :].astype(BF16)
-            for delta in range(n_rows):
-                source = around(me - delta, n_rows)
-
-                @pl.when(source >= block)
-                def _():
-                    if delta:
-                        refs_of = packed_refs[8 * (delta - 1) : 8 * delta]
-                        sent = jnp.concatenate([ref[block * rows : (block + 1) * rows, :] for ref in refs_of])
-                    else:
-                        sent = own_diag[:, at]
-                    product = jnp.dot(sent, rounded, preferred_element_type=F32)
-                    products[delta] = products[delta] + product if block else product
+        rounded = residual[...].astype(BF16)
+        half = n_rows // 2
+
+        def product(delta, first):
+            at = slice(first * piece, (first + half) * piece)
+            if not delta:
+                return jnp.dot(own_diag[:, at], rounded[at], preferred_element_type=F32)
+            blocks = range(first, first + half)
+            sent = [
+                jnp.concatenate([ref[b * rows : (b + 1) * rows, :] for b in blocks], axis=1)
+                for ref in packed_refs[8 * (delta - 1) : 8 * delta]
+            ]
+            return jnp.dot(jnp.concatenate(sent), rounded[at], preferred_element_type=F32)
+
+        for delta in range(n_rows):
+            products[delta] = product(delta, 0)
+        for delta in range(n_rows):
+
+            @pl.when(around(me - delta, n_rows) >= half)
+            def _():
+                products[delta] = products[delta] + product(delta, half)
 
         for delta in range(n_rows):
             base = around(me - delta, n_rows) * piece

time: 169 us -> 167 us (0.988)
  starting transfers between devices: 51.6 us -> 49.9 us
    ppermute x15, starting transfers between devices: 33.1 us -> 31.4 us  [shifted(): lax.ppermute(array, 'rows', [(i, (i + delta) % n_rows) for i in range(n_r...]
where the time goes in v2:
time: 167 us; the launch traced here: 166 us
  waiting for transfers between devices  80.1 us (48%)
  starting transfers between devices  49.9 us (30%)
  Pallas kernels  19.3 us (12%)
  local copies, waits for them, and re-layouts  13.8 us (8%)
  between operations  2.07 us (1%)
    ppermute x15, waiting for transfers between devices, shifted(): lax.ppermute(array, 'rows', [(i, (i + delta) % n_rows) for i in range(n_r...  43.3 us
    ppermute x15, starting transfers between devices, shifted(): lax.ppermute(array, 'rows', [(i, (i + delta) % n_rows) for i in range(n_r...  31.4 us
    ppermute x4, waiting for transfers between devices, gather_lanes(): near_partner = lax.ppermute(partner, 'rhs', across)  20.2 us
    pallas_call x6, Pallas kernels, call(): pl.pallas_call(kernel, out_shape=out_shape, in_specs=[SMEM, SMEM] + in_sp...  14.7 us
    unnamed x142, local copies, waits for them, and re-layouts  13.8 us
    ppermute x4, waiting for transfers between devices, gather_lanes(): near = lax.ppermute(block, 'rhs', across)  11.4 us
    ppermute x4, starting transfers between devices, gather_lanes(): far = lax.ppermute(near, 'rhs', onward)  6.08 us
    ppermute x4, starting transfers between devices, gather_lanes(): near_partner = lax.ppermute(partner, 'rhs', across)  5.07 us
  transfers between devices with their start and end apart: 43, of which 18 were waited for; matrix products, arithmetic and copies ran while one was open for 0% of the time, Pallas kernels for 2%

profile of v2, /device:TPU:0, one launch (start us, length us, event | category | flops | bytes accessed | tf_op | source)
XLA Modules:
  0.0 165.9 jit_solution(11225812891871413000)
XLA Ops:
  0.7 2.4 %pack.1 = (bf16[384,512]{1,0:T(8,128)(2,1)S(1)}, bf16[384,512]{1,0:T(8,128)(2,1)S(1)}, bf16[384,512]{1,0:T(8,128)(2,1)S(1)}, bf16[3,256,256]{2,1,0:T(8,128)(2,1)S(1)}) custom-call(s32[4]{0:T(128)} %owner.15, bf16[4,512,2048]{2,1,0:T(8,128)(2,1)} %diag.3, bf16[1,4,256,256]{3,2,1,0:T(8,128)(2,1)} %left_v.1, bf16[1,4,256,256]{3,2,1,0:T(8,128)(2,1)} %left_u.1), custom_call_target="tpu_custom_call" | custom-call | tf_op jit(solution)/shard_map/pack/pallas_call | solution.py:279
  3.1 3.1 %collective-permute-start.10 = (bf16[384,512]{1,0:T(8,128)(2,1)S(1)}, bf16[384,512]{1,0:T(8,128)(2,1)S(1)}, u32[]{:S(2)}, u32[]{:S(2)}) collective-permute-start(bf16[384,512]{1,0:T(8,128)(2,1)S(1)} %get-tuple-element.157), channel_id=1, source_target_pairs={{0,8},{8,16},{16,24},{24,0},{1,9},{9,17},{17,25},{25,1},{2,10},{10... | collective-permute-start | bytes 1179656 | tf_op jit(solution)/shard_map/ppermute | solution.py:272
  6.2 2.2 %keep.1 = (bf16[512,2048]{1,0:T(8,128)(2,1)S(1)}, bf16[2048,128]{1,0:T(8,128)(2,1)S(1)}) custom-call(s32[4]{0:T(128)S(1)} %copy-done.69, bf16[4,512,2048]{2,1,0:T(8,128)(2,1)} %diag.3, bf16[1,2048,128]{2,1,0:T(8,128)(2,1)S(1)} %copy-done.12), custom_call_target="tpu_custom_call" | custom-call | tf_op jit(solution)/shard_map/keep/pallas_call | solution.py:291
  8.4 2.7 %collective-permute-start.18 = (bf16[384,512]{1,0:T(8,128)(2,1)S(1)}, bf16[384,512]{1,0:T(8,128)(2,1)S(1)}, u32[]{:S(2)}, u32[]{:S(2)}) collective-permute-start(bf16[384,512]{1,0:T(8,128)(2,1)S(1)} %get-tuple-element.158), channel_id=1, source_target_pairs={{0,16},{8,24},{16,0},{24,8},{1,17},{9,25},{17,1},{25,9},{2,18},{10... | collective-permute-start | bytes 1179656 | tf_op jit(solution)/shard_map/ppermute | solution.py:272
  11.0 1.3 collective-permute-start.26
  12.4 1.5 collective-permute-start.38
  13.9 4.5 %collective-permute-done.10.refs_1_.refs_16_ = bf16[384,512]{1,0:T(8,128)(2,1)S(1)} collective-permute-done((bf16[384,512]{1,0:T(8,128)(2,1)S(1)}, bf16[384,512]{1,0:T(8,128)(2,1)S(1)}, u32[]{:S(2)}, u32[]{:S(2)}) %collective-permute-start.10) | collective-permute-done | bytes 393248 | tf_op jit(solution)/shard_map/ppermute | solution.py:272
  18.3 16.0 %collective-permute-done.18.refs_9_.refs_24_ = bf16[384,512]{1,0:T(8,128)(2,1)S(1)} collective-permute-done((bf16[384,512]{1,0:T(8,128)(2,1)S(1)}, bf16[384,512]{1,0:T(8,128)(2,1)S(1)}, u32[]{:S(2)}, u32[]{:S(2)}) %collective-permute-start.18) | collective-permute-done | bytes 393248 | tf_op jit(solution)/shard_map/ppermute | solution.py:272
  34.3 1.5 collective-permute-start.12
  35.8 1.2 collective-permute-start.20
  37.0 0.6 collective-permute-start.27
  37.6 0.5 collective-permute-start.28
  38.1 4.0 %collective-permute-done.12.refs_3_.refs_18_ = bf16[384,512]{1,0:T(8,128)(2,1)S(1)} collective-permute-done((bf16[384,512]{1,0:T(8,128)(2,1)S(1)}, bf16[384,512]{1,0:T(8,128)(2,1)S(1)}, u32[]{:S(2)}, u32[]{:S(2)}) %collective-permute-start.12) | collective-permute-done | bytes 393248 | tf_op jit(solution)/shard_map/ppermute | solution.py:58
  42.1 1.5 collective-permute-start.39
  44.1 2.2 %collective-permute-done.20.refs_11_.refs_26_ = bf16[384,512]{1,0:T(8,128)(2,1)S(1)} collective-permute-done((bf16[384,512]{1,0:T(8,128)(2,1)S(1)}, bf16[384,512]{1,0:T(8,128)(2,1)S(1)}, u32[]{:S(2)}, u32[]{:S(2)}) %collective-permute-start.20) | collective-permute-done | bytes 393248 | tf_op jit(solution)/shard_map/ppermute | solution.py:58
  46.3 1.5 collective-permute-start.14
  47.9 5.2 %collective-permute-done.28.refs_19_.refs_34_ = bf16[384,512]{1,0:T(8,128)(2,1)S(1)} collective-permute-done((bf16[384,512]{1,0:T(8,128)(2,1)S(1)}, bf16[384,512]{1,0:T(8,128)(2,1)S(1)}, u32[]{:S(2)}, u32[]{:S(2)}) %collective-permute-start.28) | collective-permute-done | bytes 393248 | tf_op jit(solution)/shard_map/ppermute | solution.py:58
  53.1 1.5 collective-permute-start.21
  54.6 4.4 %collective-permute-done.39.refs_6_ = bf16[3,256,256]{2,1,0:T(8,128)(2,1)S(1)} collective-permute-done((bf16[3,256,256]{2,1,0:T(8,128)(2,1)S(1)}, bf16[3,256,256]{2,1,0:T(8,128)(2,1)S(1)}, u32[]{:S(2)}, u32[]{:S(2)}) %collective-permute-start.39) | collective-permute-done | bytes 393248 | tf_op jit(solution)/shard_map/ppermute | solution.py:60
  59.0 1.5 collective-permute-start.22
  60.5 5.6 %collective-permute-done.13.refs_4_.refs_19_ = bf16[384,512]{1,0:T(8,128)(2,1)S(1)} collective-permute-done((bf16[384,512]{1,0:T(8,128)(2,1)S(1)}, bf16[384,512]{1,0:T(8,128)(2,1)S(1)}, u32[]{:S(2)}, u32[]{:S(2)}) %collective-permute-start.13) | collective-permute-done | bytes 393248 | tf_op jit(solution)/shard_map/ppermute | solution.py:60
  66.1 1.6 collective-permute-start.29
  67.7 1.5 collective-permute-start.30
  69.2 3.5 %collective-permute-done.21.refs_12_.refs_27_ = bf16[384,512]{1,0:T(8,128)(2,1)S(1)} collective-permute-done((bf16[384,512]{1,0:T(8,128)(2,1)S(1)}, bf16[384,512]{1,0:T(8,128)(2,1)S(1)}, u32[]{:S(2)}, u32[]{:S(2)}) %collective-permute-start.21) | collective-permute-done | bytes 393248 | tf_op jit(solution)/shard_map/ppermute | solution.py:60
  73.3 6.7 %collective-permute-done.29.refs_20_.refs_35_ = bf16[384,512]{1,0:T(8,128)(2,1)S(1)} collective-permute-done((bf16[384,512]{1,0:T(8,128)(2,1)S(1)}, bf16[384,512]{1,0:T(8,128)(2,1)S(1)}, u32[]{:S(2)}, u32[]{:S(2)}) %collective-permute-start.29) | collective-permute-done | bytes 393248 | tf_op jit(solution)/shard_map/ppermute | solution.py:60
  81.1 1.5 collective-permute-start.40
  83.4 0.6 shard_map.77
  84.1 4.8 %collective-permute-done.40.refs_7_ = bf16[3,256,256]{2,1,0:T(8,128)(2,1)S(1)} collective-permute-done((bf16[3,256,256]{2,1,0:T(8,128)(2,1)S(1)}, bf16[3,256,256]{2,1,0:T(8,128)(2,1)S(1)}, u32[]{:S(2)}, u32[]{:S(2)}) %collective-permute-start.40) | collective-permute-done | bytes 393248 | tf_op jit(solution)/shard_map/ppermute | solution.py:61
  88.9 9.8 %collective-permute-start.34 = (bf16[256,128]{1,0:T(8,128)(2,1)S(1)}, bf16[256,128]{1,0:T(8,128)(2,1)S(1)}, u32[]{:S(2)}, u32[]{:S(2)}) collective-permute-start(bf16[256,128]{1,0:T(8,128)(2,1)S(1)} %get-tuple-element.161), channel_id=1, source_target_pairs={{0,24},{8,0},{16,8},{24,16},{1,25},{9,1},{17,9},{25,17},{2,26},{10... | collective-permute-start | bytes 196616 | tf_op jit(solution)/shard_map/ppermute | solution.py:272
  98.6 0.6 collective-permute-start.36
  99.3 1.9 %collective-permute-done.34.refs_0_ = bf16[256,128]{1,0:T(8,128)(2,1)S(1)} collective-permute-done((bf16[256,128]{1,0:T(8,128)(2,1)S(1)}, bf16[256,128]{1,0:T(8,128)(2,1)S(1)}, u32[]{:S(2)}, u32[]{:S(2)}) %collective-permute-start.34) | collective-permute-done | bytes 65568 | tf_op jit(solution)/shard_map/ppermute | solution.py:272
  101.2 4.4 %collective-permute-done.35.refs_1_ = bf16[256,128]{1,0:T(8,128)(2,1)S(1)} collective-permute-done((bf16[256,128]{1,0:T(8,128)(2,1)S(1)}, bf16[256,128]{1,0:T(8,128)(2,1)S(1)}, u32[]{:S(2)}, u32[]{:S(2)}) %collective-permute-start.35) | collective-permute-done | bytes 65568 | tf_op jit(solution)/shard_map/ppermute | solution.py:272
  105.6 4.4 %shard_map.78 = (bf16[512,128]{1,0:T(8,128)(2,1)S(1)}, bf16[512,128]{1,0:T(8,128)(2,1)S(1)}, bf16[512,128]{1,0:T(8,128)(2,1)S(1)}, bf16[512,128]{1,0:T(8,128)(2,...) custom-call(s32[4]{0:T(128)S(1)} %copy-done.69, ...), custom_call_target="tpu_custom_call" | custom-call | flops 1073741824 | tf_op jit(solution)/shard_map/pallas_call | solution.py:313
  110.1 1.9 %collective-permute-start.46 = (bf16[256,128]{1,0:T(8,128)(2,1)S(1)}, bf16[256,128]{1,0:T(8,128)(2,1)S(1)}, u32[]{:S(2)}, u32[]{:S(2)}) collective-permute-start(bf16[256,128]{1,0:T(8,128)(2,1)S(1)} %get-tuple-element.173), channel_id=1, source_target_pairs={{0,8},{8,16},{16,24},{24,0},{1,9},{9,17},{17,25},{25,1},{2,10},{10... | collective-permute-start | bytes 196616 | tf_op jit(solution)/shard_map/ppermute | solution.py:272
  112.1 2.8 %collective-permute-done.44.refs_0_ = bf16[256,128]{1,0:T(8,128)(2,1)S(1)} collective-permute-done((bf16[256,128]{1,0:T(8,128)(2,1)S(1)}, bf16[256,128]{1,0:T(8,128)(2,1)S(1)}, u32[]{:S(2)}, u32[]{:S(2)}) %collective-permute-start.44) | collective-permute-done | bytes 65568 | tf_op jit(solution)/shard_map/ppermute | solution.py:272
  114.9 3.2 %collective-permute-done.45.refs_1_ = bf16[256,128]{1,0:T(8,128)(2,1)S(1)} collective-permute-done((bf16[256,128]{1,0:T(8,128)(2,1)S(1)}, bf16[256,128]{1,0:T(8,128)(2,1)S(1)}, u32[]{:S(2)}, u32[]{:S(2)}) %collective-permute-start.45) | collective-permute-done | bytes 65568 | tf_op jit(solution)/shard_map/ppermute | solution.py:272
  118.3 1.6 shard_map.79
  119.9 1.0 copy-done.10
  120.9 0.6 copy-done.13
  121.6 0.6 copy-done.15
  122.2 0.6 copy-done.17
  122.9 0.6 copy-done.19
  123.5 1.3 collective-permute-start.47
  124.9 3.5 %collective-permute-start.48 = (bf16[256,128]{1,0:T(8,128)(2,1)}, bf16[256,128]{1,0:T(8,128)(2,1)S(1)}, u32[]{:S(2)}, u32[]{:S(2)}) collective-permute-start(bf16[256,128]{1,0:T(8,128)(2,1)} %get-tuple-element.180), channel_id=1, source_target_pairs={{0,16},{8,24},{16,0},{24,8},{1,17},{9,25},{17,1},{25,9},{2,18},{10... | collective-permute-start | bytes 196616 | tf_op jit(solution)/shard_map/ppermute | solution.py:272
  128.3 2.0 %collective-permute-start.49 = (bf16[256,128]{1,0:T(8,128)(2,1)S(1)}, bf16[256,128]{1,0:T(8,128)(2,1)S(1)}, u32[]{:S(2)}, u32[]{:S(2)}) collective-permute-start(bf16[256,128]{1,0:T(8,128)(2,1)S(1)} %get-tuple-element.181), channel_id=1, source_target_pairs={{0,8},{8,16},{16,24},{24,0},{1,9},{9,17},{17,25},{25,1},{2,10},{10... | collective-permute-start | bytes 196616 | tf_op jit(solution)/shard_map/ppermute | solution.py:272
  130.3 0.7 reduce_max.9
  131.8 3.2 %collective-permute-done.48.refs_1_ = bf16[256,128]{1,0:T(8,128)(2,1)S(1)} collective-permute-done((bf16[256,128]{1,0:T(8,128)(2,1)}, bf16[256,128]{1,0:T(8,128)(2,1)S(1)}, u32[]{:S(2)}, u32[]{:S(2)}) %collective-permute-start.48) | collective-permute-done | bytes 65568 | tf_op jit(solution)/shard_map/ppermute | solution.py:272
  135.0 1.0 copy-done.1
  136.0 1.0 copy-done.3
  137.0 1.0 copy-done.5
  138.0 1.0 copy-done.7
  139.0 1.0 copy-done.9
  140.0 1.2 copy-done.11
  141.3 1.5 shard_map.82
  142.8 0.9 copy-done.14
  143.7 0.9 copy-done.16
  144.6 0.9 copy-done.18
  145.5 0.9 copy-done.20
  146.5 4.8 %shard_map.80 = (bf16[512,128]{1,0:T(8,128)(2,1)}, bf16[512,128]{1,0:T(8,128)(2,1)}, bf16[512,128]{1,0:T(8,128)(2,1)}, bf16[512,128]{1,0:T(8,128)(2,1)}) custom-call(s32[4]{0:T(128)S(1)} %copy-done.69, s32[1,4]{1,0:T(1,128)S(1)} %copy-done.70, f32[2048,128]{1,0:T(8,128)S(1)} %copy-done.11, bf16[256,128]{1,0:T(8,128)(2,1)S(1)} %collective-permute-done.47.refs_0_, ...), custom_call_target="tpu_custom_call" | custom-call | flops 1073741824 | tf_op jit(solution)/shard_map/pallas_call | solution.py:313
  151.8 2.6 %collective-permute-start.50 = (bf16[512,128]{1,0:T(8,128)(2,1)}, bf16[512,128]{1,0:T(8,128)(2,1)S(1)}, u32[]{:S(2)}, u32[]{:S(2)}) collective-permute-start(bf16[512,128]{1,0:T(8,128)(2,1)} %get-tuple-element.187), channel_id=1, source_target_pairs={{0,8},{8,16},{16,24},{24,0},{1,9},{9,17},{17,25},{25,1},{2,10},{10... | collective-permute-start | bytes 393224 | tf_op jit(solution)/shard_map/ppermute | solution.py:272
  154.3 2.4 %collective-permute-start.52 = (bf16[512,128]{1,0:T(8,128)(2,1)}, bf16[512,128]{1,0:T(8,128)(2,1)S(1)}, u32[]{:S(2)}, u32[]{:S(2)}) collective-permute-start(bf16[512,128]{1,0:T(8,128)(2,1)} %get-tuple-element.189), channel_id=1, source_target_pairs={{0,24},{8,0},{16,8},{24,16},{1,25},{9,1},{17,9},{25,17},{2,26},{10... | collective-permute-start | bytes 393224 | tf_op jit(solution)/shard_map/ppermute | solution.py:272
  156.8 3.4 %collective-permute-done.50.refs_1_ = bf16[512,128]{1,0:T(8,128)(2,1)S(1)} collective-permute-done((bf16[512,128]{1,0:T(8,128)(2,1)}, bf16[512,128]{1,0:T(8,128)(2,1)S(1)}, u32[]{:S(2)}, u32[]{:S(2)}) %collective-permute-start.50) | collective-permute-done | bytes 131104 | tf_op jit(solution)/shard_map/ppermute | solution.py:272
  160.2 3.9 %collective-permute-done.51.refs_2_ = bf16[512,128]{1,0:T(8,128)(2,1)S(1)} collective-permute-done((bf16[512,128]{1,0:T(8,128)(2,1)}, bf16[512,128]{1,0:T(8,128)(2,1)S(1)}, u32[]{:S(2)}, u32[]{:S(2)}) %collective-permute-start.51) | collective-permute-done | bytes 131104 | tf_op jit(solution)/shard_map/ppermute | solution.py:272
  164.1 1.8 %shard_map.81 = bf16[4,512,128]{2,1,0:T(8,128)(2,1)} custom-call(s32[4]{0:T(128)S(1)} %copy-done.69, s32[1,4]{1,0:T(1,128)S(1)} %copy-done.70, bf16[512,128]{1,0:T(8,128)(2,1)} %get-tuple-element.186.refs_0_, bf16[512,128]{1,0:T(8,128)(2,1)S(1)} %collective-permute-done.50.refs_1_, bf16[512,128]{1,0:T(8,128)(2,1)S(1)} %collective-permute-done.51.refs_2_, ...), custom_call_target="tpu_custom_call" | custom-call | flops 1073741824 | tf_op jit(solution)/shard_map/pallas_call | solution.py:313
  (174 shorter events, 3.6 us)
Async XLA Ops:
  0.7 82.8 %copy-start.70 = (s32[1,4]{1,0:T(1,128)S(1)}, s32[1,4]{1,0:T(1,128)}, u32[]{:S(2)}) copy-start(s32[1,4]{1,0:T(1,128)} %ranks.11) | copy-start | bytes 52
  3.1 15.2 %collective-permute-start.10 = (bf16[384,512]{1,0:T(8,128)(2,1)S(1)}, bf16[384,512]{1,0:T(8,128)(2,1)S(1)}, u32[]{:S(2)}, u32[]{:S(2)}) collective-permute-start(bf16[384,512]{1,0:T(8,128)(2,1)S(1)} %get-tuple-element.157), channel_id=1, source_target_pairs={{0,8},{8,16},{16,24},{24,0},{1,9},{9,17},{17,25},{25,1},{2,10},{10... | collective-permute-start | bytes 1179656 | tf_op jit(solution)/shard_map/ppermute | solution.py:272
  8.4 26.0 %collective-permute-start.18 = (bf16[384,512]{1,0:T(8,128)(2,1)S(1)}, bf16[384,512]{1,0:T(8,128)(2,1)S(1)}, u32[]{:S(2)}, u32[]{:S(2)}) collective-permute-start(bf16[384,512]{1,0:T(8,128)(2,1)S(1)} %get-tuple-element.158), channel_id=1, source_target_pairs={{0,16},{8,24},{16,0},{24,8},{1,17},{9,25},{17,1},{25,9},{2,18},{10... | collective-permute-start | bytes 1179656 | tf_op jit(solution)/shard_map/ppermute | solution.py:272
  11.0 24.8 %collective-permute-start.26 = (bf16[384,512]{1,0:T(8,128)(2,1)S(1)}, bf16[384,512]{1,0:T(8,128)(2,1)S(1)}, u32[]{:S(2)}, u32[]{:S(2)}) collective-permute-start(bf16[384,512]{1,0:T(8,128)(2,1)S(1)} %get-tuple-element.159), channel_id=1, source_target_pairs={{0,24},{8,0},{16,8},{24,16},{1,25},{9,1},{17,9},{25,17},{2,26},{10... | collective-permute-start | bytes 1179656 | tf_op jit(solution)/shard_map/ppermute | solution.py:272
  12.4 23.5 %collective-permute-start.37 = (bf16[3,256,256]{2,1,0:T(8,128)(2,1)S(1)}, bf16[3,256,256]{2,1,0:T(8,128)(2,1)S(1)}, u32[]{:S(2)}, u32[]{:S(2)}) collective-permute-start(bf16[3,256,256]{2,1,0:T(8,128)(2,1)S(1)} %get-tuple-element.164.refs_3_), channel_id=1, source_target_pairs={{0,1},{1,0},{2,3},{3,2},{4,5},{5,4},{6,7},{7,6},{8,9},{9,8},{10,11... | collective-permute-start | bytes 1179656 | tf_op jit(solution)/shard_map/ppermute | solution.py:59
  12.4 24.6 %collective-permute-start.38 = (bf16[3,256,256]{2,1,0:T(8,128)(2,1)S(1)}, bf16[3,256,256]{2,1,0:T(8,128)(2,1)S(1)}, u32[]{:S(2)}, u32[]{:S(2)}) collective-permute-start(bf16[3,256,256]{2,1,0:T(8,128)(2,1)S(1)} %get-tuple-element.164.refs_3_), channel_id=1, source_target_pairs={{0,2},{1,5},{2,0},{3,7},{4,6},{5,1},{6,4},{7,3},{8,10},{9,13},{10,... | collective-permute-start | bytes 1179656 | tf_op jit(solution)/shard_map/ppermute | solution.py:58
  18.3 99.7 %copy-start.21 = (bf16[384,512]{1,0:T(8,128)(2,1)}, bf16[384,512]{1,0:T(8,128)(2,1)S(1)}, u32[]{:S(2)}) copy-start(bf16[384,512]{1,0:T(8,128)(2,1)S(1)} %collective-permute-done.10.refs_1_.refs_16_) | copy-start | bytes 1179652
  18.3 19.3 %collective-permute-start.11 = (bf16[384,512]{1,0:T(8,128)(2,1)S(1)}, bf16[384,512]{1,0:T(8,128)(2,1)S(1)}, u32[]{:S(2)}, u32[]{:S(2)}) collective-permute-start(bf16[384,512]{1,0:T(8,128)(2,1)S(1)} %collective-permute-done.10.refs_1_.refs_16_), channel_id=1, source_target_pairs={{0,1},{1,0},{2,3},{3,2},{4,5},{5,4},{6,7},{7,6},{8,9},{9,8},{10,11... | collective-permute-start | bytes 1179656 | tf_op jit(solution)/shard_map/ppermute | solution.py:59
  34.3 83.7 %copy-start.23 = (bf16[384,512]{1,0:T(8,128)(2,1)}, bf16[384,512]{1,0:T(8,128)(2,1)S(1)}, u32[]{:S(2)}) copy-start(bf16[384,512]{1,0:T(8,128)(2,1)S(1)} %collective-permute-done.18.refs_9_.refs_24_) | copy-start | bytes 1179652
  34.3 7.8 %collective-permute-start.12 = (bf16[384,512]{1,0:T(8,128)(2,1)S(1)}, bf16[384,512]{1,0:T(8,128)(2,1)S(1)}, u32[]{:S(2)}, u32[]{:S(2)}) collective-permute-start(bf16[384,512]{1,0:T(8,128)(2,1)S(1)} %collective-permute-done.10.refs_1_.refs_16_), channel_id=1, source_target_pairs={{0,2},{1,5},{2,0},{3,7},{4,6},{5,1},{6,4},{7,3},{8,10},{9,13},{10,... | collective-permute-start | bytes 1179656 | tf_op jit(solution)/shard_map/ppermute | solution.py:58
  35.8 82.2 %copy-start.25 = (bf16[384,512]{1,0:T(8,128)(2,1)}, bf16[384,512]{1,0:T(8,128)(2,1)S(1)}, u32[]{:S(2)}) copy-start(bf16[384,512]{1,0:T(8,128)(2,1)S(1)} %collective-permute-done.26.refs_17_.refs_32_) | copy-start | bytes 1179652
  35.8 7.8 %collective-permute-start.19 = (bf16[384,512]{1,0:T(8,128)(2,1)S(1)}, bf16[384,512]{1,0:T(8,128)(2,1)S(1)}, u32[]{:S(2)}, u32[]{:S(2)}) collective-permute-start(bf16[384,512]{1,0:T(8,128)(2,1)S(1)} %collective-permute-done.18.refs_9_.refs_24_), channel_id=1, source_target_pairs={{0,1},{1,0},{2,3},{3,2},{4,5},{5,4},{6,7},{7,6},{8,9},{9,8},{10,11... | collective-permute-start | bytes 1179656 | tf_op jit(solution)/shard_map/ppermute | solution.py:59
  35.8 10.5 %collective-permute-start.20 = (bf16[384,512]{1,0:T(8,128)(2,1)S(1)}, bf16[384,512]{1,0:T(8,128)(2,1)S(1)}, u32[]{:S(2)}, u32[]{:S(2)}) collective-permute-start(bf16[384,512]{1,0:T(8,128)(2,1)S(1)} %collective-permute-done.18.refs_9_.refs_24_), channel_id=1, source_target_pairs={{0,2},{1,5},{2,0},{3,7},{4,6},{5,1},{6,4},{7,3},{8,10},{9,13},{10,... | collective-permute-start | bytes 1179656 | tf_op jit(solution)/shard_map/ppermute | solution.py:58
  37.0 10.8 %collective-permute-start.27 = (bf16[384,512]{1,0:T(8,128)(2,1)S(1)}, bf16[384,512]{1,0:T(8,128)(2,1)S(1)}, u32[]{:S(2)}, u32[]{:S(2)}) collective-permute-start(bf16[384,512]{1,0:T(8,128)(2,1)S(1)} %collective-permute-done.26.refs_17_.refs_32_), channel_id=1, source_target_pairs={{0,1},{1,0},{2,3},{3,2},{4,5},{5,4},{6,7},{7,6},{8,9},{9,8},{10,11... | collective-permute-start | bytes 1179656 | tf_op jit(solution)/shard_map/ppermute | solution.py:59
  37.6 80.5 %copy-start.27 = (bf16[384,512]{1,0:T(8,128)(2,1)}, bf16[384,512]{1,0:T(8,128)(2,1)S(1)}, u32[]{:S(2)}) copy-start(bf16[384,512]{1,0:T(8,128)(2,1)S(1)} %collective-permute-done.11.refs_2_.refs_17_) | copy-start | bytes 1179652
  37.6 15.5 %collective-permute-start.28 = (bf16[384,512]{1,0:T(8,128)(2,1)S(1)}, bf16[384,512]{1,0:T(8,128)(2,1)S(1)}, u32[]{:S(2)}, u32[]{:S(2)}) collective-permute-start(bf16[384,512]{1,0:T(8,128)(2,1)S(1)} %collective-permute-done.26.refs_17_.refs_32_), channel_id=1, source_target_pairs={{0,2},{1,5},{2,0},{3,7},{4,6},{5,1},{6,4},{7,3},{8,10},{9,13},{10,... | collective-permute-start | bytes 1179656 | tf_op jit(solution)/shard_map/ppermute | solution.py:58
  42.1 76.0 %copy-start.29 = (bf16[384,512]{1,0:T(8,128)(2,1)}, bf16[384,512]{1,0:T(8,128)(2,1)S(1)}, u32[]{:S(2)}) copy-start(bf16[384,512]{1,0:T(8,128)(2,1)S(1)} %collective-permute-done.12.refs_3_.refs_18_) | copy-start | bytes 1179652
  42.1 16.9 %collective-permute-start.39 = (bf16[3,256,256]{2,1,0:T(8,128)(2,1)S(1)}, bf16[3,256,256]{2,1,0:T(8,128)(2,1)S(1)}, u32[]{:S(2)}, u32[]{:S(2)}) collective-permute-start(bf16[3,256,256]{2,1,0:T(8,128)(2,1)S(1)} %collective-permute-done.37.refs_4_), channel_id=1, source_target_pairs={{0,2},{1,5},{2,0},{3,7},{4,6},{5,1},{6,4},{7,3},{8,10},{9,13},{10,... | collective-permute-start | bytes 1179656 | tf_op jit(solution)/shard_map/ppermute | solution.py:60
  43.6 74.5 %copy-start.31 = (bf16[384,512]{1,0:T(8,128)(2,1)}, bf16[384,512]{1,0:T(8,128)(2,1)S(1)}, u32[]{:S(2)}) copy-start(bf16[384,512]{1,0:T(8,128)(2,1)S(1)} %collective-permute-done.19.refs_10_.refs_25_) | copy-start | bytes 1179652
  43.6 22.5 %collective-permute-start.13 = (bf16[384,512]{1,0:T(8,128)(2,1)S(1)}, bf16[384,512]{1,0:T(8,128)(2,1)S(1)}, u32[]{:S(2)}, u32[]{:S(2)}) collective-permute-start(bf16[384,512]{1,0:T(8,128)(2,1)S(1)} %collective-permute-done.11.refs_2_.refs_17_), channel_id=1, source_target_pairs={{0,2},{1,5},{2,0},{3,7},{4,6},{5,1},{6,4},{7,3},{8,10},{9,13},{10,... | collective-permute-start | bytes 1179656 | tf_op jit(solution)/shard_map/ppermute | solution.py:60
  46.3 71.8 %copy-start.33 = (bf16[384,512]{1,0:T(8,128)(2,1)}, bf16[384,512]{1,0:T(8,128)(2,1)S(1)}, u32[]{:S(2)}) copy-start(bf16[384,512]{1,0:T(8,128)(2,1)S(1)} %collective-permute-done.20.refs_11_.refs_26_) | copy-start | bytes 1179652
  46.3 19.8 %collective-permute-start.14 = (bf16[384,512]{1,0:T(8,128)(2,1)S(1)}, bf16[384,512]{1,0:T(8,128)(2,1)S(1)}, u32[]{:S(2)}, u32[]{:S(2)}) collective-permute-start(bf16[384,512]{1,0:T(8,128)(2,1)S(1)} %collective-permute-done.12.refs_3_.refs_18_), channel_id=1, source_target_pairs={{0,4},{1,3},{2,6},{3,1},{4,0},{5,7},{6,2},{7,5},{8,12},{9,11},{10,... | collective-permute-start | bytes 1179656 | tf_op jit(solution)/shard_map/ppermute | solution.py:61
  47.8 70.3 %copy-start.35 = (bf16[384,512]{1,0:T(8,128)(2,1)}, bf16[384,512]{1,0:T(8,128)(2,1)S(1)}, u32[]{:S(2)}) copy-start(bf16[384,512]{1,0:T(8,128)(2,1)S(1)} %collective-permute-done.27.refs_18_.refs_33_) | copy-start | bytes 1179652
  47.8 19.9 %collective-permute-start.15 = (bf16[384,512]{1,0:T(8,128)(2,1)S(1)}, bf16[384,512]{1,0:T(8,128)(2,1)S(1)}, u32[]{:S(2)}, u32[]{:S(2)}) collective-permute-start(bf16[384,512]{1,0:T(8,128)(2,1)S(1)} %collective-permute-done.12.refs_3_.refs_18_), channel_id=1, source_target_pairs={{0,1},{1,0},{2,3},{3,2},{4,5},{5,4},{6,7},{7,6},{8,9},{9,8},{10,11... | collective-permute-start | bytes 1179656 | tf_op jit(solution)/shard_map/ppermute | solution.py:62
  53.1 65.0 %copy-start.37 = (bf16[384,512]{1,0:T(8,128)(2,1)}, bf16[384,512]{1,0:T(8,128)(2,1)S(1)}, u32[]{:S(2)}) copy-start(bf16[384,512]{1,0:T(8,128)(2,1)S(1)} %collective-permute-done.28.refs_19_.refs_34_) | copy-start | bytes 1179652
  53.1 19.6 %collective-permute-start.21 = (bf16[384,512]{1,0:T(8,128)(2,1)S(1)}, bf16[384,512]{1,0:T(8,128)(2,1)S(1)}, u32[]{:S(2)}, u32[]{:S(2)}) collective-permute-start(bf16[384,512]{1,0:T(8,128)(2,1)S(1)} %collective-permute-done.19.refs_10_.refs_25_), channel_id=1, source_target_pairs={{0,2},{1,5},{2,0},{3,7},{4,6},{5,1},{6,4},{7,3},{8,10},{9,13},{10,... | collective-permute-start | bytes 1179656 | tf_op jit(solution)/shard_map/ppermute | solution.py:60
  59.0 59.2 %copy-start = (bf16[3,256,256]{2,1,0:T(8,128)(2,1)}, bf16[3,256,256]{2,1,0:T(8,128)(2,1)S(1)}, u32[]{:S(2)}) copy-start(bf16[3,256,256]{2,1,0:T(8,128)(2,1)S(1)} %collective-permute-done.39.refs_6_) | copy-start | bytes 1179652
  59.0 13.8 %collective-permute-start.22 = (bf16[384,512]{1,0:T(8,128)(2,1)S(1)}, bf16[384,512]{1,0:T(8,128)(2,1)S(1)}, u32[]{:S(2)}, u32[]{:S(2)}) collective-permute-start(bf16[384,512]{1,0:T(8,128)(2,1)S(1)} %collective-permute-done.20.refs_11_.refs_26_), channel_id=1, source_target_pairs={{0,4},{1,3},{2,6},{3,1},{4,0},{5,7},{6,2},{7,5},{8,12},{9,11},{10,... | collective-permute-start | bytes 1179656 | tf_op jit(solution)/shard_map/ppermute | solution.py:61
  66.1 52.0 %copy-start.39 = (bf16[384,512]{1,0:T(8,128)(2,1)}, bf16[384,512]{1,0:T(8,128)(2,1)S(1)}, u32[]{:S(2)}) copy-start(bf16[384,512]{1,0:T(8,128)(2,1)S(1)} %collective-permute-done.13.refs_4_.refs_19_) | copy-start | bytes 1179652
  66.1 7.1 %collective-permute-start.23 = (bf16[384,512]{1,0:T(8,128)(2,1)S(1)}, bf16[384,512]{1,0:T(8,128)(2,1)S(1)}, u32[]{:S(2)}, u32[]{:S(2)}) collective-permute-start(bf16[384,512]{1,0:T(8,128)(2,1)S(1)} %collective-permute-done.20.refs_11_.refs_26_), channel_id=1, source_target_pairs={{0,1},{1,0},{2,3},{3,2},{4,5},{5,4},{6,7},{7,6},{8,9},{9,8},{10,11... | collective-permute-start | bytes 1179656 | tf_op jit(solution)/shard_map/ppermute | solution.py:62
  66.1 52.0 %copy-start.41 = (bf16[384,512]{1,0:T(8,128)(2,1)}, bf16[384,512]{1,0:T(8,128)(2,1)S(1)}, u32[]{:S(2)}) copy-start(bf16[384,512]{1,0:T(8,128)(2,1)S(1)} %collective-permute-done.14.refs_5_.refs_20_) | copy-start | bytes 1179652
  66.1 13.9 %collective-permute-start.29 = (bf16[384,512]{1,0:T(8,128)(2,1)S(1)}, bf16[384,512]{1,0:T(8,128)(2,1)S(1)}, u32[]{:S(2)}, u32[]{:S(2)}) collective-permute-start(bf16[384,512]{1,0:T(8,128)(2,1)S(1)} %collective-permute-done.27.refs_18_.refs_33_), channel_id=1, source_target_pairs={{0,2},{1,5},{2,0},{3,7},{4,6},{5,1},{6,4},{7,3},{8,10},{9,13},{10,... | collective-permute-start | bytes 1179656 | tf_op jit(solution)/shard_map/ppermute | solution.py:60
  67.7 50.5 %copy-start.43 = (bf16[384,512]{1,0:T(8,128)(2,1)}, bf16[384,512]{1,0:T(8,128)(2,1)S(1)}, u32[]{:S(2)}) copy-start(bf16[384,512]{1,0:T(8,128)(2,1)S(1)} %collective-permute-done.15.refs_6_.refs_21_) | copy-start | bytes 1179652
  67.7 12.3 %collective-permute-start.30 = (bf16[384,512]{1,0:T(8,128)(2,1)S(1)}, bf16[384,512]{1,0:T(8,128)(2,1)S(1)}, u32[]{:S(2)}, u32[]{:S(2)}) collective-permute-start(bf16[384,512]{1,0:T(8,128)(2,1)S(1)} %collective-permute-done.28.refs_19_.refs_34_), channel_id=1, source_target_pairs={{0,4},{1,3},{2,6},{3,1},{4,0},{5,7},{6,2},{7,5},{8,12},{9,11},{10,... | collective-permute-start | bytes 1179656 | tf_op jit(solution)/shard_map/ppermute | solution.py:61
  72.7 45.4 %copy-start.45 = (bf16[384,512]{1,0:T(8,128)(2,1)}, bf16[384,512]{1,0:T(8,128)(2,1)S(1)}, u32[]{:S(2)}) copy-start(bf16[384,512]{1,0:T(8,128)(2,1)S(1)} %collective-permute-done.21.refs_12_.refs_27_) | copy-start | bytes 1179652
  72.7 7.8 %collective-permute-start.31 = (bf16[384,512]{1,0:T(8,128)(2,1)S(1)}, bf16[384,512]{1,0:T(8,128)(2,1)S(1)}, u32[]{:S(2)}, u32[]{:S(2)}) collective-permute-start(bf16[384,512]{1,0:T(8,128)(2,1)S(1)} %collective-permute-done.28.refs_19_.refs_34_), channel_id=1, source_target_pairs={{0,1},{1,0},{2,3},{3,2},{4,5},{5,4},{6,7},{7,6},{8,9},{9,8},{10,11... | collective-permute-start | bytes 1179656 | tf_op jit(solution)/shard_map/ppermute | solution.py:62
  72.7 45.4 %copy-start.47 = (bf16[384,512]{1,0:T(8,128)(2,1)}, bf16[384,512]{1,0:T(8,128)(2,1)S(1)}, u32[]{:S(2)}) copy-start(bf16[384,512]{1,0:T(8,128)(2,1)S(1)} %collective-permute-done.22.refs_13_.refs_28_) | copy-start | bytes 1179652
  72.7 7.9 %collective-permute-start.16 = (bf16[384,512]{1,0:T(8,128)(2,1)S(1)}, bf16[384,512]{1,0:T(8,128)(2,1)S(1)}, u32[]{:S(2)}, u32[]{:S(2)}) collective-permute-start(bf16[384,512]{1,0:T(8,128)(2,1)S(1)} %collective-permute-done.13.refs_4_.refs_19_), channel_id=1, source_target_pairs={{0,1},{1,0},{2,3},{3,2},{4,5},{5,4},{6,7},{7,6},{8,9},{9,8},{10,11... | collective-permute-start | bytes 1179656 | tf_op jit(solution)/shard_map/ppermute | solution.py:62
  73.2 44.9 %copy-start.49 = (bf16[384,512]{1,0:T(8,128)(2,1)}, bf16[384,512]{1,0:T(8,128)(2,1)S(1)}, u32[]{:S(2)}) copy-start(bf16[384,512]{1,0:T(8,128)(2,1)S(1)} %collective-permute-done.23.refs_14_.refs_29_) | copy-start | bytes 1179652
  73.2 7.8 %collective-permute-start.17 = (bf16[384,512]{1,0:T(8,128)(2,1)S(1)}, bf16[384,512]{1,0:T(8,128)(2,1)S(1)}, u32[]{:S(2)}, u32[]{:S(2)}) collective-permute-start(bf16[384,512]{1,0:T(8,128)(2,1)S(1)} %collective-permute-done.14.refs_5_.refs_20_), channel_id=1, source_target_pairs={{0,1},{1,0},{2,3},{3,2},{4,5},{5,4},{6,7},{7,6},{8,9},{9,8},{10,11... | collective-permute-start | bytes 1179656 | tf_op jit(solution)/shard_map/ppermute | solution.py:70
  80.0 38.2 %copy-start.51 = (bf16[384,512]{1,0:T(8,128)(2,1)}, bf16[384,512]{1,0:T(8,128)(2,1)S(1)}, u32[]{:S(2)}) copy-start(bf16[384,512]{1,0:T(8,128)(2,1)S(1)} %collective-permute-done.29.refs_20_.refs_35_) | copy-start | bytes 1179652
  80.0 2.6 %collective-permute-start.24 = (bf16[384,512]{1,0:T(8,128)(2,1)S(1)}, bf16[384,512]{1,0:T(8,128)(2,1)S(1)}, u32[]{:S(2)}, u32[]{:S(2)}) collective-permute-start(bf16[384,512]{1,0:T(8,128)(2,1)S(1)} %collective-permute-done.21.refs_12_.refs_27_), channel_id=1, source_target_pairs={{0,1},{1,0},{2,3},{3,2},{4,5},{5,4},{6,7},{7,6},{8,9},{9,8},{10,11... | collective-permute-start | bytes 1179656 | tf_op jit(solution)/shard_map/ppermute | solution.py:62
  80.0 38.2 %copy-start.53 = (bf16[384,512]{1,0:T(8,128)(2,1)}, bf16[384,512]{1,0:T(8,128)(2,1)S(1)}, u32[]{:S(2)}) copy-start(bf16[384,512]{1,0:T(8,128)(2,1)S(1)} %collective-permute-done.30.refs_21_.refs_36_) | copy-start | bytes 1179652
  80.0 2.6 %collective-permute-start.25 = (bf16[384,512]{1,0:T(8,128)(2,1)S(1)}, bf16[384,512]{1,0:T(8,128)(2,1)S(1)}, u32[]{:S(2)}, u32[]{:S(2)}) collective-permute-start(bf16[384,512]{1,0:T(8,128)(2,1)S(1)} %collective-permute-done.22.refs_13_.refs_28_), channel_id=1, source_target_pairs={{0,1},{1,0},{2,3},{3,2},{4,5},{5,4},{6,7},{7,6},{8,9},{9,8},{10,11... | collective-permute-start | bytes 1179656 | tf_op jit(solution)/shard_map/ppermute | solution.py:70
  80.5 37.7 %copy-start.55 = (bf16[384,512]{1,0:T(8,128)(2,1)}, bf16[384,512]{1,0:T(8,128)(2,1)S(1)}, u32[]{:S(2)}) copy-start(bf16[384,512]{1,0:T(8,128)(2,1)S(1)} %collective-permute-done.31.refs_22_.refs_37_) | copy-start | bytes 1179652
  80.6 2.6 %collective-permute-start.32 = (bf16[384,512]{1,0:T(8,128)(2,1)S(1)}, bf16[384,512]{1,0:T(8,128)(2,1)S(1)}, u32[]{:S(2)}, u32[]{:S(2)}) collective-permute-start(bf16[384,512]{1,0:T(8,128)(2,1)S(1)} %collective-permute-done.29.refs_20_.refs_35_), channel_id=1, source_target_pairs={{0,1},{1,0},{2,3},{3,2},{4,5},{5,4},{6,7},{7,6},{8,9},{9,8},{10,11... | collective-permute-start | bytes 1179656 | tf_op jit(solution)/shard_map/ppermute | solution.py:62
  80.6 37.6 %copy-start.57 = (bf16[384,512]{1,0:T(8,128)(2,1)}, bf16[384,512]{1,0:T(8,128)(2,1)S(1)}, u32[]{:S(2)}) copy-start(bf16[384,512]{1,0:T(8,128)(2,1)S(1)} %collective-permute-done.16.refs_7_.refs_22_) | copy-start | bytes 1179652
  80.6 2.8 %collective-permute-start.33 = (bf16[384,512]{1,0:T(8,128)(2,1)S(1)}, bf16[384,512]{1,0:T(8,128)(2,1)S(1)}, u32[]{:S(2)}, u32[]{:S(2)}) collective-permute-start(bf16[384,512]{1,0:T(8,128)(2,1)S(1)} %collective-permute-done.30.refs_21_.refs_36_), channel_id=1, source_target_pairs={{0,1},{1,0},{2,3},{3,2},{4,5},{5,4},{6,7},{7,6},{8,9},{9,8},{10,11... | collective-permute-start | bytes 1179656 | tf_op jit(solution)/shard_map/ppermute | solution.py:70
  81.1 7.8 %collective-permute-start.40 = (bf16[3,256,256]{2,1,0:T(8,128)(2,1)S(1)}, bf16[3,256,256]{2,1,0:T(8,128)(2,1)S(1)}, u32[]{:S(2)}, u32[]{:S(2)}) collective-permute-start(bf16[3,256,256]{2,1,0:T(8,128)(2,1)S(1)} %collective-permute-done.38.refs_5_), channel_id=1, source_target_pairs={{0,4},{1,3},{2,6},{3,1},{4,0},{5,7},{6,2},{7,5},{8,12},{9,11},{10,... | collective-permute-start | bytes 1179656 | tf_op jit(solution)/shard_map/ppermute | solution.py:61
  82.6 16.0 %collective-permute-start.41 = (bf16[3,256,256]{2,1,0:T(8,128)(2,1)S(1)}, bf16[3,256,256]{2,1,0:T(8,128)(2,1)S(1)}, u32[]{:S(2)}, u32[]{:S(2)}) collective-permute-start(bf16[3,256,256]{2,1,0:T(8,128)(2,1)S(1)} %collective-permute-done.38.refs_5_), channel_id=1, source_target_pairs={{0,1},{1,0},{2,3},{3,2},{4,5},{5,4},{6,7},{7,6},{8,9},{9,8},{10,11... | collective-permute-start | bytes 1179656 | tf_op jit(solution)/shard_map/ppermute | solution.py:62
  82.6 16.6 %collective-permute-start.42 = (bf16[3,256,256]{2,1,0:T(8,128)(2,1)S(1)}, bf16[3,256,256]{2,1,0:T(8,128)(2,1)S(1)}, u32[]{:S(2)}, u32[]{:S(2)}) collective-permute-start(bf16[3,256,256]{2,1,0:T(8,128)(2,1)S(1)} %collective-permute-done.39.refs_6_), channel_id=1, source_target_pairs={{0,1},{1,0},{2,3},{3,2},{4,5},{5,4},{6,7},{7,6},{8,9},{9,8},{10,11... | collective-permute-start | bytes 1179656 | tf_op jit(solution)/shard_map/ppermute | solution.py:62
  88.9 16.8 %collective-permute-start.43 = (bf16[3,256,256]{2,1,0:T(8,128)(2,1)S(1)}, bf16[3,256,256]{2,1,0:T(8,128)(2,1)S(1)}, u32[]{:S(2)}, u32[]{:S(2)}) collective-permute-start(bf16[3,256,256]{2,1,0:T(8,128)(2,1)S(1)} %collective-permute-done.40.refs_7_), channel_id=1, source_target_pairs={{0,1},{1,0},{2,3},{3,2},{4,5},{5,4},{6,7},{7,6},{8,9},{9,8},{10,11... | collective-permute-start | bytes 1179656 | tf_op jit(solution)/shard_map/ppermute | solution.py:70
  88.9 12.3 %collective-permute-start.34 = (bf16[256,128]{1,0:T(8,128)(2,1)S(1)}, bf16[256,128]{1,0:T(8,128)(2,1)S(1)}, u32[]{:S(2)}, u32[]{:S(2)}) collective-permute-start(bf16[256,128]{1,0:T(8,128)(2,1)S(1)} %get-tuple-element.161), channel_id=1, source_target_pairs={{0,24},{8,0},{16,8},{24,16},{1,25},{9,1},{17,9},{25,17},{2,26},{10... | collective-permute-start | bytes 196616 | tf_op jit(solution)/shard_map/ppermute | solution.py:272
  98.6 7.0 %collective-permute-start.35 = (bf16[256,128]{1,0:T(8,128)(2,1)S(1)}, bf16[256,128]{1,0:T(8,128)(2,1)S(1)}, u32[]{:S(2)}, u32[]{:S(2)}) collective-permute-start(bf16[256,128]{1,0:T(8,128)(2,1)S(1)} %get-tuple-element.162), channel_id=1, source_target_pairs={{0,16},{8,24},{16,0},{24,8},{1,17},{9,25},{17,1},{25,9},{2,18},{10... | collective-permute-start | bytes 196616 | tf_op jit(solution)/shard_map/ppermute | solution.py:272
  98.6 7.0 %collective-permute-start.36 = (bf16[256,128]{1,0:T(8,128)(2,1)S(1)}, bf16[256,128]{1,0:T(8,128)(2,1)S(1)}, u32[]{:S(2)}, u32[]{:S(2)}) collective-permute-start(bf16[256,128]{1,0:T(8,128)(2,1)S(1)} %get-tuple-element.163), channel_id=1, source_target_pairs={{0,8},{8,16},{16,24},{24,0},{1,9},{9,17},{17,25},{25,1},{2,10},{10... | collective-permute-start | bytes 196616 | tf_op jit(solution)/shard_map/ppermute | solution.py:272
  110.0 4.9 %collective-permute-start.44 = (bf16[256,128]{1,0:T(8,128)(2,1)S(1)}, bf16[256,128]{1,0:T(8,128)(2,1)S(1)}, u32[]{:S(2)}, u32[]{:S(2)}) collective-permute-start(bf16[256,128]{1,0:T(8,128)(2,1)S(1)} %get-tuple-element.171), channel_id=1, source_target_pairs={{0,24},{8,0},{16,8},{24,16},{1,25},{9,1},{17,9},{25,17},{2,26},{10... | collective-permute-start | bytes 196616 | tf_op jit(solution)/shard_map/ppermute | solution.py:272
  110.1 8.0 %collective-permute-start.45 = (bf16[256,128]{1,0:T(8,128)(2,1)S(1)}, bf16[256,128]{1,0:T(8,128)(2,1)S(1)}, u32[]{:S(2)}, u32[]{:S(2)}) collective-permute-start(bf16[256,128]{1,0:T(8,128)(2,1)S(1)} %get-tuple-element.172), channel_id=1, source_target_pairs={{0,16},{8,24},{16,0},{24,8},{1,17},{9,25},{17,1},{25,9},{2,18},{10... | collective-permute-start | bytes 196616 | tf_op jit(solution)/shard_map/ppermute | solution.py:272
  110.1 7.9 %collective-permute-start.46 = (bf16[256,128]{1,0:T(8,128)(2,1)S(1)}, bf16[256,128]{1,0:T(8,128)(2,1)S(1)}, u32[]{:S(2)}, u32[]{:S(2)}) collective-permute-start(bf16[256,128]{1,0:T(8,128)(2,1)S(1)} %get-tuple-element.173), channel_id=1, source_target_pairs={{0,8},{8,16},{16,24},{24,0},{1,9},{9,17},{17,25},{25,1},{2,10},{10... | collective-permute-start | bytes 196616 | tf_op jit(solution)/shard_map/ppermute | solution.py:272
  123.5 8.2 %collective-permute-start.47 = (bf16[256,128]{1,0:T(8,128)(2,1)}, bf16[256,128]{1,0:T(8,128)(2,1)S(1)}, u32[]{:S(2)}, u32[]{:S(2)}) collective-permute-start(bf16[256,128]{1,0:T(8,128)(2,1)} %get-tuple-element.179), channel_id=1, source_target_pairs={{0,24},{8,0},{16,8},{24,16},{1,25},{9,1},{17,9},{25,17},{2,26},{10... | collective-permute-start | bytes 196616 | tf_op jit(solution)/shard_map/ppermute | solution.py:272
  124.9 10.1 %collective-permute-start.48 = (bf16[256,128]{1,0:T(8,128)(2,1)}, bf16[256,128]{1,0:T(8,128)(2,1)S(1)}, u32[]{:S(2)}, u32[]{:S(2)}) collective-permute-start(bf16[256,128]{1,0:T(8,128)(2,1)} %get-tuple-element.180), channel_id=1, source_target_pairs={{0,16},{8,24},{16,0},{24,8},{1,17},{9,25},{17,1},{25,9},{2,18},{10... | collective-permute-start | bytes 196616 | tf_op jit(solution)/shard_map/ppermute | solution.py:272
  128.3 6.7 %collective-permute-start.49 = (bf16[256,128]{1,0:T(8,128)(2,1)S(1)}, bf16[256,128]{1,0:T(8,128)(2,1)S(1)}, u32[]{:S(2)}, u32[]{:S(2)}) collective-permute-start(bf16[256,128]{1,0:T(8,128)(2,1)S(1)} %get-tuple-element.181), channel_id=1, source_target_pairs={{0,8},{8,16},{16,24},{24,0},{1,9},{9,17},{17,25},{25,1},{2,10},{10... | collective-permute-start | bytes 196616 | tf_op jit(solution)/shard_map/ppermute | solution.py:272
  151.8 8.4 %collective-permute-start.50 = (bf16[512,128]{1,0:T(8,128)(2,1)}, bf16[512,128]{1,0:T(8,128)(2,1)S(1)}, u32[]{:S(2)}, u32[]{:S(2)}) collective-permute-start(bf16[512,128]{1,0:T(8,128)(2,1)} %get-tuple-element.187), channel_id=1, source_target_pairs={{0,8},{8,16},{16,24},{24,0},{1,9},{9,17},{17,25},{25,1},{2,10},{10... | collective-permute-start | bytes 393224 | tf_op jit(solution)/shard_map/ppermute | solution.py:272
  154.3 9.7 %collective-permute-start.51 = (bf16[512,128]{1,0:T(8,128)(2,1)}, bf16[512,128]{1,0:T(8,128)(2,1)S(1)}, u32[]{:S(2)}, u32[]{:S(2)}) collective-permute-start(bf16[512,128]{1,0:T(8,128)(2,1)} %get-tuple-element.188), channel_id=1, source_target_pairs={{0,16},{8,24},{16,0},{24,8},{1,17},{9,25},{17,1},{25,9},{2,18},{10... | collective-permute-start | bytes 393224 | tf_op jit(solution)/shard_map/ppermute | solution.py:272
  154.3 9.7 %collective-permute-start.52 = (bf16[512,128]{1,0:T(8,128)(2,1)}, bf16[512,128]{1,0:T(8,128)(2,1)S(1)}, u32[]{:S(2)}, u32[]{:S(2)}) collective-permute-start(bf16[512,128]{1,0:T(8,128)(2,1)} %get-tuple-element.189), channel_id=1, source_target_pairs={{0,24},{8,0},{16,8},{24,16},{1,25},{9,1},{17,9},{25,17},{2,26},{10... | collective-permute-start | bytes 393224 | tf_op jit(solution)/shard_map/ppermute | solution.py:272
  (50 other events, 468.1 us)

commit v3 on v2

--- a/solution.py
+++ b/solution.py
@@ -124,7 +124,7 @@
         copy.wait()
 
 
-def apply_update(column, n_rows, owner, ranks, residual, coeff_refs, u_refs, coeff, slot):
+def apply_update(column, n_rows, owner, ranks, start, residual, coeff_refs, u_refs, coeff, slot):
     me, lane = position()
     holder = sum(jnp.where(owner[s] == column, s, 0) for s in range(n_rows))
     shift = around(holder - me, n_rows)
@@ -142,7 +142,11 @@
         for n, u_ref in enumerate(u_refs):
             at = pl.ds(first_row(n, lane, u_ref.shape[1]), u_ref.shape[1])
             update = jnp.dot(u_ref[slot], coeff[...], preferred_element_type=F32)
-            residual[at, :] = residual[at, :] - update
+            residual[at, :] = start[at, :] - update
+
+    @pl.when(column >= owner[me])
+    def _():
+        residual[...] = start[...]
 
 
 def write_coefficients(n_rows, solved, packed_refs, out_coeffs):
@@ -173,9 +177,10 @@
     solved, products, coeff = refs
     me, lane = position()
     mine = owner[me]
-    residual[...] = start[...].astype(F32)
-    if column:
-        apply_update(column - 1, n_rows, owner, ranks, residual, coeff_refs, u_refs, coeff, column - 1)
+    if not column:
+        residual[...] = start[...].astype(F32)
+    else:
+        apply_update(column - 1, n_rows, owner, ranks, start, residual, coeff_refs, u_refs, coeff, column - 1)
 
         @pl.when(mine < column)
         def _():
@@ -238,8 +243,7 @@
 def last_kernel(column, slot, n_rows, owner, ranks, start, *refs):
     coeff_refs, u_refs = refs[: n_rows - 1], refs[n_rows - 1 : n_rows + 7]
     residual, updated, coeff = refs[n_rows + 7 :]
-    residual[...] = start[...]
-    apply_update(column, n_rows, owner, ranks, residual, coeff_refs, u_refs, coeff, slot)
+    apply_update(column, n_rows, owner, ranks, start, residual, coeff_refs, u_refs, coeff, slot)
     updated[...] = residual[...].astype(BF16)
 
 

time: 167 us -> 167 us (level)
  no operation moved by 1% of the time
where the time goes in v3:
time: 167 us; the launch traced here: 166 us
  waiting for transfers between devices  80.1 us (48%)
  starting transfers between devices  49.7 us (30%)
  Pallas kernels  19.3 us (12%)
  local copies, waits for them, and re-layouts  13.8 us (8%)
  between operations  2.07 us (1%)
    ppermute x15, waiting for transfers between devices, shifted(): lax.ppermute(array, 'rows', [(i, (i + delta) % n_rows) for i in range(n_r...  43.3 us
    ppermute x15, starting transfers between devices, shifted(): lax.ppermute(array, 'rows', [(i, (i + delta) % n_rows) for i in range(n_r...  31.2 us
    ppermute x4, waiting for transfers between devices, gather_lanes(): near_partner = lax.ppermute(partner, 'rhs', across)  20.2 us
    pallas_call x6, Pallas kernels, call(): pl.pallas_call(kernel, out_shape=out_shape, in_specs=[SMEM, SMEM] + in_sp...  14.7 us
    unnamed x142, local copies, waits for them, and re-layouts  13.8 us
    ppermute x4, waiting for transfers between devices, gather_lanes(): near = lax.ppermute(block, 'rhs', across)  11.4 us
    ppermute x4, starting transfers between devices, gather_lanes(): far = lax.ppermute(near, 'rhs', onward)  6.08 us
    ppermute x4, starting transfers between devices, gather_lanes(): near_partner = lax.ppermute(partner, 'rhs', across)  5.07 us
  transfers between devices with their start and end apart: 43, of which 18 were waited for; matrix products, arithmetic and copies ran while one was open for 0% of the time, Pallas kernels for 2%

profile of v3, /device:TPU:0, one launch (start us, length us, event | category | flops | bytes accessed | tf_op | source)
XLA Modules:
  0.0 165.7 jit_solution(3540035632705465507)
XLA Ops:
  0.7 2.4 %pack.1 = (bf16[384,512]{1,0:T(8,128)(2,1)S(1)}, bf16[384,512]{1,0:T(8,128)(2,1)S(1)}, bf16[384,512]{1,0:T(8,128)(2,1)S(1)}, bf16[3,256,256]{2,1,0:T(8,128)(2,1)S(1)}) custom-call(s32[4]{0:T(128)} %owner.15, bf16[4,512,2048]{2,1,0:T(8,128)(2,1)} %diag.3, bf16[1,4,256,256]{3,2,1,0:T(8,128)(2,1)} %left_v.1, bf16[1,4,256,256]{3,2,1,0:T(8,128)(2,1)} %left_u.1), custom_call_target="tpu_custom_call" | custom-call | tf_op jit(solution)/shard_map/pack/pallas_call | solution.py:283
  3.1 3.1 %collective-permute-start.10 = (bf16[384,512]{1,0:T(8,128)(2,1)S(1)}, bf16[384,512]{1,0:T(8,128)(2,1)S(1)}, u32[]{:S(2)}, u32[]{:S(2)}) collective-permute-start(bf16[384,512]{1,0:T(8,128)(2,1)S(1)} %get-tuple-element.157), channel_id=1, source_target_pairs={{0,8},{8,16},{16,24},{24,0},{1,9},{9,17},{17,25},{25,1},{2,10},{10... | collective-permute-start | bytes 1179656 | tf_op jit(solution)/shard_map/ppermute | solution.py:276
  6.2 2.2 %keep.1 = (bf16[512,2048]{1,0:T(8,128)(2,1)S(1)}, bf16[2048,128]{1,0:T(8,128)(2,1)S(1)}) custom-call(s32[4]{0:T(128)S(1)} %copy-done.69, bf16[4,512,2048]{2,1,0:T(8,128)(2,1)} %diag.3, bf16[1,2048,128]{2,1,0:T(8,128)(2,1)S(1)} %copy-done.12), custom_call_target="tpu_custom_call" | custom-call | tf_op jit(solution)/shard_map/keep/pallas_call | solution.py:295
  8.4 2.7 %collective-permute-start.18 = (bf16[384,512]{1,0:T(8,128)(2,1)S(1)}, bf16[384,512]{1,0:T(8,128)(2,1)S(1)}, u32[]{:S(2)}, u32[]{:S(2)}) collective-permute-start(bf16[384,512]{1,0:T(8,128)(2,1)S(1)} %get-tuple-element.158), channel_id=1, source_target_pairs={{0,16},{8,24},{16,0},{24,8},{1,17},{9,25},{17,1},{25,9},{2,18},{10... | collective-permute-start | bytes 1179656 | tf_op jit(solution)/shard_map/ppermute | solution.py:276
  11.0 1.3 collective-permute-start.26
  12.4 1.5 collective-permute-start.38
  13.9 4.5 %collective-permute-done.10.refs_1_.refs_16_ = bf16[384,512]{1,0:T(8,128)(2,1)S(1)} collective-permute-done((bf16[384,512]{1,0:T(8,128)(2,1)S(1)}, bf16[384,512]{1,0:T(8,128)(2,1)S(1)}, u32[]{:S(2)}, u32[]{:S(2)}) %collective-permute-start.10) | collective-permute-done | bytes 393248 | tf_op jit(solution)/shard_map/ppermute | solution.py:276
  18.3 16.0 %collective-permute-done.18.refs_9_.refs_24_ = bf16[384,512]{1,0:T(8,128)(2,1)S(1)} collective-permute-done((bf16[384,512]{1,0:T(8,128)(2,1)S(1)}, bf16[384,512]{1,0:T(8,128)(2,1)S(1)}, u32[]{:S(2)}, u32[]{:S(2)}) %collective-permute-start.18) | collective-permute-done | bytes 393248 | tf_op jit(solution)/shard_map/ppermute | solution.py:276
  34.3 1.5 collective-permute-start.12
  35.8 1.2 collective-permute-start.20
  37.0 0.6 collective-permute-start.27
  37.6 0.5 collective-permute-start.28
  38.1 4.0 %collective-permute-done.12.refs_3_.refs_18_ = bf16[384,512]{1,0:T(8,128)(2,1)S(1)} collective-permute-done((bf16[384,512]{1,0:T(8,128)(2,1)S(1)}, bf16[384,512]{1,0:T(8,128)(2,1)S(1)}, u32[]{:S(2)}, u32[]{:S(2)}) %collective-permute-start.12) | collective-permute-done | bytes 393248 | tf_op jit(solution)/shard_map/ppermute | solution.py:58
  42.1 1.5 collective-permute-start.39
  44.1 2.2 %collective-permute-done.20.refs_11_.refs_26_ = bf16[384,512]{1,0:T(8,128)(2,1)S(1)} collective-permute-done((bf16[384,512]{1,0:T(8,128)(2,1)S(1)}, bf16[384,512]{1,0:T(8,128)(2,1)S(1)}, u32[]{:S(2)}, u32[]{:S(2)}) %collective-permute-start.20) | collective-permute-done | bytes 393248 | tf_op jit(solution)/shard_map/ppermute | solution.py:58
  46.3 1.5 collective-permute-start.14
  47.9 5.2 %collective-permute-done.28.refs_19_.refs_34_ = bf16[384,512]{1,0:T(8,128)(2,1)S(1)} collective-permute-done((bf16[384,512]{1,0:T(8,128)(2,1)S(1)}, bf16[384,512]{1,0:T(8,128)(2,1)S(1)}, u32[]{:S(2)}, u32[]{:S(2)}) %collective-permute-start.28) | collective-permute-done | bytes 393248 | tf_op jit(solution)/shard_map/ppermute | solution.py:58
  53.1 1.5 collective-permute-start.21
  54.6 4.4 %collective-permute-done.39.refs_6_ = bf16[3,256,256]{2,1,0:T(8,128)(2,1)S(1)} collective-permute-done((bf16[3,256,256]{2,1,0:T(8,128)(2,1)S(1)}, bf16[3,256,256]{2,1,0:T(8,128)(2,1)S(1)}, u32[]{:S(2)}, u32[]{:S(2)}) %collective-permute-start.39) | collective-permute-done | bytes 393248 | tf_op jit(solution)/shard_map/ppermute | solution.py:60
  59.0 1.5 collective-permute-start.22
  60.5 5.6 %collective-permute-done.13.refs_4_.refs_19_ = bf16[384,512]{1,0:T(8,128)(2,1)S(1)} collective-permute-done((bf16[384,512]{1,0:T(8,128)(2,1)S(1)}, bf16[384,512]{1,0:T(8,128)(2,1)S(1)}, u32[]{:S(2)}, u32[]{:S(2)}) %collective-permute-start.13) | collective-permute-done | bytes 393248 | tf_op jit(solution)/shard_map/ppermute | solution.py:60
  66.1 1.6 collective-permute-start.29
  67.7 1.5 collective-permute-start.30
  69.2 3.5 %collective-permute-done.21.refs_12_.refs_27_ = bf16[384,512]{1,0:T(8,128)(2,1)S(1)} collective-permute-done((bf16[384,512]{1,0:T(8,128)(2,1)S(1)}, bf16[384,512]{1,0:T(8,128)(2,1)S(1)}, u32[]{:S(2)}, u32[]{:S(2)}) %collective-permute-start.21) | collective-permute-done | bytes 393248 | tf_op jit(solution)/shard_map/ppermute | solution.py:60
  73.3 6.7 %collective-permute-done.29.refs_20_.refs_35_ = bf16[384,512]{1,0:T(8,128)(2,1)S(1)} collective-permute-done((bf16[384,512]{1,0:T(8,128)(2,1)S(1)}, bf16[384,512]{1,0:T(8,128)(2,1)S(1)}, u32[]{:S(2)}, u32[]{:S(2)}) %collective-permute-start.29) | collective-permute-done | bytes 393248 | tf_op jit(solution)/shard_map/ppermute | solution.py:60
  81.1 1.5 collective-permute-start.40
  83.4 0.6 shard_map.77
  84.1 4.8 %collective-permute-done.40.refs_7_ = bf16[3,256,256]{2,1,0:T(8,128)(2,1)S(1)} collective-permute-done((bf16[3,256,256]{2,1,0:T(8,128)(2,1)S(1)}, bf16[3,256,256]{2,1,0:T(8,128)(2,1)S(1)}, u32[]{:S(2)}, u32[]{:S(2)}) %collective-permute-start.40) | collective-permute-done | bytes 393248 | tf_op jit(solution)/shard_map/ppermute | solution.py:61
  88.9 9.8 %collective-permute-start.34 = (bf16[256,128]{1,0:T(8,128)(2,1)S(1)}, bf16[256,128]{1,0:T(8,128)(2,1)S(1)}, u32[]{:S(2)}, u32[]{:S(2)}) collective-permute-start(bf16[256,128]{1,0:T(8,128)(2,1)S(1)} %get-tuple-element.161), channel_id=1, source_target_pairs={{0,24},{8,0},{16,8},{24,16},{1,25},{9,1},{17,9},{25,17},{2,26},{10... | collective-permute-start | bytes 196616 | tf_op jit(solution)/shard_map/ppermute | solution.py:276
  98.6 0.6 collective-permute-start.36
  99.3 1.9 %collective-permute-done.34.refs_0_ = bf16[256,128]{1,0:T(8,128)(2,1)S(1)} collective-permute-done((bf16[256,128]{1,0:T(8,128)(2,1)S(1)}, bf16[256,128]{1,0:T(8,128)(2,1)S(1)}, u32[]{:S(2)}, u32[]{:S(2)}) %collective-permute-start.34) | collective-permute-done | bytes 65568 | tf_op jit(solution)/shard_map/ppermute | solution.py:276
  101.2 4.4 %collective-permute-done.35.refs_1_ = bf16[256,128]{1,0:T(8,128)(2,1)S(1)} collective-permute-done((bf16[256,128]{1,0:T(8,128)(2,1)S(1)}, bf16[256,128]{1,0:T(8,128)(2,1)S(1)}, u32[]{:S(2)}, u32[]{:S(2)}) %collective-permute-start.35) | collective-permute-done | bytes 65568 | tf_op jit(solution)/shard_map/ppermute | solution.py:276
  105.6 4.3 %shard_map.78 = (bf16[512,128]{1,0:T(8,128)(2,1)S(1)}, bf16[512,128]{1,0:T(8,128)(2,1)S(1)}, bf16[512,128]{1,0:T(8,128)(2,1)S(1)}, bf16[512,128]{1,0:T(8,128)(2,...) custom-call(s32[4]{0:T(128)S(1)} %copy-done.69, ...), custom_call_target="tpu_custom_call" | custom-call | flops 1073741824 | tf_op jit(solution)/shard_map/pallas_call | solution.py:317
  110.1 1.9 %collective-permute-start.46 = (bf16[256,128]{1,0:T(8,128)(2,1)S(1)}, bf16[256,128]{1,0:T(8,128)(2,1)S(1)}, u32[]{:S(2)}, u32[]{:S(2)}) collective-permute-start(bf16[256,128]{1,0:T(8,128)(2,1)S(1)} %get-tuple-element.173), channel_id=1, source_target_pairs={{0,8},{8,16},{16,24},{24,0},{1,9},{9,17},{17,25},{25,1},{2,10},{10... | collective-permute-start | bytes 196616 | tf_op jit(solution)/shard_map/ppermute | solution.py:276
  112.0 2.8 %collective-permute-done.44.refs_0_ = bf16[256,128]{1,0:T(8,128)(2,1)S(1)} collective-permute-done((bf16[256,128]{1,0:T(8,128)(2,1)S(1)}, bf16[256,128]{1,0:T(8,128)(2,1)S(1)}, u32[]{:S(2)}, u32[]{:S(2)}) %collective-permute-start.44) | collective-permute-done | bytes 65568 | tf_op jit(solution)/shard_map/ppermute | solution.py:276
  114.8 3.2 %collective-permute-done.45.refs_1_ = bf16[256,128]{1,0:T(8,128)(2,1)S(1)} collective-permute-done((bf16[256,128]{1,0:T(8,128)(2,1)S(1)}, bf16[256,128]{1,0:T(8,128)(2,1)S(1)}, u32[]{:S(2)}, u32[]{:S(2)}) %collective-permute-start.45) | collective-permute-done | bytes 65568 | tf_op jit(solution)/shard_map/ppermute | solution.py:276
  118.2 1.7 shard_map.79
  119.9 1.0 copy-done.10
  120.9 0.6 copy-done.13
  121.6 0.6 copy-done.15
  122.2 0.6 copy-done.17
  122.9 0.6 copy-done.19
  123.5 1.3 collective-permute-start.47
  124.8 3.4 %collective-permute-start.48 = (bf16[256,128]{1,0:T(8,128)(2,1)}, bf16[256,128]{1,0:T(8,128)(2,1)S(1)}, u32[]{:S(2)}, u32[]{:S(2)}) collective-permute-start(bf16[256,128]{1,0:T(8,128)(2,1)} %get-tuple-element.180), channel_id=1, source_target_pairs={{0,16},{8,24},{16,0},{24,8},{1,17},{9,25},{17,1},{25,9},{2,18},{10... | collective-permute-start | bytes 196616 | tf_op jit(solution)/shard_map/ppermute | solution.py:276
  128.2 2.0 %collective-permute-start.49 = (bf16[256,128]{1,0:T(8,128)(2,1)S(1)}, bf16[256,128]{1,0:T(8,128)(2,1)S(1)}, u32[]{:S(2)}, u32[]{:S(2)}) collective-permute-start(bf16[256,128]{1,0:T(8,128)(2,1)S(1)} %get-tuple-element.181), channel_id=1, source_target_pairs={{0,8},{8,16},{16,24},{24,0},{1,9},{9,17},{17,25},{25,1},{2,10},{10... | collective-permute-start | bytes 196616 | tf_op jit(solution)/shard_map/ppermute | solution.py:276
  130.3 0.7 reduce_max.9
  131.7 3.2 %collective-permute-done.48.refs_1_ = bf16[256,128]{1,0:T(8,128)(2,1)S(1)} collective-permute-done((bf16[256,128]{1,0:T(8,128)(2,1)}, bf16[256,128]{1,0:T(8,128)(2,1)S(1)}, u32[]{:S(2)}, u32[]{:S(2)}) %collective-permute-start.48) | collective-permute-done | bytes 65568 | tf_op jit(solution)/shard_map/ppermute | solution.py:276
  134.9 1.0 copy-done.1
  135.9 1.0 copy-done.3
  136.9 1.0 copy-done.5
  137.9 1.0 copy-done.7
  138.9 1.0 copy-done.9
  139.9 1.2 copy-done.11
  141.2 1.5 shard_map.82
  142.7 0.9 copy-done.14
  143.6 0.9 copy-done.16
  144.5 0.9 copy-done.18
  145.4 0.9 copy-done.20
  146.4 4.9 %shard_map.80 = (bf16[512,128]{1,0:T(8,128)(2,1)}, bf16[512,128]{1,0:T(8,128)(2,1)}, bf16[512,128]{1,0:T(8,128)(2,1)}, bf16[512,128]{1,0:T(8,128)(2,1)}) custom-call(s32[4]{0:T(128)S(1)} %copy-done.69, s32[1,4]{1,0:T(1,128)S(1)} %copy-done.70, f32[2048,128]{1,0:T(8,128)S(1)} %copy-done.11, bf16[256,128]{1,0:T(8,128)(2,1)S(1)} %collective-permute-done.47.refs_0_, ...), custom_call_target="tpu_custom_call" | custom-call | flops 1073741824 | tf_op jit(solution)/shard_map/pallas_call | solution.py:317
  151.7 2.5 %collective-permute-start.50 = (bf16[512,128]{1,0:T(8,128)(2,1)}, bf16[512,128]{1,0:T(8,128)(2,1)S(1)}, u32[]{:S(2)}, u32[]{:S(2)}) collective-permute-start(bf16[512,128]{1,0:T(8,128)(2,1)} %get-tuple-element.187), channel_id=1, source_target_pairs={{0,8},{8,16},{16,24},{24,0},{1,9},{9,17},{17,25},{25,1},{2,10},{10... | collective-permute-start | bytes 393224 | tf_op jit(solution)/shard_map/ppermute | solution.py:276
  154.2 2.4 %collective-permute-start.52 = (bf16[512,128]{1,0:T(8,128)(2,1)}, bf16[512,128]{1,0:T(8,128)(2,1)S(1)}, u32[]{:S(2)}, u32[]{:S(2)}) collective-permute-start(bf16[512,128]{1,0:T(8,128)(2,1)} %get-tuple-element.189), channel_id=1, source_target_pairs={{0,24},{8,0},{16,8},{24,16},{1,25},{9,1},{17,9},{25,17},{2,26},{10... | collective-permute-start | bytes 393224 | tf_op jit(solution)/shard_map/ppermute | solution.py:276
  156.6 3.5 %collective-permute-done.50.refs_1_ = bf16[512,128]{1,0:T(8,128)(2,1)S(1)} collective-permute-done((bf16[512,128]{1,0:T(8,128)(2,1)}, bf16[512,128]{1,0:T(8,128)(2,1)S(1)}, u32[]{:S(2)}, u32[]{:S(2)}) %collective-permute-start.50) | collective-permute-done | bytes 131104 | tf_op jit(solution)/shard_map/ppermute | solution.py:276
  160.1 3.8 %collective-permute-done.51.refs_2_ = bf16[512,128]{1,0:T(8,128)(2,1)S(1)} collective-permute-done((bf16[512,128]{1,0:T(8,128)(2,1)}, bf16[512,128]{1,0:T(8,128)(2,1)S(1)}, u32[]{:S(2)}, u32[]{:S(2)}) %collective-permute-start.51) | collective-permute-done | bytes 131104 | tf_op jit(solution)/shard_map/ppermute | solution.py:276
  163.9 1.8 %shard_map.81 = bf16[4,512,128]{2,1,0:T(8,128)(2,1)} custom-call(s32[4]{0:T(128)S(1)} %copy-done.69, s32[1,4]{1,0:T(1,128)S(1)} %copy-done.70, bf16[512,128]{1,0:T(8,128)(2,1)} %get-tuple-element.186.refs_0_, bf16[512,128]{1,0:T(8,128)(2,1)S(1)} %collective-permute-done.50.refs_1_, bf16[512,128]{1,0:T(8,128)(2,1)S(1)} %collective-permute-done.51.refs_2_, ...), custom_call_target="tpu_custom_call" | custom-call | flops 1073741824 | tf_op jit(solution)/shard_map/pallas_call | solution.py:317
  (174 shorter events, 3.6 us)
Async XLA Ops:
  0.7 82.8 %copy-start.70 = (s32[1,4]{1,0:T(1,128)S(1)}, s32[1,4]{1,0:T(1,128)}, u32[]{:S(2)}) copy-start(s32[1,4]{1,0:T(1,128)} %ranks.11) | copy-start | bytes 52
  3.1 15.2 %collective-permute-start.10 = (bf16[384,512]{1,0:T(8,128)(2,1)S(1)}, bf16[384,512]{1,0:T(8,128)(2,1)S(1)}, u32[]{:S(2)}, u32[]{:S(2)}) collective-permute-start(bf16[384,512]{1,0:T(8,128)(2,1)S(1)} %get-tuple-element.157), channel_id=1, source_target_pairs={{0,8},{8,16},{16,24},{24,0},{1,9},{9,17},{17,25},{25,1},{2,10},{10... | collective-permute-start | bytes 1179656 | tf_op jit(solution)/shard_map/ppermute | solution.py:276
  8.4 26.0 %collective-permute-start.18 = (bf16[384,512]{1,0:T(8,128)(2,1)S(1)}, bf16[384,512]{1,0:T(8,128)(2,1)S(1)}, u32[]{:S(2)}, u32[]{:S(2)}) collective-permute-start(bf16[384,512]{1,0:T(8,128)(2,1)S(1)} %get-tuple-element.158), channel_id=1, source_target_pairs={{0,16},{8,24},{16,0},{24,8},{1,17},{9,25},{17,1},{25,9},{2,18},{10... | collective-permute-start | bytes 1179656 | tf_op jit(solution)/shard_map/ppermute | solution.py:276
  11.0 24.8 %collective-permute-start.26 = (bf16[384,512]{1,0:T(8,128)(2,1)S(1)}, bf16[384,512]{1,0:T(8,128)(2,1)S(1)}, u32[]{:S(2)}, u32[]{:S(2)}) collective-permute-start(bf16[384,512]{1,0:T(8,128)(2,1)S(1)} %get-tuple-element.159), channel_id=1, source_target_pairs={{0,24},{8,0},{16,8},{24,16},{1,25},{9,1},{17,9},{25,17},{2,26},{10... | collective-permute-start | bytes 1179656 | tf_op jit(solution)/shard_map/ppermute | solution.py:276
  12.4 23.5 %collective-permute-start.37 = (bf16[3,256,256]{2,1,0:T(8,128)(2,1)S(1)}, bf16[3,256,256]{2,1,0:T(8,128)(2,1)S(1)}, u32[]{:S(2)}, u32[]{:S(2)}) collective-permute-start(bf16[3,256,256]{2,1,0:T(8,128)(2,1)S(1)} %get-tuple-element.164.refs_3_), channel_id=1, source_target_pairs={{0,1},{1,0},{2,3},{3,2},{4,5},{5,4},{6,7},{7,6},{8,9},{9,8},{10,11... | collective-permute-start | bytes 1179656 | tf_op jit(solution)/shard_map/ppermute | solution.py:59
  12.4 24.6 %collective-permute-start.38 = (bf16[3,256,256]{2,1,0:T(8,128)(2,1)S(1)}, bf16[3,256,256]{2,1,0:T(8,128)(2,1)S(1)}, u32[]{:S(2)}, u32[]{:S(2)}) collective-permute-start(bf16[3,256,256]{2,1,0:T(8,128)(2,1)S(1)} %get-tuple-element.164.refs_3_), channel_id=1, source_target_pairs={{0,2},{1,5},{2,0},{3,7},{4,6},{5,1},{6,4},{7,3},{8,10},{9,13},{10,... | collective-permute-start | bytes 1179656 | tf_op jit(solution)/shard_map/ppermute | solution.py:58
  18.3 99.7 %copy-start.21 = (bf16[384,512]{1,0:T(8,128)(2,1)}, bf16[384,512]{1,0:T(8,128)(2,1)S(1)}, u32[]{:S(2)}) copy-start(bf16[384,512]{1,0:T(8,128)(2,1)S(1)} %collective-permute-done.10.refs_1_.refs_16_) | copy-start | bytes 1179652
  18.3 19.3 %collective-permute-start.11 = (bf16[384,512]{1,0:T(8,128)(2,1)S(1)}, bf16[384,512]{1,0:T(8,128)(2,1)S(1)}, u32[]{:S(2)}, u32[]{:S(2)}) collective-permute-start(bf16[384,512]{1,0:T(8,128)(2,1)S(1)} %collective-permute-done.10.refs_1_.refs_16_), channel_id=1, source_target_pairs={{0,1},{1,0},{2,3},{3,2},{4,5},{5,4},{6,7},{7,6},{8,9},{9,8},{10,11... | collective-permute-start | bytes 1179656 | tf_op jit(solution)/shard_map/ppermute | solution.py:59
  34.3 83.7 %copy-start.23 = (bf16[384,512]{1,0:T(8,128)(2,1)}, bf16[384,512]{1,0:T(8,128)(2,1)S(1)}, u32[]{:S(2)}) copy-start(bf16[384,512]{1,0:T(8,128)(2,1)S(1)} %collective-permute-done.18.refs_9_.refs_24_) | copy-start | bytes 1179652
  34.3 7.8 %collective-permute-start.12 = (bf16[384,512]{1,0:T(8,128)(2,1)S(1)}, bf16[384,512]{1,0:T(8,128)(2,1)S(1)}, u32[]{:S(2)}, u32[]{:S(2)}) collective-permute-start(bf16[384,512]{1,0:T(8,128)(2,1)S(1)} %collective-permute-done.10.refs_1_.refs_16_), channel_id=1, source_target_pairs={{0,2},{1,5},{2,0},{3,7},{4,6},{5,1},{6,4},{7,3},{8,10},{9,13},{10,... | collective-permute-start | bytes 1179656 | tf_op jit(solution)/shard_map/ppermute | solution.py:58
  35.8 82.2 %copy-start.25 = (bf16[384,512]{1,0:T(8,128)(2,1)}, bf16[384,512]{1,0:T(8,128)(2,1)S(1)}, u32[]{:S(2)}) copy-start(bf16[384,512]{1,0:T(8,128)(2,1)S(1)} %collective-permute-done.26.refs_17_.refs_32_) | copy-start | bytes 1179652
  35.8 7.8 %collective-permute-start.19 = (bf16[384,512]{1,0:T(8,128)(2,1)S(1)}, bf16[384,512]{1,0:T(8,128)(2,1)S(1)}, u32[]{:S(2)}, u32[]{:S(2)}) collective-permute-start(bf16[384,512]{1,0:T(8,128)(2,1)S(1)} %collective-permute-done.18.refs_9_.refs_24_), channel_id=1, source_target_pairs={{0,1},{1,0},{2,3},{3,2},{4,5},{5,4},{6,7},{7,6},{8,9},{9,8},{10,11... | collective-permute-start | bytes 1179656 | tf_op jit(solution)/shard_map/ppermute | solution.py:59
  35.8 10.5 %collective-permute-start.20 = (bf16[384,512]{1,0:T(8,128)(2,1)S(1)}, bf16[384,512]{1,0:T(8,128)(2,1)S(1)}, u32[]{:S(2)}, u32[]{:S(2)}) collective-permute-start(bf16[384,512]{1,0:T(8,128)(2,1)S(1)} %collective-permute-done.18.refs_9_.refs_24_), channel_id=1, source_target_pairs={{0,2},{1,5},{2,0},{3,7},{4,6},{5,1},{6,4},{7,3},{8,10},{9,13},{10,... | collective-permute-start | bytes 1179656 | tf_op jit(solution)/shard_map/ppermute | solution.py:58
  37.0 10.8 %collective-permute-start.27 = (bf16[384,512]{1,0:T(8,128)(2,1)S(1)}, bf16[384,512]{1,0:T(8,128)(2,1)S(1)}, u32[]{:S(2)}, u32[]{:S(2)}) collective-permute-start(bf16[384,512]{1,0:T(8,128)(2,1)S(1)} %collective-permute-done.26.refs_17_.refs_32_), channel_id=1, source_target_pairs={{0,1},{1,0},{2,3},{3,2},{4,5},{5,4},{6,7},{7,6},{8,9},{9,8},{10,11... | collective-permute-start | bytes 1179656 | tf_op jit(solution)/shard_map/ppermute | solution.py:59
  37.6 80.4 %copy-start.27 = (bf16[384,512]{1,0:T(8,128)(2,1)}, bf16[384,512]{1,0:T(8,128)(2,1)S(1)}, u32[]{:S(2)}) copy-start(bf16[384,512]{1,0:T(8,128)(2,1)S(1)} %collective-permute-done.11.refs_2_.refs_17_) | copy-start | bytes 1179652
  37.6 15.5 %collective-permute-start.28 = (bf16[384,512]{1,0:T(8,128)(2,1)S(1)}, bf16[384,512]{1,0:T(8,128)(2,1)S(1)}, u32[]{:S(2)}, u32[]{:S(2)}) collective-permute-start(bf16[384,512]{1,0:T(8,128)(2,1)S(1)} %collective-permute-done.26.refs_17_.refs_32_), channel_id=1, source_target_pairs={{0,2},{1,5},{2,0},{3,7},{4,6},{5,1},{6,4},{7,3},{8,10},{9,13},{10,... | collective-permute-start | bytes 1179656 | tf_op jit(solution)/shard_map/ppermute | solution.py:58
  42.1 75.9 %copy-start.29 = (bf16[384,512]{1,0:T(8,128)(2,1)}, bf16[384,512]{1,0:T(8,128)(2,1)S(1)}, u32[]{:S(2)}) copy-start(bf16[384,512]{1,0:T(8,128)(2,1)S(1)} %collective-permute-done.12.refs_3_.refs_18_) | copy-start | bytes 1179652
  42.1 16.9 %collective-permute-start.39 = (bf16[3,256,256]{2,1,0:T(8,128)(2,1)S(1)}, bf16[3,256,256]{2,1,0:T(8,128)(2,1)S(1)}, u32[]{:S(2)}, u32[]{:S(2)}) collective-permute-start(bf16[3,256,256]{2,1,0:T(8,128)(2,1)S(1)} %collective-permute-done.37.refs_4_), channel_id=1, source_target_pairs={{0,2},{1,5},{2,0},{3,7},{4,6},{5,1},{6,4},{7,3},{8,10},{9,13},{10,... | collective-permute-start | bytes 1179656 | tf_op jit(solution)/shard_map/ppermute | solution.py:60
  43.6 74.4 %copy-start.31 = (bf16[384,512]{1,0:T(8,128)(2,1)}, bf16[384,512]{1,0:T(8,128)(2,1)S(1)}, u32[]{:S(2)}) copy-start(bf16[384,512]{1,0:T(8,128)(2,1)S(1)} %collective-permute-done.19.refs_10_.refs_25_) | copy-start | bytes 1179652
  43.6 22.5 %collective-permute-start.13 = (bf16[384,512]{1,0:T(8,128)(2,1)S(1)}, bf16[384,512]{1,0:T(8,128)(2,1)S(1)}, u32[]{:S(2)}, u32[]{:S(2)}) collective-permute-start(bf16[384,512]{1,0:T(8,128)(2,1)S(1)} %collective-permute-done.11.refs_2_.refs_17_), channel_id=1, source_target_pairs={{0,2},{1,5},{2,0},{3,7},{4,6},{5,1},{6,4},{7,3},{8,10},{9,13},{10,... | collective-permute-start | bytes 1179656 | tf_op jit(solution)/shard_map/ppermute | solution.py:60
  46.3 71.7 %copy-start.33 = (bf16[384,512]{1,0:T(8,128)(2,1)}, bf16[384,512]{1,0:T(8,128)(2,1)S(1)}, u32[]{:S(2)}) copy-start(bf16[384,512]{1,0:T(8,128)(2,1)S(1)} %collective-permute-done.20.refs_11_.refs_26_) | copy-start | bytes 1179652
  46.3 19.8 %collective-permute-start.14 = (bf16[384,512]{1,0:T(8,128)(2,1)S(1)}, bf16[384,512]{1,0:T(8,128)(2,1)S(1)}, u32[]{:S(2)}, u32[]{:S(2)}) collective-permute-start(bf16[384,512]{1,0:T(8,128)(2,1)S(1)} %collective-permute-done.12.refs_3_.refs_18_), channel_id=1, source_target_pairs={{0,4},{1,3},{2,6},{3,1},{4,0},{5,7},{6,2},{7,5},{8,12},{9,11},{10,... | collective-permute-start | bytes 1179656 | tf_op jit(solution)/shard_map/ppermute | solution.py:61
  47.8 70.2 %copy-start.35 = (bf16[384,512]{1,0:T(8,128)(2,1)}, bf16[384,512]{1,0:T(8,128)(2,1)S(1)}, u32[]{:S(2)}) copy-start(bf16[384,512]{1,0:T(8,128)(2,1)S(1)} %collective-permute-done.27.refs_18_.refs_33_) | copy-start | bytes 1179652
  47.8 19.9 %collective-permute-start.15 = (bf16[384,512]{1,0:T(8,128)(2,1)S(1)}, bf16[384,512]{1,0:T(8,128)(2,1)S(1)}, u32[]{:S(2)}, u32[]{:S(2)}) collective-permute-start(bf16[384,512]{1,0:T(8,128)(2,1)S(1)} %collective-permute-done.12.refs_3_.refs_18_), channel_id=1, source_target_pairs={{0,1},{1,0},{2,3},{3,2},{4,5},{5,4},{6,7},{7,6},{8,9},{9,8},{10,11... | collective-permute-start | bytes 1179656 | tf_op jit(solution)/shard_map/ppermute | solution.py:62
  53.1 65.0 %copy-start.37 = (bf16[384,512]{1,0:T(8,128)(2,1)}, bf16[384,512]{1,0:T(8,128)(2,1)S(1)}, u32[]{:S(2)}) copy-start(bf16[384,512]{1,0:T(8,128)(2,1)S(1)} %collective-permute-done.28.refs_19_.refs_34_) | copy-start | bytes 1179652
  53.1 19.6 %collective-permute-start.21 = (bf16[384,512]{1,0:T(8,128)(2,1)S(1)}, bf16[384,512]{1,0:T(8,128)(2,1)S(1)}, u32[]{:S(2)}, u32[]{:S(2)}) collective-permute-start(bf16[384,512]{1,0:T(8,128)(2,1)S(1)} %collective-permute-done.19.refs_10_.refs_25_), channel_id=1, source_target_pairs={{0,2},{1,5},{2,0},{3,7},{4,6},{5,1},{6,4},{7,3},{8,10},{9,13},{10,... | collective-permute-start | bytes 1179656 | tf_op jit(solution)/shard_map/ppermute | solution.py:60
  59.0 59.1 %copy-start = (bf16[3,256,256]{2,1,0:T(8,128)(2,1)}, bf16[3,256,256]{2,1,0:T(8,128)(2,1)S(1)}, u32[]{:S(2)}) copy-start(bf16[3,256,256]{2,1,0:T(8,128)(2,1)S(1)} %collective-permute-done.39.refs_6_) | copy-start | bytes 1179652
  59.0 13.8 %collective-permute-start.22 = (bf16[384,512]{1,0:T(8,128)(2,1)S(1)}, bf16[384,512]{1,0:T(8,128)(2,1)S(1)}, u32[]{:S(2)}, u32[]{:S(2)}) collective-permute-start(bf16[384,512]{1,0:T(8,128)(2,1)S(1)} %collective-permute-done.20.refs_11_.refs_26_), channel_id=1, source_target_pairs={{0,4},{1,3},{2,6},{3,1},{4,0},{5,7},{6,2},{7,5},{8,12},{9,11},{10,... | collective-permute-start | bytes 1179656 | tf_op jit(solution)/shard_map/ppermute | solution.py:61
  66.1 52.0 %copy-start.39 = (bf16[384,512]{1,0:T(8,128)(2,1)}, bf16[384,512]{1,0:T(8,128)(2,1)S(1)}, u32[]{:S(2)}) copy-start(bf16[384,512]{1,0:T(8,128)(2,1)S(1)} %collective-permute-done.13.refs_4_.refs_19_) | copy-start | bytes 1179652
  66.1 7.1 %collective-permute-start.23 = (bf16[384,512]{1,0:T(8,128)(2,1)S(1)}, bf16[384,512]{1,0:T(8,128)(2,1)S(1)}, u32[]{:S(2)}, u32[]{:S(2)}) collective-permute-start(bf16[384,512]{1,0:T(8,128)(2,1)S(1)} %collective-permute-done.20.refs_11_.refs_26_), channel_id=1, source_target_pairs={{0,1},{1,0},{2,3},{3,2},{4,5},{5,4},{6,7},{7,6},{8,9},{9,8},{10,11... | collective-permute-start | bytes 1179656 | tf_op jit(solution)/shard_map/ppermute | solution.py:62
  66.1 52.0 %copy-start.41 = (bf16[384,512]{1,0:T(8,128)(2,1)}, bf16[384,512]{1,0:T(8,128)(2,1)S(1)}, u32[]{:S(2)}) copy-start(bf16[384,512]{1,0:T(8,128)(2,1)S(1)} %collective-permute-done.14.refs_5_.refs_20_) | copy-start | bytes 1179652
  66.1 13.9 %collective-permute-start.29 = (bf16[384,512]{1,0:T(8,128)(2,1)S(1)}, bf16[384,512]{1,0:T(8,128)(2,1)S(1)}, u32[]{:S(2)}, u32[]{:S(2)}) collective-permute-start(bf16[384,512]{1,0:T(8,128)(2,1)S(1)} %collective-permute-done.27.refs_18_.refs_33_), channel_id=1, source_target_pairs={{0,2},{1,5},{2,0},{3,7},{4,6},{5,1},{6,4},{7,3},{8,10},{9,13},{10,... | collective-permute-start | bytes 1179656 | tf_op jit(solution)/shard_map/ppermute | solution.py:60
  67.7 50.4 %copy-start.43 = (bf16[384,512]{1,0:T(8,128)(2,1)}, bf16[384,512]{1,0:T(8,128)(2,1)S(1)}, u32[]{:S(2)}) copy-start(bf16[384,512]{1,0:T(8,128)(2,1)S(1)} %collective-permute-done.15.refs_6_.refs_21_) | copy-start | bytes 1179652
  67.7 12.3 %collective-permute-start.30 = (bf16[384,512]{1,0:T(8,128)(2,1)S(1)}, bf16[384,512]{1,0:T(8,128)(2,1)S(1)}, u32[]{:S(2)}, u32[]{:S(2)}) collective-permute-start(bf16[384,512]{1,0:T(8,128)(2,1)S(1)} %collective-permute-done.28.refs_19_.refs_34_), channel_id=1, source_target_pairs={{0,4},{1,3},{2,6},{3,1},{4,0},{5,7},{6,2},{7,5},{8,12},{9,11},{10,... | collective-permute-start | bytes 1179656 | tf_op jit(solution)/shard_map/ppermute | solution.py:61
  72.7 45.4 %copy-start.45 = (bf16[384,512]{1,0:T(8,128)(2,1)}, bf16[384,512]{1,0:T(8,128)(2,1)S(1)}, u32[]{:S(2)}) copy-start(bf16[384,512]{1,0:T(8,128)(2,1)S(1)} %collective-permute-done.21.refs_12_.refs_27_) | copy-start | bytes 1179652
  72.7 7.8 %collective-permute-start.31 = (bf16[384,512]{1,0:T(8,128)(2,1)S(1)}, bf16[384,512]{1,0:T(8,128)(2,1)S(1)}, u32[]{:S(2)}, u32[]{:S(2)}) collective-permute-start(bf16[384,512]{1,0:T(8,128)(2,1)S(1)} %collective-permute-done.28.refs_19_.refs_34_), channel_id=1, source_target_pairs={{0,1},{1,0},{2,3},{3,2},{4,5},{5,4},{6,7},{7,6},{8,9},{9,8},{10,11... | collective-permute-start | bytes 1179656 | tf_op jit(solution)/shard_map/ppermute | solution.py:62
  72.7 45.4 %copy-start.47 = (bf16[384,512]{1,0:T(8,128)(2,1)}, bf16[384,512]{1,0:T(8,128)(2,1)S(1)}, u32[]{:S(2)}) copy-start(bf16[384,512]{1,0:T(8,128)(2,1)S(1)} %collective-permute-done.22.refs_13_.refs_28_) | copy-start | bytes 1179652
  72.7 7.9 %collective-permute-start.16 = (bf16[384,512]{1,0:T(8,128)(2,1)S(1)}, bf16[384,512]{1,0:T(8,128)(2,1)S(1)}, u32[]{:S(2)}, u32[]{:S(2)}) collective-permute-start(bf16[384,512]{1,0:T(8,128)(2,1)S(1)} %collective-permute-done.13.refs_4_.refs_19_), channel_id=1, source_target_pairs={{0,1},{1,0},{2,3},{3,2},{4,5},{5,4},{6,7},{7,6},{8,9},{9,8},{10,11... | collective-permute-start | bytes 1179656 | tf_op jit(solution)/shard_map/ppermute | solution.py:62
  73.2 44.9 %copy-start.49 = (bf16[384,512]{1,0:T(8,128)(2,1)}, bf16[384,512]{1,0:T(8,128)(2,1)S(1)}, u32[]{:S(2)}) copy-start(bf16[384,512]{1,0:T(8,128)(2,1)S(1)} %collective-permute-done.23.refs_14_.refs_29_) | copy-start | bytes 1179652
  73.2 7.8 %collective-permute-start.17 = (bf16[384,512]{1,0:T(8,128)(2,1)S(1)}, bf16[384,512]{1,0:T(8,128)(2,1)S(1)}, u32[]{:S(2)}, u32[]{:S(2)}) collective-permute-start(bf16[384,512]{1,0:T(8,128)(2,1)S(1)} %collective-permute-done.14.refs_5_.refs_20_), channel_id=1, source_target_pairs={{0,1},{1,0},{2,3},{3,2},{4,5},{5,4},{6,7},{7,6},{8,9},{9,8},{10,11... | collective-permute-start | bytes 1179656 | tf_op jit(solution)/shard_map/ppermute | solution.py:70
  80.0 38.1 %copy-start.51 = (bf16[384,512]{1,0:T(8,128)(2,1)}, bf16[384,512]{1,0:T(8,128)(2,1)S(1)}, u32[]{:S(2)}) copy-start(bf16[384,512]{1,0:T(8,128)(2,1)S(1)} %collective-permute-done.29.refs_20_.refs_35_) | copy-start | bytes 1179652
  80.0 2.6 %collective-permute-start.24 = (bf16[384,512]{1,0:T(8,128)(2,1)S(1)}, bf16[384,512]{1,0:T(8,128)(2,1)S(1)}, u32[]{:S(2)}, u32[]{:S(2)}) collective-permute-start(bf16[384,512]{1,0:T(8,128)(2,1)S(1)} %collective-permute-done.21.refs_12_.refs_27_), channel_id=1, source_target_pairs={{0,1},{1,0},{2,3},{3,2},{4,5},{5,4},{6,7},{7,6},{8,9},{9,8},{10,11... | collective-permute-start | bytes 1179656 | tf_op jit(solution)/shard_map/ppermute | solution.py:62
  80.0 38.1 %copy-start.53 = (bf16[384,512]{1,0:T(8,128)(2,1)}, bf16[384,512]{1,0:T(8,128)(2,1)S(1)}, u32[]{:S(2)}) copy-start(bf16[384,512]{1,0:T(8,128)(2,1)S(1)} %collective-permute-done.30.refs_21_.refs_36_) | copy-start | bytes 1179652
  80.0 2.6 %collective-permute-start.25 = (bf16[384,512]{1,0:T(8,128)(2,1)S(1)}, bf16[384,512]{1,0:T(8,128)(2,1)S(1)}, u32[]{:S(2)}, u32[]{:S(2)}) collective-permute-start(bf16[384,512]{1,0:T(8,128)(2,1)S(1)} %collective-permute-done.22.refs_13_.refs_28_), channel_id=1, source_target_pairs={{0,1},{1,0},{2,3},{3,2},{4,5},{5,4},{6,7},{7,6},{8,9},{9,8},{10,11... | collective-permute-start | bytes 1179656 | tf_op jit(solution)/shard_map/ppermute | solution.py:70
  80.5 37.6 %copy-start.55 = (bf16[384,512]{1,0:T(8,128)(2,1)}, bf16[384,512]{1,0:T(8,128)(2,1)S(1)}, u32[]{:S(2)}) copy-start(bf16[384,512]{1,0:T(8,128)(2,1)S(1)} %collective-permute-done.31.refs_22_.refs_37_) | copy-start | bytes 1179652
  80.6 2.6 %collective-permute-start.32 = (bf16[384,512]{1,0:T(8,128)(2,1)S(1)}, bf16[384,512]{1,0:T(8,128)(2,1)S(1)}, u32[]{:S(2)}, u32[]{:S(2)}) collective-permute-start(bf16[384,512]{1,0:T(8,128)(2,1)S(1)} %collective-permute-done.29.refs_20_.refs_35_), channel_id=1, source_target_pairs={{0,1},{1,0},{2,3},{3,2},{4,5},{5,4},{6,7},{7,6},{8,9},{9,8},{10,11... | collective-permute-start | bytes 1179656 | tf_op jit(solution)/shard_map/ppermute | solution.py:62
  80.6 37.5 %copy-start.57 = (bf16[384,512]{1,0:T(8,128)(2,1)}, bf16[384,512]{1,0:T(8,128)(2,1)S(1)}, u32[]{:S(2)}) copy-start(bf16[384,512]{1,0:T(8,128)(2,1)S(1)} %collective-permute-done.16.refs_7_.refs_22_) | copy-start | bytes 1179652
  80.6 2.8 %collective-permute-start.33 = (bf16[384,512]{1,0:T(8,128)(2,1)S(1)}, bf16[384,512]{1,0:T(8,128)(2,1)S(1)}, u32[]{:S(2)}, u32[]{:S(2)}) collective-permute-start(bf16[384,512]{1,0:T(8,128)(2,1)S(1)} %collective-permute-done.30.refs_21_.refs_36_), channel_id=1, source_target_pairs={{0,1},{1,0},{2,3},{3,2},{4,5},{5,4},{6,7},{7,6},{8,9},{9,8},{10,11... | collective-permute-start | bytes 1179656 | tf_op jit(solution)/shard_map/ppermute | solution.py:70
  81.1 7.8 %collective-permute-start.40 = (bf16[3,256,256]{2,1,0:T(8,128)(2,1)S(1)}, bf16[3,256,256]{2,1,0:T(8,128)(2,1)S(1)}, u32[]{:S(2)}, u32[]{:S(2)}) collective-permute-start(bf16[3,256,256]{2,1,0:T(8,128)(2,1)S(1)} %collective-permute-done.38.refs_5_), channel_id=1, source_target_pairs={{0,4},{1,3},{2,6},{3,1},{4,0},{5,7},{6,2},{7,5},{8,12},{9,11},{10,... | collective-permute-start | bytes 1179656 | tf_op jit(solution)/shard_map/ppermute | solution.py:61
  82.6 16.0 %collective-permute-start.41 = (bf16[3,256,256]{2,1,0:T(8,128)(2,1)S(1)}, bf16[3,256,256]{2,1,0:T(8,128)(2,1)S(1)}, u32[]{:S(2)}, u32[]{:S(2)}) collective-permute-start(bf16[3,256,256]{2,1,0:T(8,128)(2,1)S(1)} %collective-permute-done.38.refs_5_), channel_id=1, source_target_pairs={{0,1},{1,0},{2,3},{3,2},{4,5},{5,4},{6,7},{7,6},{8,9},{9,8},{10,11... | collective-permute-start | bytes 1179656 | tf_op jit(solution)/shard_map/ppermute | solution.py:62
  82.6 16.6 %collective-permute-start.42 = (bf16[3,256,256]{2,1,0:T(8,128)(2,1)S(1)}, bf16[3,256,256]{2,1,0:T(8,128)(2,1)S(1)}, u32[]{:S(2)}, u32[]{:S(2)}) collective-permute-start(bf16[3,256,256]{2,1,0:T(8,128)(2,1)S(1)} %collective-permute-done.39.refs_6_), channel_id=1, source_target_pairs={{0,1},{1,0},{2,3},{3,2},{4,5},{5,4},{6,7},{7,6},{8,9},{9,8},{10,11... | collective-permute-start | bytes 1179656 | tf_op jit(solution)/shard_map/ppermute | solution.py:62
  88.9 16.8 %collective-permute-start.43 = (bf16[3,256,256]{2,1,0:T(8,128)(2,1)S(1)}, bf16[3,256,256]{2,1,0:T(8,128)(2,1)S(1)}, u32[]{:S(2)}, u32[]{:S(2)}) collective-permute-start(bf16[3,256,256]{2,1,0:T(8,128)(2,1)S(1)} %collective-permute-done.40.refs_7_), channel_id=1, source_target_pairs={{0,1},{1,0},{2,3},{3,2},{4,5},{5,4},{6,7},{7,6},{8,9},{9,8},{10,11... | collective-permute-start | bytes 1179656 | tf_op jit(solution)/shard_map/ppermute | solution.py:70
  88.9 12.3 %collective-permute-start.34 = (bf16[256,128]{1,0:T(8,128)(2,1)S(1)}, bf16[256,128]{1,0:T(8,128)(2,1)S(1)}, u32[]{:S(2)}, u32[]{:S(2)}) collective-permute-start(bf16[256,128]{1,0:T(8,128)(2,1)S(1)} %get-tuple-element.161), channel_id=1, source_target_pairs={{0,24},{8,0},{16,8},{24,16},{1,25},{9,1},{17,9},{25,17},{2,26},{10... | collective-permute-start | bytes 196616 | tf_op jit(solution)/shard_map/ppermute | solution.py:276
  98.6 7.0 %collective-permute-start.35 = (bf16[256,128]{1,0:T(8,128)(2,1)S(1)}, bf16[256,128]{1,0:T(8,128)(2,1)S(1)}, u32[]{:S(2)}, u32[]{:S(2)}) collective-permute-start(bf16[256,128]{1,0:T(8,128)(2,1)S(1)} %get-tuple-element.162), channel_id=1, source_target_pairs={{0,16},{8,24},{16,0},{24,8},{1,17},{9,25},{17,1},{25,9},{2,18},{10... | collective-permute-start | bytes 196616 | tf_op jit(solution)/shard_map/ppermute | solution.py:276
  98.6 7.0 %collective-permute-start.36 = (bf16[256,128]{1,0:T(8,128)(2,1)S(1)}, bf16[256,128]{1,0:T(8,128)(2,1)S(1)}, u32[]{:S(2)}, u32[]{:S(2)}) collective-permute-start(bf16[256,128]{1,0:T(8,128)(2,1)S(1)} %get-tuple-element.163), channel_id=1, source_target_pairs={{0,8},{8,16},{16,24},{24,0},{1,9},{9,17},{17,25},{25,1},{2,10},{10... | collective-permute-start | bytes 196616 | tf_op jit(solution)/shard_map/ppermute | solution.py:276
  109.9 4.9 %collective-permute-start.44 = (bf16[256,128]{1,0:T(8,128)(2,1)S(1)}, bf16[256,128]{1,0:T(8,128)(2,1)S(1)}, u32[]{:S(2)}, u32[]{:S(2)}) collective-permute-start(bf16[256,128]{1,0:T(8,128)(2,1)S(1)} %get-tuple-element.171), channel_id=1, source_target_pairs={{0,24},{8,0},{16,8},{24,16},{1,25},{9,1},{17,9},{25,17},{2,26},{10... | collective-permute-start | bytes 196616 | tf_op jit(solution)/shard_map/ppermute | solution.py:276
  110.0 8.0 %collective-permute-start.45 = (bf16[256,128]{1,0:T(8,128)(2,1)S(1)}, bf16[256,128]{1,0:T(8,128)(2,1)S(1)}, u32[]{:S(2)}, u32[]{:S(2)}) collective-permute-start(bf16[256,128]{1,0:T(8,128)(2,1)S(1)} %get-tuple-element.172), channel_id=1, source_target_pairs={{0,16},{8,24},{16,0},{24,8},{1,17},{9,25},{17,1},{25,9},{2,18},{10... | collective-permute-start | bytes 196616 | tf_op jit(solution)/shard_map/ppermute | solution.py:276
  110.1 7.9 %collective-permute-start.46 = (bf16[256,128]{1,0:T(8,128)(2,1)S(1)}, bf16[256,128]{1,0:T(8,128)(2,1)S(1)}, u32[]{:S(2)}, u32[]{:S(2)}) collective-permute-start(bf16[256,128]{1,0:T(8,128)(2,1)S(1)} %get-tuple-element.173), channel_id=1, source_target_pairs={{0,8},{8,16},{16,24},{24,0},{1,9},{9,17},{17,25},{25,1},{2,10},{10... | collective-permute-start | bytes 196616 | tf_op jit(solution)/shard_map/ppermute | solution.py:276
  123.5 8.2 %collective-permute-start.47 = (bf16[256,128]{1,0:T(8,128)(2,1)}, bf16[256,128]{1,0:T(8,128)(2,1)S(1)}, u32[]{:S(2)}, u32[]{:S(2)}) collective-permute-start(bf16[256,128]{1,0:T(8,128)(2,1)} %get-tuple-element.179), channel_id=1, source_target_pairs={{0,24},{8,0},{16,8},{24,16},{1,25},{9,1},{17,9},{25,17},{2,26},{10... | collective-permute-start | bytes 196616 | tf_op jit(solution)/shard_map/ppermute | solution.py:276
  124.8 10.1 %collective-permute-start.48 = (bf16[256,128]{1,0:T(8,128)(2,1)}, bf16[256,128]{1,0:T(8,128)(2,1)S(1)}, u32[]{:S(2)}, u32[]{:S(2)}) collective-permute-start(bf16[256,128]{1,0:T(8,128)(2,1)} %get-tuple-element.180), channel_id=1, source_target_pairs={{0,16},{8,24},{16,0},{24,8},{1,17},{9,25},{17,1},{25,9},{2,18},{10... | collective-permute-start | bytes 196616 | tf_op jit(solution)/shard_map/ppermute | solution.py:276
  128.2 6.7 %collective-permute-start.49 = (bf16[256,128]{1,0:T(8,128)(2,1)S(1)}, bf16[256,128]{1,0:T(8,128)(2,1)S(1)}, u32[]{:S(2)}, u32[]{:S(2)}) collective-permute-start(bf16[256,128]{1,0:T(8,128)(2,1)S(1)} %get-tuple-element.181), channel_id=1, source_target_pairs={{0,8},{8,16},{16,24},{24,0},{1,9},{9,17},{17,25},{25,1},{2,10},{10... | collective-permute-start | bytes 196616 | tf_op jit(solution)/shard_map/ppermute | solution.py:276
  151.7 8.4 %collective-permute-start.50 = (bf16[512,128]{1,0:T(8,128)(2,1)}, bf16[512,128]{1,0:T(8,128)(2,1)S(1)}, u32[]{:S(2)}, u32[]{:S(2)}) collective-permute-start(bf16[512,128]{1,0:T(8,128)(2,1)} %get-tuple-element.187), channel_id=1, source_target_pairs={{0,8},{8,16},{16,24},{24,0},{1,9},{9,17},{17,25},{25,1},{2,10},{10... | collective-permute-start | bytes 393224 | tf_op jit(solution)/shard_map/ppermute | solution.py:276
  154.2 9.7 %collective-permute-start.51 = (bf16[512,128]{1,0:T(8,128)(2,1)}, bf16[512,128]{1,0:T(8,128)(2,1)S(1)}, u32[]{:S(2)}, u32[]{:S(2)}) collective-permute-start(bf16[512,128]{1,0:T(8,128)(2,1)} %get-tuple-element.188), channel_id=1, source_target_pairs={{0,16},{8,24},{16,0},{24,8},{1,17},{9,25},{17,1},{25,9},{2,18},{10... | collective-permute-start | bytes 393224 | tf_op jit(solution)/shard_map/ppermute | solution.py:276
  154.2 9.7 %collective-permute-start.52 = (bf16[512,128]{1,0:T(8,128)(2,1)}, bf16[512,128]{1,0:T(8,128)(2,1)S(1)}, u32[]{:S(2)}, u32[]{:S(2)}) collective-permute-start(bf16[512,128]{1,0:T(8,128)(2,1)} %get-tuple-element.189), channel_id=1, source_target_pairs={{0,24},{8,0},{16,8},{24,16},{1,25},{9,1},{17,9},{25,17},{2,26},{10... | collective-permute-start | bytes 393224 | tf_op jit(solution)/shard_map/ppermute | solution.py:276
  (50 other events, 468.5 us)
